TPU v7x, 16 devices: a 4x2x1 block of a 4x4x8 slice. The times are simulated.
16 devices in a mesh: data: 2 (over y, z), tensor: 8 (over x, core).
Axes of the slice: x: 4, y: 2, z: 1, core: 2. Of those that a mesh axis runs over, the one named last changes fastest.
The devices are a block of a 4x4x8 slice.
Arguments:
- x_in: bfloat16 [128, 128, 2048], P('data'), parts along dimension 0
- adapter_ids: int32 [128], P('data'), parts along dimension 0
- gain_attn: float32 [2048], replicated
- gain_mlp: float32 [2048], replicated
- w_q: bfloat16 [2048, 32, 64], P(None, 'tensor')
- w_k: bfloat16 [2048, 8, 64], P(None, 'tensor')
- w_v: bfloat16 [2048, 8, 64], P(None, 'tensor')
- w_o: bfloat16 [32, 64, 2048], P('tensor')
- w_gate: bfloat16 [2048, 8192], P(None, 'tensor')
- w_up: bfloat16 [2048, 8192], P(None, 'tensor')
- w_down: bfloat16 [8192, 2048], P('tensor')
- a_q: bfloat16 [2, 2048, 256], P(None, None, 'tensor')
- b_q: bfloat16 [2, 256, 32, 64], P(None, None, 'tensor')
- a_k: bfloat16 [2, 2048, 256], P(None, None, 'tensor')
- b_k: bfloat16 [2, 256, 8, 64], P(None, None, 'tensor')
- a_v: bfloat16 [2, 2048, 256], P(None, None, 'tensor')
- b_v: bfloat16 [2, 256, 8, 64], P(None, None, 'tensor')
- a_o: bfloat16 [2, 32, 64, 256], P(None, 'tensor')
- b_o: bfloat16 [2, 256, 2048], P(None, None, 'tensor')
- a_gate: bfloat16 [2, 2048, 256], P(None, None, 'tensor')
- b_gate: bfloat16 [2, 256, 8192], P(None, None, 'tensor')
- a_up: bfloat16 [2, 2048, 256], P(None, None, 'tensor')
- b_up: bfloat16 [2, 256, 8192], P(None, None, 'tensor')
- a_down: bfloat16 [2, 8192, 256], P(None, 'tensor')
- b_down: bfloat16 [2, 256, 2048], P(None, None, 'tensor')
Outputs:
- output: bfloat16 [128, 128, 2048], P('data'), parts along dimension 0
There are 2 independent parts. A program takes and returns all parts, laid end to end along the dimension named above; an argument that names none is the same for every part.
All inputs are finite; a program needn't handle non-finite values.
Results may differ from a plain program's by a relative error of at most 0.02.
Values are sent between devices in bfloat16 or wider.
A program may use at most 768 MiB of HBM per device.

v0:
```python
import jax
import jax.numpy as jnp
from jax import lax
from jax.sharding import PartitionSpec as P

ALPHA = 16.0
ROPE_BASE = 10000.0
EPSILON = 1e-5


def rms_gain(act_in, gain_vec):
    act_f32 = act_in.astype(jnp.float32)
    inv_rms = lax.rsqrt(jnp.mean(act_f32 * act_f32, axis=-1, keepdims=True) + EPSILON)
    return (act_f32 * inv_rms * gain_vec).astype(jnp.bfloat16)


def rope_rotate(head_vals):
    seq_len = head_vals.shape[1]
    head_dim = head_vals.shape[-1]
    half_dim = head_dim // 2
    inv_freq = ROPE_BASE ** (-2.0 * jnp.arange(half_dim, dtype=jnp.float32) / head_dim)
    angle_tab = jnp.arange(seq_len, dtype=jnp.float32)[:, None] * inv_freq[None, :]
    cos_tab = jnp.cos(angle_tab)[:, None, :]
    sin_tab = jnp.sin(angle_tab)[:, None, :]
    first_half = head_vals[..., :half_dim]
    second_half = head_vals[..., half_dim:]
    return jnp.concatenate([first_half * cos_tab - second_half * sin_tab, second_half * cos_tab + first_half * sin_tab], axis=-1)


def causal_attention(q_heads, k_heads, v_heads):
    batch_size, seq_len, q_count, head_dim = q_heads.shape
    kv_count = k_heads.shape[2]
    q_group = q_heads.reshape(batch_size, seq_len, kv_count, q_count // kv_count, head_dim)
    scores = jnp.einsum('bskgd,btkd->bkgst', q_group, k_heads, preferred_element_type=jnp.float32) * head_dim ** -0.5
    causal = jnp.arange(seq_len)[:, None] >= jnp.arange(seq_len)[None, :]
    attn_prob = jax.nn.softmax(jnp.where(causal, scores, -1e30), axis=-1).astype(jnp.bfloat16)
    mixed_out = jnp.einsum('bkgst,btkd->bskgd', attn_prob, v_heads, preferred_element_type=jnp.float32)
    return mixed_out.astype(jnp.bfloat16).reshape(batch_size, seq_len, q_count, head_dim)


def solution(mesh):
    tp_size = mesh.shape['tensor']
    head_split = P(None, 'tensor', None)
    last_split = P(None, None, 'tensor')
    b_head_split = P(None, None, 'tensor', None)
    in_specs = (P('data', None, None), P('data'), P(None), P(None),
                head_split, head_split, head_split, P('tensor', None, None),
                P(None, 'tensor'), P(None, 'tensor'), P('tensor', None),
                last_split, b_head_split, last_split, b_head_split, last_split, b_head_split,
                P(None, 'tensor', None, None), last_split,
                last_split, last_split, last_split, last_split,
                P(None, 'tensor', None), last_split)

    def local_layer(x_in, adapter_ids, gain_attn, gain_mlp, w_q, w_k, w_v, w_o, w_gate, w_up, w_down, a_q, b_q, a_k, b_k, a_v, b_v, a_o, b_o, a_gate, b_gate, a_up, b_up, a_down, b_down):
        value_a10 = ALPHA / b_q.shape[1]
        shard_width = x_in.shape[2] // tp_size
        my_index = lax.axis_index('tensor')

        def per_sequence(table_stack):
            return jnp.take(table_stack, adapter_ids, axis=0)

        def column_proj(act_in, weight, a_stack, b_stack, base_form, up_form):
            low_part = jnp.einsum('bsd,bdr->bsr', act_in, per_sequence(a_stack), preferred_element_type=jnp.float32)
            low_rank = lax.all_gather(low_part.astype(jnp.bfloat16), 'tensor', axis=2, tiled=True)
            base_out = jnp.einsum(base_form, act_in, weight, preferred_element_type=jnp.float32)
            return base_out + value_a10 * jnp.einsum(up_form, low_rank, per_sequence(b_stack), preferred_element_type=jnp.float32)

        def row_proj(act_in, weight, a_stack, b_stack, base_form, low_form, resid_shard):
            base_part = jnp.einsum(base_form, act_in, weight, preferred_element_type=jnp.float32).astype(jnp.bfloat16)
            low_part = jnp.einsum(low_form, act_in, per_sequence(a_stack), preferred_element_type=jnp.float32).astype(jnp.bfloat16)
            low_rank = lax.psum(low_part, 'tensor')
            base_shard = lax.psum_scatter(base_part, 'tensor', scatter_dimension=2, tiled=True)
            delta_out = jnp.einsum('bsr,brd->bsd', low_rank, per_sequence(b_stack), preferred_element_type=jnp.float32)
            out_shard = (resid_shard.astype(jnp.float32) + base_shard.astype(jnp.float32) + value_a10 * delta_out).astype(jnp.bfloat16)
            return out_shard, lax.all_gather(out_shard, 'tensor', axis=2, tiled=True)

        h_attn = rms_gain(x_in, gain_attn)
        z_q = column_proj(h_attn, w_q, a_q, b_q, 'bsd,dhe->bshe', 'bsr,brhe->bshe')
        z_k = column_proj(h_attn, w_k, a_k, b_k, 'bsd,dhe->bshe', 'bsr,brhe->bshe')
        z_v = column_proj(h_attn, w_v, a_v, b_v, 'bsd,dhe->bshe', 'bsr,brhe->bshe')
        attn_out = causal_attention(rope_rotate(z_q).astype(jnp.bfloat16), rope_rotate(z_k).astype(jnp.bfloat16), z_v.astype(jnp.bfloat16))
        x_shard = lax.dynamic_slice_in_dim(x_in, my_index * shard_width, shard_width, axis=2)
        mid_shard, x_mid = row_proj(attn_out, w_o, a_o, b_o, 'bshe,hed->bsd', 'bshe,bher->bsr', x_shard)
        h_mlp = rms_gain(x_mid, gain_mlp)
        z_gate = column_proj(h_mlp, w_gate, a_gate, b_gate, 'bsd,df->bsf', 'bsr,brf->bsf')
        z_up = column_proj(h_mlp, w_up, a_up, b_up, 'bsd,df->bsf', 'bsr,brf->bsf')
        hidden = (jax.nn.silu(z_gate) * z_up).astype(jnp.bfloat16)
        return row_proj(hidden, w_down, a_down, b_down, 'bsf,fd->bsd', 'bsf,bfr->bsr', mid_shard)[1]

    return jax.shard_map(local_layer, mesh=mesh, in_specs=in_specs, out_specs=P('data', None, None), check_vma=False)
```

profile of v0, /device:TPU:113, one launch (start us, length us, event | category | flops | bytes accessed | tf_op | source)
XLA Modules:
  0.0 1338.9 jit_solution(2953397791899983899)
XLA Ops:
  8.0 11.4 fusion
  19.4 5.5 gather_fusion.5
  24.9 18.6 %fusion.97 = bf16[64,128,32]{1,2,0:T(8,128)(2,1)} fusion(bf16[64,2048,32]{1,2,0:T(8,128)(2,1)} %gather_fusion.5, pred[64]{0:T(512)(128)(4,1)S(1)} %compare_and_fusion, bf16[64,128,2048]{2,1,0:T(8,128)(2,1)} %param.33, f32[2048]{0:T(1024)S(1)} %copy-done.21, f32[64,128]{1,0:T(8,128)S(1)} %add_rsqrt_fusion.1), kind=kOutput, calls=%fused_computation.112 | convolution fusion | flops 1145307136 | bytes 42508352 | tf_op jit(solution)/shard_map/bsd,bdr->bsr/dot_general | solution.py:63
  44.5 5.5 gather_fusion.7
  50.0 18.7 %fusion.100 = bf16[64,128,32]{1,2,0:T(8,128)(2,1)} fusion(bf16[64,2048,32]{1,2,0:T(8,128)(2,1)} %gather_fusion.7, pred[64]{0:T(512)(128)(4,1)S(1)} %compare_and_fusion, bf16[64,128,2048]{2,1,0:T(8,128)(2,1)} %param.33, f32[2048]{0:T(1024)S(1)} %copy-done.21, f32[64,128]{1,0:T(8,128)S(1)} %add_rsqrt_fusion.1), kind=kOutput, calls=%fused_computation.113 | convolution fusion | flops 1145307136 | bytes 42508352 | tf_op jit(solution)/shard_map/bsd,bdr->bsr/dot_general | solution.py:63
  69.6 5.5 gather_fusion.3
  75.2 17.9 %fusion.41 = bf16[64,128,32]{1,2,0:T(8,128)(2,1)S(1)} fusion(bf16[64,2048,32]{1,2,0:T(8,128)(2,1)} %gather_fusion.3, pred[64]{0:T(512)(128)(4,1)S(1)} %compare_and_fusion, bf16[64,128,2048]{2,1,0:T(8,128)(2,1)} %param.33, f32[2048]{0:T(1024)S(1)} %copy-done.21, f32[64,128]{1,0:T(8,128)S(1)} %add_rsqrt_fusion.1), kind=kOutput, calls=%fused_computation.62 | convolution fusion | flops 1145044992 | bytes 42508352 | tf_op jit(solution)/shard_map/bsd,bdr->bsr/dot_general | solution.py:63
  93.1 1.0 copy.39
  94.2 5.5 gather_fusion
  99.7 7.7 broadcast_select_fusion
  108.1 17.4 %fusion.122 = f32[64,128,64]{1,2,0:T(8,128)} fusion(bf16[2048,1,64]{0,2,1:T(8,128)(2,1)} %param.38, bf16[64,128,2048]{2,1,0:T(8,128)(2,1)} %param.33, f32[2048]{0:T(1024)S(1)} %copy-done.21, f32[64,128]{1,0:T(8,128)S(1)} %add_rsqrt_fusion.1), kind=kOutput, calls=%fused_computation.129 | convolution fusion | flops 2214592512 | bytes 35954688 | tf_op jit(solution)/shard_map/bsd,dhe->bshe/dot_general | solution.py:65
  125.5 2.1 gather_fusion.4
  127.6 5.4 gather_fusion.1
  133.2 3.7 add_bitcast_fusion
  137.2 10.3 fusion.152
  147.5 31.2 %multiply_add_fusion = f32[64,128,4,64]{1,3,2,0:T(8,128)} fusion(f32[64,128,4,64]{1,3,2,0:T(8,128)} %bitcast.124, bf16[2048,4,64]{0,2,1:T(8,128)(2,1)S(1)} %copy-done.20, bf16[64,128,2048]{2,1,0:T(8,128)(2,1)} %param.33, f32[2048]{0:T(1024)S(1)} %copy-done.21, f32[64,128]{1,0:T(8,128)S(1)} %copy-done.18), kind=kOutput, calls=%fused_computation.68 | convolution fusion | flops 8661237760 | bytes 51421184 | tf_op jit(solution)/shard_map/bsd,dhe->bshe/dot_general | solution.py:65
  178.7 4.7 subtract_convert_fusion
  183.4 7.5 fusion.21
  190.9 10.4 fusion.20
  201.4 7.9 fusion.63
  209.2 23.7 %fusion.79 = bf16[64,64,4,128]{3,1,2,0:T(8,128)(2,1)} fusion(f32[64,4,128]{2,1,0:T(4,128)S(1)} %fusion.20, f32[64,4,128]{2,1,0:T(4,128)S(1)} %get-tuple-element.15, f32[64,128,128,4]{2,1,3,0:T(8,128)} %get-tuple-element.16, pred[128,128]{0,1:T(8,128)(4,1)S(1)} %iota_compare_fusion, f32[64,128,64]{1,2,0:T(8,128)} %fusion.63, ...), kind=kOutput, calls=%fused_computation.100 | convolution fusion | flops 2776104960 | bytes 57204736 | tf_op jit(solution)/shard_map/bkgst,btkd->bskgd/dot_general | solution.py:37
  233.0 8.4 bitcast_convert_fusion.1
  241.5 16.5 %bitcast_convert_fusion = bf16[64,128,2048]{2,1,0:T(8,128)(2,1)} fusion(bf16[64,64,4,128]{3,1,2,0:T(8,128)(2,1)} %fusion.79, bf16[4,64,2048]{2,1,0:T(8,128)(2,1)S(1)} %copy-done), kind=kOutput, calls=%fused_computation.24 | convolution fusion | flops 8606711808 | bytes 38797312 | tf_op jit(solution)/shard_map/bshe,hed->bsd/dot_general | solution.py:69
  259.0 5.8 gather_fusion.8
  264.8 41.9 %all-reduce.3.cloned.1.call-done = bf16[64,128,256]{2,1,0:T(8,128)(2,1)} async-done(((bf16[64,128,256]{2,1,0:T(8,128)(2,1)}), bf16[64,128,256]{2,1,0:T(8,128)(2,1)}) %all-reduce.3.cloned.1.call-update) | async-done | bytes 4194320 | tf_op jit(solution)/shard_map/psum | solution.py:71
  306.7 170.0 %reduce-scatter.3.cloned.1.call-done = bf16[64,128,256]{2,1,0:T(8,128)(2,1)} async-done(((bf16[64,128,2048]{2,1,0:T(8,128)(2,1)}), bf16[64,128,256]{2,1,0:T(8,128)(2,1)}) %reduce-scatter.3.cloned.1.call-update) | async-done | bytes 4194320 | tf_op jit(solution)/shard_map/reduce_scatter | solution.py:72
  476.7 11.2 add_convert_fusion.1
  488.9 5.5 gather_fusion.9
  494.4 153.4 %all-gather.14.cloned.1.call-done = bf16[64,128,2048]{2,1,0:T(8,128)(2,1)} async-done(((bf16[64,128,256]{2,1,0:T(8,128)(2,1)}), bf16[64,128,2048]{2,1,0:T(8,128)(2,1)}) %all-gather.14.cloned.1.call-update) | async-done | bytes 33554448 | tf_op jit(solution)/shard_map/all_gather | solution.py:75
  647.8 11.3 fusion.3
  659.2 18.8 %fusion.103 = bf16[64,128,32]{1,2,0:T(8,128)(2,1)} fusion(bf16[64,2048,32]{1,2,0:T(8,128)(2,1)} %gather_fusion.9, pred[64]{0:T(512)(128)(4,1)S(1)} %compare_and_fusion, bf16[64,128,2048]{2,1,0:T(8,128)(2,1)} %all-gather.14.cloned.1.call-done, f32[2048]{0:T(1024)S(1)} %copy-done.22, f32[64,128]{1,0:T(8,128)S(1)} %add_rsqrt_fusion), kind=kOutput, calls=%fused_computation.114 | convolution fusion | flops 1145307136 | bytes 42508352 | tf_op jit(solution)/shard_map/bsd,bdr->bsr/dot_general | solution.py:63
  678.1 12.3 gather_fusion.10
  690.4 5.4 gather_fusion.11
  695.8 12.3 gather_fusion.12
  708.1 12.1 gather_fusion.2
  720.2 18.6 %fusion.108 = bf16[64,128,32]{1,2,0:T(8,128)(2,1)} fusion(bf16[64,2048,32]{1,2,0:T(8,128)(2,1)} %gather_fusion.11, pred[64]{0:T(512)(128)(4,1)S(1)} %compare_and_fusion, bf16[64,128,2048]{2,1,0:T(8,128)(2,1)} %all-gather.14.cloned.1.call-done, f32[2048]{0:T(1024)S(1)} %copy-done.22, f32[64,128]{1,0:T(8,128)S(1)} %add_rsqrt_fusion), kind=kOutput, calls=%fused_computation.115 | convolution fusion | flops 1145307136 | bytes 42508352 | tf_op jit(solution)/shard_map/bsd,bdr->bsr/dot_general | solution.py:63
  739.0 42.2 %fusion.27 = f32[64,128,1024]{2,1,0:T(8,128)} fusion(bf16[64,128,2048]{2,1,0:T(8,128)(2,1)} %all-gather.14.cloned.1.call-done, f32[2048]{0:T(1024)S(1)} %copy-done.22, f32[64,128]{1,0:T(8,128)S(1)} %add_rsqrt_fusion, bf16[2048,1024]{1,0:T(8,128)(2,1)} %param.41), kind=kOutput, calls=%fused_computation.48 | convolution fusion | flops 34426847232 | bytes 71344128 | tf_op jit(solution)/shard_map/bsd,df->bsf/dot_general | solution.py:65
  781.2 23.2 %fusion.10 = f32[64,128,1024]{2,1,0:T(8,128)} fusion(bf16[64,128,256]{1,2,0:T(8,128)(2,1)} %all-gather.16.cloned.1.call-done, bf16[64,256,1024]{2,1,0:T(8,128)(2,1)} %gather_fusion.10, pred[64]{0:T(512)(128)(4,1)S(1)} %compare_and_fusion), kind=kOutput, calls=%fused_computation.29 | convolution fusion | flops 4311744512 | bytes 71303232 | tf_op jit(solution)/shard_map/bsr,brf->bsf/dot_general | solution.py:66
  804.4 23.2 %fusion.8 = f32[64,128,1024]{2,1,0:T(8,128)} fusion(bf16[64,128,256]{1,2,0:T(8,128)(2,1)} %all-gather.18.cloned.1.call-done, bf16[64,256,1024]{2,1,0:T(8,128)(2,1)} %gather_fusion.12, pred[64]{0:T(512)(128)(4,1)S(1)} %compare_and_fusion), kind=kOutput, calls=%fused_computation.27 | convolution fusion | flops 4311744512 | bytes 71303232 | tf_op jit(solution)/shard_map/bsr,brf->bsf/dot_general | solution.py:66
  827.6 56.8 %multiply_convert_fusion = bf16[64,128,1024]{2,1,0:T(8,128)(2,1)} fusion(f32[64,128,1024]{2,1,0:T(8,128)} %fusion.8, f32[64,128,1024]{2,1,0:T(8,128)} %fusion.27, f32[64,128,1024]{2,1,0:T(8,128)} %fusion.10, bf16[64,128,2048]{2,1,0:T(8,128)(2,1)} %all-gather.14.cloned.1.call-done, f32[2048]{0:T(1024)S(1)} %copy-done.22, f32[64,128]{1,0:T(8,128)S(1)} %add_rsqrt_fusion, ...), kind=kOutput, calls=%fused_computation.33 | convolution fusion | flops 34510733312 | bytes 155230208 | tf_op jit(solution)/shard_map/bsd,df->bsf/dot_general | solution.py:65
  884.4 20.4 %fusion.82 = bf16[64,128,256]{2,1,0:T(8,128)(2,1)} fusion(bf16[64,128,1024]{2,1,0:T(8,128)(2,1)} %multiply_convert_fusion, bf16[64,1024,256]{2,1,0:T(8,128)(2,1)} %gather_fusion.2, pred[64]{0:T(512)(128)(4,1)S(1)} %compare_and_fusion), kind=kOutput, calls=%fused_computation.101 | convolution fusion | flops 4313841664 | bytes 54526016 | tf_op jit(solution)/shard_map/bsf,bfr->bsr/dot_general | solution.py:70
  904.9 45.2 %convolution_convert_fusion = bf16[64,128,2048]{2,1,0:T(8,128)(2,1)} fusion(bf16[64,128,1024]{2,1,0:T(8,128)(2,1)} %multiply_convert_fusion, bf16[1024,2048]{1,0:T(8,128)(2,1)} %param.43), kind=kOutput, calls=%fused_computation.37 | convolution fusion | flops 34376515584 | bytes 54525952 | tf_op jit(solution)/shard_map/bsf,fd->bsd/dot_general | solution.py:69
  951.0 5.8 gather_fusion.13
  956.8 11.0 all-reduce.5.cloned.1.call-done
  967.8 170.0 %reduce-scatter.5.cloned.1.call-done = bf16[64,128,256]{2,1,0:T(8,128)(2,1)} async-done(((bf16[64,128,2048]{2,1,0:T(8,128)(2,1)}), bf16[64,128,256]{2,1,0:T(8,128)(2,1)}) %reduce-scatter.5.cloned.1.call-update) | async-done | bytes 4194320 | tf_op jit(solution)/shard_map/reduce_scatter | solution.py:72
  1137.7 11.2 add_convert_fusion
  1149.0 159.8 %all-gather.20.cloned.1.call-done = bf16[64,128,2048]{2,1,0:T(8,128)(2,1)} async-done(((bf16[64,128,256]{2,1,0:T(8,128)(2,1)}), bf16[64,128,2048]{2,1,0:T(8,128)(2,1)}) %all-gather.20.cloned.1.call-update) | async-done | bytes 33554448 | tf_op jit(solution)/shard_map/all_gather | solution.py:75
  1308.8 23.0 %copy.43 = bf16[64,128,2048]{2,1,0:T(8,128)(2,1)} copy(bf16[64,128,2048]{2,1,0:T(8,128)(2,1)} %all-gather.20.cloned.1.call-done) | data formatting | bytes 67108864
  (83 shorter events, 8.0 us)
Async XLA Ops:
  6.5 235.0 %copy-start = (bf16[4,64,2048]{2,1,0:T(8,128)(2,1)S(1)}, bf16[4,64,2048]{2,1,0:T(8,128)(2,1)}, u32[]{:S(2)}) copy-start(bf16[4,64,2048]{2,1,0:T(8,128)(2,1)} %param.40) | copy-start | bytes 3145732
  6.6 126.6 %all-gather.10.cloned.1.call-start = ((), (), s32[]{:S(2)}) async-start(), calls=%async_computation.3 | async-start | bytes 4718592 | tf_op jit(solution)/shard_map/all_gather | solution.py:64
  8.0 700.1 %copy-start.19 = (s32[1024]{0:T(1024)}, s32[1024]{0:T(1024)S(1)}, u32[]{:S(2)}) copy-start(s32[1024]{0:T(1024)S(1)} %pad_clamp_fusion) | copy-start | bytes 12292
  8.0 11.4 copy-start.2
  19.4 88.7 %copy-start.17 = (f32[64,128]{1,0:T(8,128)}, f32[64,128]{1,0:T(8,128)S(1)}, u32[]{:S(2)}) copy-start(f32[64,128]{1,0:T(8,128)S(1)} %add_rsqrt_fusion.1) | copy-start | bytes 98308
  19.4 5.5 copy-start.21
  43.6 0.9 copy-start.3
  43.6 93.5 %all-gather.12.cloned.1.call-start = ((), (), s32[]{:S(2)}) async-start(), calls=%async_computation.4 | async-start | bytes 4718592 | tf_op jit(solution)/shard_map/all_gather | solution.py:64
  68.7 0.9 copy-start.4
  68.8 132.6 %all-gather.8.cloned.1.call-start = ((), (), s32[]{:S(2)}) async-start(), calls=%async_computation.2 | async-start | bytes 4718592 | tf_op jit(solution)/shard_map/all_gather | solution.py:64
  93.1 1.2 copy-start.10
  94.1 212.6 %all-reduce.3.cloned.1.call-start = ((), (), s32[]{:S(2)}) async-start(), calls=%async_computation.6 | async-start | bytes 8388608 | tf_op jit(solution)/shard_map/psum | solution.py:71
  99.7 7.7 copy-start.14
  108.1 17.4 %copy-start.15 = (bf16[2,256,1,64]{1,3,2,0:T(8,128)(2,1)S(1)}, bf16[2,256,1,64]{1,3,2,0:T(8,128)(2,1)}, u32[]{:S(2)}) copy-start(bf16[2,256,1,64]{1,3,2,0:T(8,128)(2,1)} %param.49) | copy-start | bytes 196612
  125.5 2.1 copy-start.11
  137.2 10.3 copy-start.18
  137.2 10.3 copy-start.20
  190.9 10.4 copy-start.16
  241.4 235.3 %reduce-scatter.3.cloned.1.call-start = ((), (), s32[]{:S(2)}) async-start(), calls=%async_computation.5 | async-start | bytes 37748736 | tf_op jit(solution)/shard_map/reduce_scatter | solution.py:72
  258.1 0.9 copy-start.12
  258.1 389.7 %all-gather.14.cloned.1.call-start = ((), (), s32[]{:S(2)}) async-start(), calls=%async_computation.7 | async-start | bytes 37748736 | tf_op jit(solution)/shard_map/all_gather | solution.py:75
  487.9 0.9 copy-start.5
  488.0 293.2 %all-gather.16.cloned.1.call-start = ((), (), s32[]{:S(2)}) async-start(), calls=%async_computation.8 | async-start | bytes 4718592 | tf_op jit(solution)/shard_map/all_gather | solution.py:64
  494.4 164.8 %copy-start.22 = (f32[2048]{0:T(1024)S(1)}, f32[2048]{0:T(1024)}, u32[]{:S(2)}) copy-start(f32[2048]{0:T(1024)} %param.36) | copy-start | bytes 24580
  659.2 18.9 %copy-start.7 = (bf16[2,256,1024]{2,1,0:T(8,128)(2,1)S(1)}, bf16[2,256,1024]{2,1,0:T(8,128)(2,1)}, u32[]{:S(2)}) copy-start(bf16[2,256,1024]{2,1,0:T(8,128)(2,1)} %param.53) | copy-start | bytes 3145732
  678.0 126.4 %all-gather.18.cloned.1.call-start = ((), (), s32[]{:S(2)}) async-start(), calls=%async_computation.9 | async-start | bytes 4718592 | tf_op jit(solution)/shard_map/all_gather | solution.py:64
  678.1 12.3 copy-start.6
  690.4 5.4 copy-start.8
  695.8 12.3 copy-start.9
  738.9 228.8 %all-reduce.5.cloned.1.call-start = ((), (), s32[]{:S(2)}) async-start(), calls=%async_computation.11 | async-start | bytes 8388608 | tf_op jit(solution)/shard_map/psum | solution.py:71
  904.8 232.9 %reduce-scatter.5.cloned.1.call-start = ((), (), s32[]{:S(2)}) async-start(), calls=%async_computation.10 | async-start | bytes 37748736 | tf_op jit(solution)/shard_map/reduce_scatter | solution.py:72
  950.0 0.9 copy-start.13
  950.1 358.7 %all-gather.20.cloned.1.call-start = ((), (), s32[]{:S(2)}) async-start(), calls=%async_computation.12 | async-start | bytes 37748736 | tf_op jit(solution)/shard_map/all_gather | solution.py:75
  1308.8 23.0 %copy-start.1 = (bf16[4,64,2048]{2,1,0:T(8,128)(2,1)S(1)}, bf16[4,64,2048]{2,1,0:T(8,128)(2,1)}, u32[]{:S(2)}) copy-start(bf16[4,64,2048]{2,1,0:T(8,128)(2,1)} %param.40) | copy-start | bytes 3145732
Sparse Core Ops, SparseCore 0:
  43.8 31.0 all-gather.9
  76.4 27.6 all-gather.11
  105.7 27.6 all-gather.7
  241.6 65.1 all-reduce.2
  308.9 167.7 reduce-scatter.2
  488.1 159.6 all-gather.13
  678.1 28.6 all-gather.15
  739.0 28.6 all-gather.17
  904.9 62.8 all-reduce.4
  970.0 167.7 reduce-scatter.4
  1149.1 159.6 all-gather.19
where the time goes:
time: 1350 us; the launch traced here: 1340 us
  waiting for transfers between devices  707 us (52%)
  matrix products  452 us (33%)
  local copies, waits for them, and re-layouts  117 us (9%)
  other arithmetic  47.4 us (4%)
  between operations  14.1 us (1%)
    reduce_scatter x2, waiting for transfers between devices, row_proj(): lax.psum_scatter(base_part, 'tensor', scatter_dimension=2, tiled=True)  340 us
    all_gather x2, waiting for transfers between devices, row_proj(): return (out_shard, lax.all_gather(out_shard, 'tensor', axis=2, tiled=True))  313 us
    dot_general x4, matrix products, column_proj(): jnp.einsum(base_form, act_in, weight, preferred_element_type=jnp.float32)  148 us
    dot_general x5, matrix products, column_proj(): jnp.einsum('bsd,bdr->bsr', act_in, per_sequence(a_stack), preferred_eleme...  92.6 us
    gather x14, local copies, waits for them, and re-layouts, per_sequence(): return jnp.take(table_stack, adapter_ids, axis=0)  89.4 us
    dot_general x2, matrix products, row_proj(): jnp.einsum(base_form, act_in, weight, preferred_element_type=jnp.float32)  61.7 us
    dot_general x4, matrix products, column_proj(): jnp.einsum(up_form, low_rank, per_sequence(b_stack), preferred_element_ty...  58 us
    psum x2, waiting for transfers between devices, row_proj(): low_rank = lax.psum(low_part, 'tensor')  52.9 us
  transfers between devices with their start and end apart: 11, of which 6 were waited for; matrix products, arithmetic and copies ran while one was open for 27% of the time, Pallas kernels for 0%

commit v1 on v0

v1 whole, which is shorter than its diff:
```python
import functools

import jax
import jax.numpy as jnp
from jax import lax
from jax.experimental import pallas as pl
from jax.experimental.pallas import tpu as pltpu
from jax.sharding import PartitionSpec as P

ALPHA = 16.0
ROPE_BASE = 10000.0
EPSILON = 1e-5
CORES = 2
CHUNKS = 4
VMEM_LIMIT = 62 * 1024 * 1024
F32, BF16 = jnp.float32, jnp.bfloat16


def dot_nn(a, b):
    return lax.dot_general(a, b, (((1,), (0,)), ((), ())), preferred_element_type=F32)


def dot_nt(a, b):
    return lax.dot_general(a, b, (((1,), (1,)), ((), ())), preferred_element_type=F32)


def norm_tile(load_rows, gain_ref, dst_ref, n_rows):
    step_rows = 16

    @pl.loop(0, n_rows // step_rows)
    def _(i):
        v = load_rows(i, step_rows).astype(F32)
        inv = lax.rsqrt(jnp.mean(v * v, axis=-1, keepdims=True) + EPSILON)
        rows = pl.ds(pl.multiple_of(i * step_rows, step_rows), step_rows)
        dst_ref[rows, :] = (v * inv * gain_ref[...]).astype(BF16)


def attn_body(dims, meta, x_ref, gain_ref, cosq_ref, sinq_ref, cosk_ref, sink_ref,
              gw_ref, aqkv_ref, gb_ref, gwo_ref, out_ref,
              wq, wk, wv, aq, bq, bk, bv, wo, ao, bo, h_scr, low_scr, k_scr, v_scr, attn_scr, sems):
    n_dev, seqs, S, hd, nq, rank, D, spc, base_step, chips = dims
    half = hd // 2
    qw = nq * hd
    scale = ALPHA / rank
    step = pl.program_id(0)
    core = meta[meta.shape[0] - 1]

    plans = [[], [], [], []]
    plans[0].append((aqkv_ref, aq))
    for d in range(n_dev):
        plans[1].append((gw_ref.at[d, pl.ds(qw, half)], wk.at[pl.ds(d * half, half)]))
        plans[1].append((gw_ref.at[d, pl.ds(qw + half, half)], wk.at[pl.ds((n_dev + d) * half, half)]))
        plans[1].append((gw_ref.at[d, pl.ds(qw + hd, hd)], wv.at[pl.ds(d * hd, hd)]))
        for a in range(2):
            o = a * (qw + 2 * hd)
            plans[1].append((gb_ref.at[d, pl.ds(o + qw, half)], bk.at[a, pl.ds(d * half, half)]))
            plans[1].append((gb_ref.at[d, pl.ds(o + qw + half, half)], bk.at[a, pl.ds((n_dev + d) * half, half)]))
            plans[1].append((gb_ref.at[d, pl.ds(o + qw + hd, hd)], bv.at[a, pl.ds(d * hd, hd)]))
    for d in range(n_dev):
        plans[2].append((gw_ref.at[d, pl.ds(0, qw)], wq.at[pl.ds(d * qw, qw)]))
        for a in range(2):
            o = a * (qw + 2 * hd)
            plans[2].append((gb_ref.at[d, pl.ds(o, qw)], bq.at[a, pl.ds(d * qw, qw)]))
    off = 2 * (qw + 2 * hd)
    for d in range(n_dev):
        plans[3].append((gwo_ref.at[d], wo.at[pl.ds(d * qw, qw)]))
        for a in range(2):
            plans[3].append((gb_ref.at[d, pl.ds(off + a * qw, qw)], ao.at[a, pl.ds(d * qw, qw)]))
            plans[3].append((gb_ref.at[d, pl.ds(off + 2 * qw + a * rank, rank)],
                             bo.at[a, :, pl.ds(d * qw, qw)]))

    @pl.when(step == 0)
    def _():
        for i, plan in enumerate(plans):
            for src, dst in plan:
                pltpu.make_async_copy(src, dst, sems.at[i]).start()

    def arrive(i):
        @pl.when(step == 0)
        def _():
            for src, dst in plans[i]:
                pltpu.make_async_copy(src, dst, sems.at[i]).wait()

    per = seqs // chips
    ids = [meta[t * per + core * (per // CORES) + base_step + step] for t in range(chips)]
    M = chips * S

    def load_x(i, n):
        t = i // (S // n)
        r = i % (S // n)
        return x_ref[t, 0, pl.ds(pl.multiple_of(r * n, n), n), :]

    norm_tile(load_x, gain_ref, h_scr, M)
    arrive(0)
    for t in range(chips):
        low_scr[pl.ds(t * S, S), :] = dot_nn(h_scr[pl.ds(t * S, S), :], aq[ids[t]]).astype(BF16)
    arrive(1)
    kh = n_dev * half
    zk = dot_nt(h_scr[...], wk[...])
    for t in range(chips):
        z = zk[t * S:(t + 1) * S] + scale * dot_nt(low_scr[pl.ds(t * S, S), rank:2 * rank], bk[ids[t]])
        f, s = z[:, :kh], z[:, kh:]
        k_scr[pl.ds(t * S, S), :kh] = (f * cosk_ref[...] - s * sink_ref[...]).astype(BF16).astype(F32)
        k_scr[pl.ds(t * S, S), kh:] = (s * cosk_ref[...] + f * sink_ref[...]).astype(BF16).astype(F32)
    zv = dot_nt(h_scr[...], wv[...])
    for t in range(chips):
        z = zv[t * S:(t + 1) * S] + scale * dot_nt(low_scr[pl.ds(t * S, S), 2 * rank:], bv[ids[t]])
        v_scr[pl.ds(t * S, S), :] = z.astype(BF16).astype(F32)
    arrive(2)

    lanes = nq * half
    per_vreg = lanes // half
    per_v = lanes // hd

    @pl.loop(0, n_dev)
    def _(g):
        zq = dot_nt(h_scr[...], wq[pl.ds(pl.multiple_of(g * qw, qw), qw), :])
        lane = lax.broadcasted_iota(jnp.int32, (S, lanes), 1)
        row = lax.broadcasted_iota(jnp.int32, (S, S), 0)
        col = lax.broadcasted_iota(jnp.int32, (S, S), 1)
        causal = col <= row
        kbase = pl.multiple_of((g // per_vreg) * lanes, lanes)
        vbase = pl.multiple_of((g // per_v) * lanes, lanes)
        mine_k = (lane // half) == (g % per_vreg)
        mine_v = (lane // hd) == (g % per_v)
        for t in range(chips):
            rows = pl.ds(t * S, S)
            z = zq[t * S:(t + 1) * S] + scale * dot_nt(
                low_scr[rows, :rank], bq[ids[t], pl.ds(pl.multiple_of(g * qw, qw), qw), :])
            f, s = z[:, :lanes], z[:, lanes:]
            q = jnp.concatenate([(f * cosq_ref[...] - s * sinq_ref[...]).astype(BF16),
                                 (s * cosq_ref[...] + f * sinq_ref[...]).astype(BF16)], axis=1)

            def spread(v, mine, width):
                v = jnp.where(mine, v, 0.0)
                while width < lanes:
                    v = v + pltpu.roll(v, width, axis=1)
                    width *= 2
                return v

            kf = spread(k_scr[rows, pl.ds(kbase, lanes)], mine_k, half)
            ks = spread(k_scr[rows, pl.ds(kh + kbase, lanes)], mine_k, half)
            vv = spread(v_scr[rows, pl.ds(vbase, lanes)], mine_v, hd)
            kd, vd = [], []
            for hh in range(nq):
                sel = (lane // half) == hh
                kd.append(jnp.concatenate([jnp.where(sel, kf, 0.0).astype(BF16),
                                           jnp.where(sel, ks, 0.0).astype(BF16)], axis=1))
                parts = []
                for w in range(qw // lanes):
                    if hh // per_v == w:
                        parts.append(jnp.where((lane // hd) == (hh % per_v), vv, 0.0).astype(BF16))
                    else:
                        parts.append(jnp.zeros((S, lanes), BF16))
                vd.append(jnp.concatenate(parts, axis=1))
            sc = dot_nt(q, jnp.concatenate(kd, axis=0))
            ps = []
            for hh in range(nq):
                sh = jnp.where(causal, sc[:, hh * S:(hh + 1) * S], -1e30)
                e = jnp.exp(sh - jnp.max(sh, axis=1, keepdims=True))
                ps.append((e * (1.0 / jnp.sum(e, axis=1, keepdims=True))).astype(BF16))
            o = dot_nn(jnp.concatenate(ps, axis=1), jnp.concatenate(vd, axis=0))
            attn_scr[rows, pl.ds(pl.multiple_of(g * qw, qw), qw)] = o.astype(BF16)

    arrive(3)
    for t in range(chips):
        low_scr[pl.ds(t * S, S), :rank] = dot_nn(attn_scr[pl.ds(t * S, S), :], ao[ids[t]]).astype(BF16)
    nt = 256

    @pl.loop(0, D // nt)
    def _(j):
        cols = pl.ds(pl.multiple_of(j * nt, nt), nt)
        zo = dot_nn(attn_scr[...], wo[:, cols])
        for t in range(chips):
            z = zo[t * S:(t + 1) * S] + scale * dot_nn(low_scr[pl.ds(t * S, S), :rank], bo[ids[t], :, cols])
            out_ref[t, :, cols] = (x_ref[t, 0, :, cols].astype(F32) + z).astype(BF16)


def mlp_body(dims, meta, x_ref, gain_ref, agu_ref, wg0, wg1, wu0, wu1, wd0, wd1, bg0, bg1, bu0, bu1, ad0, ad1,
             out_ref, wg, wu, wd, bg, bu, agu, ad, h_scr, low_scr, hid_scr, sems):
    seqs, S, rank, D, spc, base_step, chips = dims
    scale = ALPHA / rank
    step = pl.program_id(0)
    core = meta[meta.shape[0] - 1]
    fw = wg0.shape[1]
    plans = [[(agu_ref, agu)], [], []]
    for i, (g, u, b1, b2) in enumerate(((wg0, wu0, bg0, bu0), (wg1, wu1, bg1, bu1))):
        c = pl.ds(i * fw, fw)
        plans[1] += [(g, wg.at[:, c]), (u, wu.at[:, c]), (b1, bg.at[:, :, c]), (b2, bu.at[:, :, c])]
    for i, (d, a) in enumerate(((wd0, ad0), (wd1, ad1))):
        c = pl.ds(i * fw, fw)
        plans[2] += [(a, ad.at[:, c]), (d, wd.at[c])]

    @pl.when(step == 0)
    def _():
        for i, plan in enumerate(plans):
            for src, dst in plan:
                pltpu.make_async_copy(src, dst, sems.at[i]).start()

    def arrive(i):
        @pl.when(step == 0)
        def _():
            for src, dst in plans[i]:
                pltpu.make_async_copy(src, dst, sems.at[i]).wait()

    per = seqs // chips
    ids = [meta[t * per + core * (per // CORES) + base_step + step] for t in range(chips)]
    M = chips * S

    def load_x(i, n):
        t = i // (S // n)
        r = i % (S // n)
        return x_ref[t, pl.ds(pl.multiple_of(r * n, n), n), :]

    norm_tile(load_x, gain_ref, h_scr, M)
    arrive(0)
    for t in range(chips):
        low_scr[pl.ds(t * S, S), :] = dot_nn(h_scr[pl.ds(t * S, S), :], agu[ids[t]]).astype(BF16)
    arrive(1)
    nt = 256

    @pl.loop(0, wg.shape[1] // nt)
    def _(j):
        cols = pl.ds(pl.multiple_of(j * nt, nt), nt)
        zg = dot_nn(h_scr[...], wg[:, cols])
        zu = dot_nn(h_scr[...], wu[:, cols])
        for t in range(chips):
            rows = pl.ds(t * S, S)
            g = zg[t * S:(t + 1) * S] + scale * dot_nn(low_scr[rows, :rank], bg[ids[t], :, cols])
            u = zu[t * S:(t + 1) * S] + scale * dot_nn(low_scr[rows, rank:], bu[ids[t], :, cols])
            hid_scr[rows, cols] = (jax.nn.silu(g) * u).astype(BF16)

    arrive(2)
    for t in range(chips):
        out_ref[t, :, D:] = dot_nn(hid_scr[pl.ds(t * S, S), :], ad[ids[t]]).astype(BF16)

    @pl.loop(0, D // nt)
    def _(j):
        cols = pl.ds(pl.multiple_of(j * nt, nt), nt)
        z = dot_nn(hid_scr[...], wd[:, cols])
        for t in range(chips):
            out_ref[t, :, cols] = z[t * S:(t + 1) * S].astype(BF16)


def finish_body(dims, meta, x_ref, rs_ref, bd_ref, out_ref):
    rank, D = dims
    scale = ALPHA / rank
    nt = 256
    low = rs_ref[0, :, D:]

    @pl.loop(0, D // nt)
    def _(j):
        cols = pl.ds(pl.multiple_of(j * nt, nt), nt)
        delta = scale * dot_nn(low, bd_ref[0, :, cols])
        out_ref[0, :, cols] = (x_ref[0, 0, :, cols].astype(F32) + rs_ref[0, :, cols].astype(F32) + delta).astype(BF16)


def solution(mesh):
    n_dev = mesh.shape['tensor']
    chips = n_dev // CORES
    head_split = P(None, 'tensor', None)
    last_split = P(None, None, 'tensor')
    b_head_split = P(None, None, 'tensor', None)
    in_specs = (P('data', None, None), P('data'), P(None), P(None),
                head_split, head_split, head_split, P('tensor', None, None),
                P(None, 'tensor'), P(None, 'tensor'), P('tensor', None),
                last_split, b_head_split, last_split, b_head_split, last_split, b_head_split,
                P(None, 'tensor', None, None), last_split,
                last_split, last_split, last_split, last_split,
                P(None, 'tensor', None), last_split)
    same_core = [[c + CORES * i for i in range(chips)] for c in range(CORES)]
    swap = [(i, i ^ 1) for i in range(n_dev)]
    ANY = pl.BlockSpec(memory_space=pl.ANY)

    def local_layer(x_in, adapter_ids, gain_attn, gain_mlp, w_q, w_k, w_v, w_o, w_gate, w_up, w_down, a_q, b_q, a_k, b_k, a_v, b_v, a_o, b_o, a_gate, b_gate, a_up, b_up, a_down, b_down):
        seqs, S, D = x_in.shape
        nq, hd = w_q.shape[1], w_q.shape[2]
        n_ad, rank = b_q.shape[0], b_q.shape[1]
        rl = a_q.shape[2]
        half = hd // 2
        qw = nq * hd
        me = lax.axis_index('tensor')
        core, chip = me % CORES, me // CORES
        meta = jnp.concatenate([adapter_ids.astype(jnp.int32), core.reshape(1).astype(jnp.int32)])
        per = seqs // chips
        steps = per // CORES
        spc = steps // CHUNKS

        def rows_t(w):
            return jnp.transpose(w, (1, 2, 0)).reshape(-1, w.shape[0])

        def split_halves(wt, heads):
            return wt.reshape(heads, 2, half, -1).transpose(1, 0, 2, 3).reshape(heads * hd, -1)

        gather = functools.partial(lax.all_gather, axis_name='tensor', axis=0)
        swapped = functools.partial(lax.ppermute, axis_name='tensor', perm=swap)

        g_a = gather(jnp.concatenate([jnp.transpose(a, (0, 2, 1)).reshape(n_ad * rl, D)
                                      for a in (a_q, a_k, a_v, a_gate, a_up)], axis=0))
        g_a = g_a.reshape(n_dev, 5, n_ad, rl, D)
        a_qkv = g_a[:, :3].transpose(2, 4, 1, 0, 3).reshape(n_ad, D, 3 * rank)
        a_gu = g_a[:, 3:].transpose(2, 4, 1, 0, 3).reshape(n_ad, D, 2 * rank)
        g_w = gather(jnp.concatenate([split_halves(rows_t(w_q), nq), rows_t(w_k), rows_t(w_v)], axis=0))

        def b_rows(b):
            return jnp.transpose(b, (1, 2, 0)).reshape(-1, rank)

        b_parts = []
        for a in range(n_ad):
            b_parts += [split_halves(b_rows(b_q[a]), nq), b_rows(b_k[a]), b_rows(b_v[a])]
        b_parts += [a_o.reshape(n_ad * qw, rank), b_o.reshape(n_ad * rank, qw)]
        g_b = gather(jnp.concatenate(b_parts, axis=0))
        g_wo = gather(w_o.reshape(qw, D))
        g_bd = gather(b_down.reshape(n_ad * rank, qw))
        bd_full = g_bd.reshape(n_dev, n_ad, rank, qw).transpose(1, 2, 0, 3).reshape(n_ad, rank, D)
        mlp_own = (w_gate, w_up, w_down, b_gate, b_up, a_down)
        mlp_other = tuple(swapped(w) for w in mlp_own)

        inv_freq = ROPE_BASE ** (-2.0 * jnp.arange(half, dtype=F32) / hd)
        ang = jnp.arange(S, dtype=F32)[:, None] * inv_freq[None, :]
        cos, sin = jnp.cos(ang), jnp.sin(ang)
        qs = hd ** -0.5
        cosq, sinq = jnp.tile(cos, (1, nq)) * qs, jnp.tile(sin, (1, nq)) * qs
        cosk, sink = jnp.tile(cos, (1, n_dev)), jnp.tile(sin, (1, n_dev))

        x4 = x_in.reshape(chips, per, S, D)
        M = chips * S
        Fc = CORES * w_gate.shape[1]
        full = lambda shape: pl.BlockSpec(shape, lambda i, m: (0,) * len(shape))
        params = pltpu.CompilerParams(vmem_limit_bytes=VMEM_LIMIT, dimension_semantics=("arbitrary",))
        y = jnp.zeros((n_dev, steps * S, D), BF16)
        for c in range(CHUNKS):
            base_step = c * spc
            tok = M * spc
            x1 = pl.pallas_call(
                functools.partial(attn_body, (n_dev, seqs, S, hd, nq, rank, D, spc, base_step, chips)),
                grid_spec=pltpu.PrefetchScalarGridSpec(
                    num_scalar_prefetch=1, grid=(spc,),
                    in_specs=[pl.BlockSpec((chips, 1, S, D), lambda i, m, b=base_step: (0, m[seqs] * steps + b + i, 0, 0)),
                              full((1, D)), full((S, nq * half)), full((S, nq * half)),
                              full((S, n_dev * half)), full((S, n_dev * half)), ANY, ANY, ANY, ANY],
                    out_specs=pl.BlockSpec((chips, S, D), lambda i, m: (0, i, 0)),
                    scratch_shapes=[
                        pltpu.VMEM((n_dev * qw, D), BF16), pltpu.VMEM((n_dev * hd, D), BF16), pltpu.VMEM((n_dev * hd, D), BF16),
                        pltpu.VMEM((n_ad, D, 3 * rank), BF16),
                        pltpu.VMEM((n_ad, n_dev * qw, rank), BF16), pltpu.VMEM((n_ad, n_dev * hd, rank), BF16),
                        pltpu.VMEM((n_ad, n_dev * hd, rank), BF16),
                        pltpu.VMEM((n_dev * qw, D), BF16), pltpu.VMEM((n_ad, n_dev * qw, rank), BF16),
                        pltpu.VMEM((n_ad, rank, n_dev * qw), BF16),
                        pltpu.VMEM((M, D), BF16), pltpu.VMEM((M, 3 * rank), BF16),
                        pltpu.VMEM((M, n_dev * hd), F32), pltpu.VMEM((M, n_dev * hd), F32),
                        pltpu.VMEM((M, n_dev * qw), BF16), pltpu.SemaphoreType.DMA((4,))]),
                out_shape=jax.ShapeDtypeStruct((chips, spc * S, D), BF16),
                compiler_params=params, name="attn_block",
                cost_estimate=pl.CostEstimate(flops=2 * tok * D * (2 * n_dev * qw + 2 * n_dev * hd + 5 * rank) * 3 // 2,
                                              bytes_accessed=4 * tok * D + 33 * 2**20, transcendentals=0),
            )(meta, x4, gain_attn.reshape(1, D), cosq, sinq, cosk, sink, g_w, a_qkv, g_b, g_wo)
            pairs = [w for own, other in zip(mlp_own, mlp_other) for w in (own, other)]
            part = pl.pallas_call(
                functools.partial(mlp_body, (seqs, S, rank, D, spc, base_step, chips)),
                grid_spec=pltpu.PrefetchScalarGridSpec(
                    num_scalar_prefetch=1, grid=(spc,),
                    in_specs=[pl.BlockSpec((chips, S, D), lambda i, m: (0, i, 0)), full((1, D))] + [ANY] * 13,
                    out_specs=pl.BlockSpec((chips, S, D + rank), lambda i, m: (0, i, 0)),
                    scratch_shapes=[
                        pltpu.VMEM((D, Fc), BF16), pltpu.VMEM((D, Fc), BF16), pltpu.VMEM((Fc, D), BF16),
                        pltpu.VMEM((n_ad, rank, Fc), BF16), pltpu.VMEM((n_ad, rank, Fc), BF16),
                        pltpu.VMEM((n_ad, D, 2 * rank), BF16), pltpu.VMEM((n_ad, Fc, rank), BF16),
                        pltpu.VMEM((M, D), BF16), pltpu.VMEM((M, 2 * rank), BF16), pltpu.VMEM((M, Fc), BF16),
                        pltpu.SemaphoreType.DMA((3,))]),
                out_shape=jax.ShapeDtypeStruct((chips, spc * S, D + rank), BF16),
                compiler_params=params, name="mlp_block",
                cost_estimate=pl.CostEstimate(flops=2 * tok * D * (3 * Fc + 4 * rank),
                                              bytes_accessed=4 * tok * D + 34 * 2**20, transcendentals=tok * Fc),
            )(meta, x1, gain_mlp.reshape(1, D), a_gu, *pairs)
            rs = lax.psum_scatter(part, 'tensor', scatter_dimension=0, axis_index_groups=same_core, tiled=True)
            own = [adapter_ids[chip * per + core * steps + base_step + i] for i in range(spc)]
            meta2 = jnp.concatenate([jnp.stack(own).astype(jnp.int32), chip.reshape(1).astype(jnp.int32)])
            y_own = pl.pallas_call(
                functools.partial(finish_body, (rank, D)),
                grid_spec=pltpu.PrefetchScalarGridSpec(
                    num_scalar_prefetch=1, grid=(spc,),
                    in_specs=[pl.BlockSpec((1, 1, S, D), lambda i, m: (m[spc], i, 0, 0)),
                              pl.BlockSpec((1, S, D + rank), lambda i, m: (i, 0, 0)),
                              pl.BlockSpec((1, rank, D), lambda i, m: (m[i], 0, 0))],
                    out_specs=pl.BlockSpec((1, S, D), lambda i, m: (i, 0, 0))),
                out_shape=jax.ShapeDtypeStruct((spc, S, D), BF16),
                compiler_params=pltpu.CompilerParams(dimension_semantics=("arbitrary",)), name="finish",
                cost_estimate=pl.CostEstimate(flops=2 * spc * S * rank * D, bytes_accessed=10 * spc * S * D, transcendentals=0),
            )(meta2, x1.reshape(chips, spc, S, D), rs.reshape(spc, S, D + rank), bd_full)
            y_all = gather(y_own.reshape(spc * S, D))
            y = lax.dynamic_update_slice(y, y_all, (0, base_step * S, 0))
        return y.reshape(seqs, S, D)

    return jax.shard_map(local_layer, mesh=mesh, in_specs=in_specs, out_specs=P('data', None, None), check_vma=False)
```

time: 1350 us -> 1070 us (0.79)
  Pallas kernels: 0 us -> 603 us
  matrix products: 452 us -> 0 us
  waiting for transfers between devices: 707 us -> 344 us
  other arithmetic: 47.4 us -> 9.69 us
  local copies, waits for them, and re-layouts: 117 us -> 82.5 us
    pallas_call x0 -> x12, Pallas kernels: none -> 603 us  [the longest x4 365 us: local_layer(): pl.pallas_call(functools.partial(attn_body, (n_dev, seqs, S, hd, nq, rank...]
    dot_general x21 -> x0, matrix products: 442 us -> none  [the longest x4 148 us: column_proj(): jnp.einsum(base_form, act_in, weight, preferred_element_type=jnp.float32)]
    reduce_scatter x2 -> x4, waiting for transfers between devices: 340 us -> 14.7 us  [local_layer(): lax.psum_scatter(part, 'tensor', scatter_dimension=0, axis_index_groups=s...]
    gather x14 -> x0, local copies, waits for them, and re-layouts: 89.4 us -> none  [per_sequence(): return jnp.take(table_stack, adapter_ids, axis=0)]
    psum x2 -> x0, waiting for transfers between devices: 52.9 us -> none  [row_proj(): low_rank = lax.psum(low_part, 'tensor')]
    dynamic_update_slice x0 -> x4, local copies, waits for them, and re-layouts: none -> 38.8 us  [local_layer(): y = lax.dynamic_update_slice(y, y_all, (0, base_step * S, 0))]
    reduce_sum x3 -> x0, other arithmetic: 33.1 us -> none  [the longest x2 22.7 us: rms_gain(): jnp.mean(act_f32 * act_f32, axis=-1, keepdims=True) + EPSILON]
    unnamed x47 -> x37, local copies, waits for them, and re-layouts: 26.9 us -> 6.29 us
  transfers between devices with their start and end apart: 11 -> 19, of which waited for: 6 -> 9; matrix products, arithmetic and copies ran while one was open for 27% -> 7% of each run, Pallas kernels for 0% -> 57%
where the time goes in v1:
time: 1070 us; the launch traced here: 1060 us
  Pallas kernels  603 us (56%)
  waiting for transfers between devices  344 us (32%)
  local copies, waits for them, and re-layouts  82.5 us (8%)
  between operations  14.2 us (1%)
    pallas_call x4, Pallas kernels, local_layer(): pl.pallas_call(functools.partial(attn_body, (n_dev, seqs, S, hd, nq, rank...  365 us
    pallas_call x4, Pallas kernels, local_layer(): pl.pallas_call(functools.partial(mlp_body, (seqs, S, rank, D, spc, base_s...  215 us
    all_gather x4, waiting for transfers between devices, local_layer(): y_all = gather(y_own.reshape(spc * S, D))  153 us
    all_gather x1, waiting for transfers between devices, local_layer(): gather(jnp.concatenate([split_halves(rows_t(w_q), nq), rows_t(w_k), rows_...  64.9 us
    all_gather x1, waiting for transfers between devices, local_layer(): gather(jnp.concatenate([jnp.transpose(a, (0, 2, 1)).reshape(n_ad * rl, D)...  47.3 us
    all_gather x1, waiting for transfers between devices, local_layer(): g_wo = gather(w_o.reshape(qw, D))  47.3 us
    dynamic_update_slice x4, local copies, waits for them, and re-layouts, local_layer(): y = lax.dynamic_update_slice(y, y_all, (0, base_step * S, 0))  38.8 us
    pallas_call x4, Pallas kernels, local_layer(): pl.pallas_call(functools.partial(finish_body, (rank, D)), grid_spec=pltpu...  23.7 us
  transfers between devices with their start and end apart: 19, of which 9 were waited for; matrix products, arithmetic and copies ran while one was open for 7% of the time, Pallas kernels for 57%

profile of v1, /device:TPU:113, one launch (start us, length us, event | category | flops | bytes accessed | tf_op | source)
XLA Modules:
  0.0 1057.5 jit_solution(11477935261369492312)
XLA Ops:
  6.6 1.0 constant_dynamic-update-slice_fusion.4
  7.7 1.1 constant_dynamic-update-slice_fusion.3
  8.7 1.0 constant_dynamic-update-slice_fusion.2
  9.7 1.0 constant_dynamic-update-slice_fusion.1
  10.7 1.0 constant_dynamic-update-slice_fusion
  11.7 1.0 copy-done
  12.8 1.0 fusion.2
  14.1 0.9 copy-done.1
  16.1 1.3 pad_maximum_fusion
  17.5 0.8 collective-permute-start.3
  21.1 0.8 copy.67.sink_ref
  23.3 47.3 %all-gather.27.cloned.1.call-done = bf16[2560,2048]{1,0:T(8,128)(2,1)} async-done(((bf16[320,2048]{1,0:T(8,128)(2,1)}), bf16[2560,2048]{1,0:T(8,128)(2,1)}) %all-gather.27.cloned.1.call-update) | async-done | bytes 10485776 | tf_op jit(solution)/shard_map/all_gather | solution.py:298
  70.6 3.4 slice_bitcast_fusion
  73.9 3.3 copy.61
  77.2 8.6 copy.68.aqkv_ref
  85.9 2.5 slice_bitcast_fusion.1
  88.4 2.3 copy.69
  90.7 6.4 copy.70.agu_ref
  97.3 16.1 %all-gather.29.cloned.1.call-done = bf16[14336,256]{1,0:T(8,128)(2,1)} async-done(((bf16[1792,256]{1,0:T(8,128)(2,1)}), bf16[14336,256]{1,0:T(8,128)(2,1)}) %all-gather.29.cloned.1.call-update) | async-done | bytes 7340048 | tf_op jit(solution)/shard_map/all_gather | solution.py:312
  113.5 47.3 %all-gather.13.cloned.1.call-done.gwo_ref = bf16[8,256,2048]{2,1,0:T(8,128)(2,1)} async-done(((bf16[1,256,2048]{2,1,0:T(8,128)(2,1)}), bf16[8,256,2048]{2,1,0:T(8,128)(2,1)}) %all-gather.13.cloned.1.call-update) | async-done | bytes 8388624 | tf_op jit(solution)/shard_map/all_gather | solution.py:313
  160.7 64.9 %all-gather.25.cloned.1.call-done = bf16[3072,2048]{1,0:T(8,128)(2,1)} async-done(((bf16[384,2048]{1,0:T(8,128)(2,1)}), bf16[3072,2048]{1,0:T(8,128)(2,1)}) %all-gather.25.cloned.1.call-update) | async-done | bytes 12582928 | tf_op jit(solution)/shard_map/all_gather | solution.py:303
  225.7 91.1 %attn_block.4.x_ref = bf16[4,256,2048]{2,1,0:T(8,128)(2,1)} custom-call(s32[65]{0:T(128)} %pad_add_fusion.meta, bf16[4,16,128,2048]{3,2,1,0:T(8,128)(2,1)} %bitcast.147, f32[1,2048]{1,0:T(1,128)} %bitcast.159, f32[128,128]{1,0:T(8,128)} %copy.64.cosq_ref, f32[128,128]{1,0:T(8,128)} %copy.65.sinq_ref, f32[128,256]{1,0:T(8,128)} %copy.66.cosk_ref, ...), custom_call_target="tpu_custom_call" | custom-call | flops 40265318400 | bytes 42991616 | tf_op jit(solution)/shard_map/attn_block/pallas_call | solution.py:335
  316.9 54.0 %mlp_block.4 = bf16[4,256,2304]{2,1,0:T(8,128)(2,1)} custom-call(s32[65]{0:T(128)} %pad_add_fusion.meta, bf16[4,256,2048]{2,1,0:T(8,128)(2,1)} %attn_block.4.x_ref, f32[1,2048]{1,0:T(1,128)} %bitcast.163, bf16[2,2048,512]{2,1,0:T(8,128)(2,1)} %copy.70.agu_ref, bf16[2048,1024]{1,0:T(8,128)(2,1)} %wg0.7, bf16[2048,1024]{1,0:T(8,128)(2,1)} %collective-permute-done.wg1, ...), custom_call_target="tpu_custom_call" | custom-call | flops 30064771072 | bytes 44040192 | tf_op jit(solution)/shard_map/mlp_block/pallas_call | solution.py:359
  371.0 91.1 %attn_block.5.x_ref = bf16[4,256,2048]{2,1,0:T(8,128)(2,1)} custom-call(s32[65]{0:T(128)} %pad_add_fusion.meta, bf16[4,16,128,2048]{3,2,1,0:T(8,128)(2,1)} %bitcast.148, f32[1,2048]{1,0:T(1,128)} %bitcast.160, f32[128,128]{1,0:T(8,128)} %copy.64.cosq_ref, f32[128,128]{1,0:T(8,128)} %copy.65.sinq_ref, f32[128,256]{1,0:T(8,128)} %copy.66.cosk_ref, ...), custom_call_target="tpu_custom_call" | custom-call | flops 40265318400 | bytes 42991616 | tf_op jit(solution)/shard_map/attn_block/pallas_call | solution.py:335
  462.1 53.6 %mlp_block.5 = bf16[4,256,2304]{2,1,0:T(8,128)(2,1)} custom-call(s32[65]{0:T(128)} %pad_add_fusion.meta, bf16[4,256,2048]{2,1,0:T(8,128)(2,1)} %attn_block.5.x_ref, f32[1,2048]{1,0:T(1,128)} %bitcast.164, bf16[2,2048,512]{2,1,0:T(8,128)(2,1)} %copy.70.agu_ref, bf16[2048,1024]{1,0:T(8,128)(2,1)} %wg0.7, bf16[2048,1024]{1,0:T(8,128)(2,1)} %collective-permute-done.wg1, ...), custom_call_target="tpu_custom_call" | custom-call | flops 30064771072 | bytes 44040192 | tf_op jit(solution)/shard_map/mlp_block/pallas_call | solution.py:359
  515.9 91.3 %attn_block.6.x_ref = bf16[4,256,2048]{2,1,0:T(8,128)(2,1)} custom-call(s32[65]{0:T(128)} %pad_add_fusion.meta, bf16[4,16,128,2048]{3,2,1,0:T(8,128)(2,1)} %bitcast.149, f32[1,2048]{1,0:T(1,128)} %bitcast.161, f32[128,128]{1,0:T(8,128)} %copy.64.cosq_ref, f32[128,128]{1,0:T(8,128)} %copy.65.sinq_ref, f32[128,256]{1,0:T(8,128)} %copy.66.cosk_ref, ...), custom_call_target="tpu_custom_call" | custom-call | flops 40265318400 | bytes 42991616 | tf_op jit(solution)/shard_map/attn_block/pallas_call | solution.py:335
  607.2 53.7 %mlp_block.6 = bf16[4,256,2304]{2,1,0:T(8,128)(2,1)} custom-call(s32[65]{0:T(128)} %pad_add_fusion.meta, bf16[4,256,2048]{2,1,0:T(8,128)(2,1)} %attn_block.6.x_ref, f32[1,2048]{1,0:T(1,128)} %bitcast.165, bf16[2,2048,512]{2,1,0:T(8,128)(2,1)} %copy.70.agu_ref, bf16[2048,1024]{1,0:T(8,128)(2,1)} %wg0.7, bf16[2048,1024]{1,0:T(8,128)(2,1)} %collective-permute-done.wg1, ...), custom_call_target="tpu_custom_call" | custom-call | flops 30064771072 | bytes 44040192 | tf_op jit(solution)/shard_map/mlp_block/pallas_call | solution.py:359
  661.0 91.3 %attn_block.7.x_ref = bf16[4,256,2048]{2,1,0:T(8,128)(2,1)} custom-call(s32[65]{0:T(128)} %pad_add_fusion.meta, bf16[4,16,128,2048]{3,2,1,0:T(8,128)(2,1)} %bitcast.150, f32[1,2048]{1,0:T(1,128)} %bitcast.162, f32[128,128]{1,0:T(8,128)} %copy.64.cosq_ref, f32[128,128]{1,0:T(8,128)} %copy.65.sinq_ref, f32[128,256]{1,0:T(8,128)} %copy.66.cosk_ref, ...), custom_call_target="tpu_custom_call" | custom-call | flops 40265318400 | bytes 42991616 | tf_op jit(solution)/shard_map/attn_block/pallas_call | solution.py:335
  752.3 53.7 %mlp_block.7 = bf16[4,256,2304]{2,1,0:T(8,128)(2,1)} custom-call(s32[65]{0:T(128)} %pad_add_fusion.meta, bf16[4,256,2048]{2,1,0:T(8,128)(2,1)} %attn_block.7.x_ref, f32[1,2048]{1,0:T(1,128)} %bitcast.166, bf16[2,2048,512]{2,1,0:T(8,128)(2,1)} %copy.70.agu_ref, bf16[2048,1024]{1,0:T(8,128)(2,1)} %wg0.7, bf16[2048,1024]{1,0:T(8,128)(2,1)} %collective-permute-done.wg1, ...), custom_call_target="tpu_custom_call" | custom-call | flops 30064771072 | bytes 44040192 | tf_op jit(solution)/shard_map/mlp_block/pallas_call | solution.py:359
  807.3 2.0 add_add_fusion.meta
  809.3 2.8 copy.91
  812.1 2.4 reshape.202.bd_ref
  814.5 5.9 finish.4
  820.5 1.9 add_add_fusion.1.meta
  822.4 5.9 finish.5
  828.5 1.9 add_add_fusion.2.meta
  830.4 5.9 finish.6
  836.4 1.9 add_add_fusion.3.meta
  838.3 14.7 %reduce-scatter.11.cloned.1.call-done = bf16[1,256,2304]{2,1,0:T(8,128)(2,1)} async-done(((bf16[4,256,2304]{2,1,0:T(8,128)(2,1)}), bf16[1,256,2304]{2,1,0:T(8,128)(2,1)}) %reduce-scatter.11.cloned.1.call-update) | async-done | bytes 1179664 | tf_op jit(solution)/shard_map/reduce_scatter | solution.py:376
  853.0 5.9 finish.7
  859.0 41.3 %all-gather.17.cloned.1.call-done = bf16[8,256,2048]{2,1,0:T(8,128)(2,1)} async-done(((bf16[1,256,2048]{2,1,0:T(8,128)(2,1)}), bf16[8,256,2048]{2,1,0:T(8,128)(2,1)}) %all-gather.17.cloned.1.call-update) | async-done | bytes 8388624 | tf_op jit(solution)/shard_map/all_gather | solution.py:391
  900.3 13.5 %dynamic_update_slice.12 = bf16[8,1024,2048]{2,1,0:T(8,128)(2,1)} pad(bf16[8,256,2048]{2,1,0:T(8,128)(2,1)} %all-gather.17.cloned.1.call-done, bf16[]{:T(256)} %constant.62.clone.1), padding=0_0x0_768x0_0 | pad | bytes 41943040 | tf_op jit(solution)/shard_map/dynamic_update_slice | solution.py:392
  913.8 33.8 %all-gather.19.cloned.1.call-done = bf16[8,256,2048]{2,1,0:T(8,128)(2,1)} async-done(((bf16[1,256,2048]{2,1,0:T(8,128)(2,1)}), bf16[8,256,2048]{2,1,0:T(8,128)(2,1)}) %all-gather.19.cloned.1.call-update) | async-done | bytes 8388624 | tf_op jit(solution)/shard_map/all_gather | solution.py:391
  947.6 8.4 constant_dynamic-update-slice_fusion.11
  956.0 38.7 %all-gather.21.cloned.1.call-done = bf16[8,256,2048]{2,1,0:T(8,128)(2,1)} async-done(((bf16[1,256,2048]{2,1,0:T(8,128)(2,1)}), bf16[8,256,2048]{2,1,0:T(8,128)(2,1)}) %all-gather.21.cloned.1.call-update) | async-done | bytes 8388624 | tf_op jit(solution)/shard_map/all_gather | solution.py:391
  994.7 8.4 constant_dynamic-update-slice_fusion.10
  1003.2 38.8 %all-gather.23.cloned.1.call-done = bf16[8,256,2048]{2,1,0:T(8,128)(2,1)} async-done(((bf16[1,256,2048]{2,1,0:T(8,128)(2,1)}), bf16[8,256,2048]{2,1,0:T(8,128)(2,1)}) %all-gather.23.cloned.1.call-update) | async-done | bytes 8388624 | tf_op jit(solution)/shard_map/all_gather | solution.py:391
  1042.0 8.4 constant_dynamic-update-slice_fusion.9
  (87 shorter events, 7.9 us)
Async XLA Ops:
  6.5 7.3 copy-start.7
  6.5 7.4 copy-start.8
  6.6 7.4 copy-start.5
  6.6 7.5 copy-start.6
  6.6 64.0 %all-gather.27.cloned.1.call-start = ((), (), s32[]{:S(2)}) async-start(), calls=%async_computation.15 | async-start | bytes 11796480 | tf_op jit(solution)/shard_map/all_gather | solution.py:298
  7.7 8.3 copy-start.2
  11.6 1.1 copy-start
  11.7 4.4 copy-start.3
  11.7 4.4 copy-start.4
  12.8 100.7 %all-gather.29.cloned.1.call-start = ((), (), s32[]{:S(2)}) async-start(), calls=%async_computation.16 | async-start | bytes 8257536 | tf_op jit(solution)/shard_map/all_gather | solution.py:312
  14.1 0.9 copy-start.1
  15.0 2.4 copy-start.11
  15.1 145.7 %all-gather.13.cloned.1.call-start = ((), (), s32[]{:S(2)}) async-start(), calls=%async_computation.4 | async-start | bytes 9437184 | tf_op jit(solution)/shard_map/all_gather | solution.py:313
  15.9 209.8 %all-gather.25.cloned.1.call-start = ((), (), s32[]{:S(2)}) async-start(), calls=%async_computation.14 | async-start | bytes 14155776 | tf_op jit(solution)/shard_map/all_gather | solution.py:303
  15.9 6.7 copy-start.9
  17.4 791.9 %all-gather.15.cloned.1.call-start = ((), (), s32[]{:S(2)}) async-start(), calls=%async_computation.6 | async-start | bytes 2359296 | tf_op jit(solution)/shard_map/all_gather | solution.py:314
  17.5 79.6 %collective-permute-start.3 = (bf16[2,256,1024]{2,1,0:T(8,128)(2,1)S(1)}, bf16[2,256,1024]{2,1,0:T(8,128)(2,1)}, u32[]{:S(2)}, u32[]{:S(2)}) collective-permute-start(bf16[2,256,1024]{2,1,0:T(8,128)(2,1)S(1)} %copy-done.11), channel_id=1, source_target_pairs={{0,1},{1,0},{2,3},{3,2},{4,5},{5,4},{6,7},{7,6},{8,9},{9,8},{10,11... | collective-permute-start | bytes 3145736 | tf_op jit(solution)/shard_map/ppermute | solution.py:317
  18.3 298.5 %collective-permute-start.4 = (bf16[2,256,1024]{2,1,0:T(8,128)(2,1)}, bf16[2,256,1024]{2,1,0:T(8,128)(2,1)}, u32[]{:S(2)}, u32[]{:S(2)}) collective-permute-start(bf16[2,256,1024]{2,1,0:T(8,128)(2,1)} %bu0.7), channel_id=1, source_target_pairs={{0,1},{1,0},{2,3},{3,2},{4,5},{5,4},{6,7},{7,6},{8,9},{9,8},{10,11... | collective-permute-start | bytes 3145736 | tf_op jit(solution)/shard_map/ppermute | solution.py:317
  18.4 298.4 %collective-permute-start = (bf16[2048,1024]{1,0:T(8,128)(2,1)}, bf16[2048,1024]{1,0:T(8,128)(2,1)}, u32[]{:S(2)}, u32[]{:S(2)}) collective-permute-start(bf16[2048,1024]{1,0:T(8,128)(2,1)} %wg0.7), channel_id=1, source_target_pairs={{0,1},{1,0},{2,3},{3,2},{4,5},{5,4},{6,7},{7,6},{8,9},{9,8},{10,11... | collective-permute-start | bytes 12582920 | tf_op jit(solution)/shard_map/ppermute | solution.py:317
  18.8 298.0 %collective-permute-start.1 = (bf16[2048,1024]{1,0:T(8,128)(2,1)}, bf16[2048,1024]{1,0:T(8,128)(2,1)}, u32[]{:S(2)}, u32[]{:S(2)}) collective-permute-start(bf16[2048,1024]{1,0:T(8,128)(2,1)} %wu0.7), channel_id=1, source_target_pairs={{0,1},{1,0},{2,3},{3,2},{4,5},{5,4},{6,7},{7,6},{8,9},{9,8},{10,11... | collective-permute-start | bytes 12582920 | tf_op jit(solution)/shard_map/ppermute | solution.py:317
  18.9 297.9 %collective-permute-start.2 = (bf16[1024,2048]{1,0:T(8,128)(2,1)}, bf16[1024,2048]{1,0:T(8,128)(2,1)}, u32[]{:S(2)}, u32[]{:S(2)}) collective-permute-start(bf16[1024,2048]{1,0:T(8,128)(2,1)} %wd0.7), channel_id=1, source_target_pairs={{0,1},{1,0},{2,3},{3,2},{4,5},{5,4},{6,7},{7,6},{8,9},{9,8},{10,11... | collective-permute-start | bytes 12582920 | tf_op jit(solution)/shard_map/ppermute | solution.py:317
  19.4 795.1 %reduce-scatter.5.cloned.1.call-start = ((), (), s32[]{:S(2)}) async-start(), calls=%async_computation.5 | async-start | bytes 5898240 | tf_op jit(solution)/shard_map/reduce_scatter | solution.py:376
  90.7 6.4 copy-start.12
  97.1 219.7 %collective-permute-start.5 = (bf16[2,1024,256]{2,1,0:T(8,128)(2,1)S(1)}, bf16[2,1024,256]{2,1,0:T(8,128)(2,1)}, u32[]{:S(2)}, u32[]{:S(2)}) collective-permute-start(bf16[2,1024,256]{2,1,0:T(8,128)(2,1)S(1)} %copy-done.12), channel_id=1, source_target_pairs={{0,1},{1,0},{2,3},{3,2},{4,5},{5,4},{6,7},{7,6},{8,9},{9,8},{10,11... | collective-permute-start | bytes 3145736 | tf_op jit(solution)/shard_map/ppermute | solution.py:317
  370.9 451.5 %reduce-scatter.7.cloned.1.call-start = ((), (), s32[]{:S(2)}) async-start(), calls=%async_computation.8 | async-start | bytes 5898240 | tf_op jit(solution)/shard_map/reduce_scatter | solution.py:376
  515.8 314.6 %reduce-scatter.9.cloned.1.call-start = ((), (), s32[]{:S(2)}) async-start(), calls=%async_computation.10 | async-start | bytes 5898240 | tf_op jit(solution)/shard_map/reduce_scatter | solution.py:376
  660.9 192.1 %reduce-scatter.11.cloned.1.call-start = ((), (), s32[]{:S(2)}) async-start(), calls=%async_computation.12 | async-start | bytes 5898240 | tf_op jit(solution)/shard_map/reduce_scatter | solution.py:376
  806.0 0.7 copy-start.10
  806.1 94.2 %all-gather.17.cloned.1.call-start = ((), (), s32[]{:S(2)}) async-start(), calls=%async_computation.7 | async-start | bytes 9437184 | tf_op jit(solution)/shard_map/all_gather | solution.py:391
  820.4 127.2 %all-gather.19.cloned.1.call-start = ((), (), s32[]{:S(2)}) async-start(), calls=%async_computation.9 | async-start | bytes 9437184 | tf_op jit(solution)/shard_map/all_gather | solution.py:391
  828.4 166.3 %all-gather.21.cloned.1.call-start = ((), (), s32[]{:S(2)}) async-start(), calls=%async_computation.11 | async-start | bytes 9437184 | tf_op jit(solution)/shard_map/all_gather | solution.py:391
  836.4 205.7 %all-gather.23.cloned.1.call-start = ((), (), s32[]{:S(2)}) async-start(), calls=%async_computation.13 | async-start | bytes 9437184 | tf_op jit(solution)/shard_map/all_gather | solution.py:391
Sparse Core Ops, SparseCore 0:
  12.9 57.6 all-gather.26
  72.2 41.2 all-gather.28
  115.1 45.5 all-gather.12
  162.2 63.4 all-gather.24
  227.1 21.4 all-gather.14
  371.0 46.8 reduce-scatter.4
  515.9 46.8 reduce-scatter.6
  661.0 46.7 reduce-scatter.8
  806.2 46.7 reduce-scatter.10
  854.5 45.8 all-gather.16
  901.9 45.6 all-gather.18
  949.1 45.6 all-gather.20
  996.3 45.6 all-gather.22

commit v2 on v1

v2 whole, which is shorter than its diff:
```python
import functools

import jax
import jax.numpy as jnp
from jax import lax
from jax.experimental import pallas as pl
from jax.experimental.pallas import tpu as pltpu
from jax.sharding import PartitionSpec as P

ALPHA = 16.0
ROPE_BASE = 10000.0
EPSILON = 1e-5
CORES = 2
CHUNKS = 4
VMEM_LIMIT = 62 * 1024 * 1024
F32, BF16 = jnp.float32, jnp.bfloat16


def dot_nn(a, b):
    return lax.dot_general(a, b, (((1,), (0,)), ((), ())), preferred_element_type=F32)


def dot_nt(a, b):
    return lax.dot_general(a, b, (((1,), (1,)), ((), ())), preferred_element_type=F32)


def norm_tile(load_rows, gain_ref, dst_ref, n_rows):
    step_rows = 16

    @pl.loop(0, n_rows // step_rows)
    def _(i):
        v = load_rows(i, step_rows).astype(F32)
        inv = lax.rsqrt(jnp.mean(v * v, axis=-1, keepdims=True) + EPSILON)
        rows = pl.ds(pl.multiple_of(i * step_rows, step_rows), step_rows)
        dst_ref[rows, :] = (v * inv * gain_ref[...]).astype(BF16)


def attn_body(dims, ids_ref, x_ref, gain_ref, cos_ref, sin_ref, gw_ref, aqkv_ref, gb_ref, gwo_ref, out_ref,
              h, low, attn, w, bw, q_scr, k_scr, v_scr, lowo, wsem, xsem, osem):
    n_dev, seqs, S, hd, nq, rank, D, chips = dims
    half = hd // 2
    qw = nq * hd
    n_ad = 2
    scale = ALPHA / rank
    core = lax.axis_index('tensor') % CORES
    per = seqs // chips
    steps = per // CORES
    M = chips * S
    pw = CORES * (qw + 2 * hd)
    kw = CORES * qw
    vw = kw + CORES * hd

    def seq_id(i, t):
        return ids_ref[t * per + core * steps + i]

    def tile(i):
        return pl.ds(pl.multiple_of(i * M, M), M)

    a_rows = n_ad * 3 * rank
    x_base = 4 * M
    plan_a = [(aqkv_ref, attn.at[pl.ds(0, a_rows)])]
    plan_w = []
    for p in range(chips):
        plan = []
        for c in range(CORES):
            d = p * CORES + c
            plan += [(gw_ref.at[d, pl.ds(0, qw)], w.at[p, pl.ds(c * qw, qw)]),
                     (gw_ref.at[d, pl.ds(qw, hd)], w.at[p, pl.ds(kw + c * hd, hd)]),
                     (gw_ref.at[d, pl.ds(qw + hd, hd)], w.at[p, pl.ds(vw + c * hd, hd)])]
            for a in range(n_ad):
                o = a * (qw + 2 * hd)
                plan += [(gb_ref.at[d, pl.ds(o, qw)], bw.at[p, a, pl.ds(c * qw, qw)]),
                         (gb_ref.at[d, pl.ds(o + qw, hd)], bw.at[p, a, pl.ds(kw + c * hd, hd)]),
                         (gb_ref.at[d, pl.ds(o + qw + hd, hd)], bw.at[p, a, pl.ds(vw + c * hd, hd)])]
        plan_w.append(plan)
    plan_o = []
    off = n_ad * (qw + 2 * hd)
    for d in range(n_dev):
        plan_o.append((gwo_ref.at[d], h.at[pl.ds(d * qw, qw)]))
        for a in range(n_ad):
            plan_o.append((gb_ref.at[d, pl.ds(off + a * qw, qw)], low.at[pl.ds((a * n_dev + d) * qw, qw), pl.ds(0, rank)]))
            plan_o.append((gb_ref.at[d, pl.ds(off + n_ad * qw + a * rank, rank)],
                           h.at[pl.ds(n_dev * qw + a * rank, rank), pl.ds(d * qw, qw)]))

    def start(plan, sem):
        for s, d in plan:
            pltpu.make_async_copy(s, d, sem).start()

    def finish(plan, sem):
        for s, d in plan:
            pltpu.make_async_copy(s, d, sem).wait()

    def x_copies(i, buf, base, slot):
        return [pltpu.make_async_copy(x_ref.at[t, core * steps + i],
                                      buf.at[pl.ds(pl.multiple_of(base + slot * M + t * S, S), S)], xsem.at[slot])
                for t in range(chips)]

    start(plan_a, wsem.at[chips])
    for c in x_copies(0, attn, x_base, 0):
        c.start()
    for p in range(chips):
        start(plan_w[p], wsem.at[p])

    rb = 16

    @pl.loop(0, steps)
    def _(i):
        slot = i % 2
        for c in x_copies(i, attn, x_base, slot):
            c.wait()

        @pl.when(i + 1 < steps)
        def _():
            for c in x_copies(i + 1, attn, x_base, 1 - slot):
                c.start()

        @pl.loop(0, M // rb)
        def _(r):
            v = attn[pl.ds(pl.multiple_of(x_base + slot * M + r * rb, rb), rb), :].astype(F32)
            inv = lax.rsqrt(jnp.mean(v * v, axis=-1, keepdims=True) + EPSILON)
            h[pl.ds(pl.multiple_of(i * M + r * rb, rb), rb), :] = (v * inv * gain_ref[...]).astype(BF16)

        @pl.when(i == 0)
        def _():
            finish(plan_a, wsem.at[chips])
        for t in range(chips):
            rows = pl.ds(pl.multiple_of(i * M + t * S, S), S)
            a = attn[pl.ds(pl.multiple_of(seq_id(i, t) * 3 * rank, 3 * rank), 3 * rank), :]
            low[rows, :] = dot_nt(h[rows, :], a).astype(BF16)

    def produce(it, slot):
        p, i = it // steps, it % steps
        z = dot_nt(w[p], h[tile(i), :])
        for t in range(chips):
            rows = pl.ds(pl.multiple_of(i * M + t * S, S), S)
            b = bw[p, seq_id(i, t)]
            lo = low[rows, :]
            cols = slice(t * S, (t + 1) * S)
            zq = z[:kw, cols] + scale * dot_nt(b[:kw], lo[:, :rank])
            zk = z[kw:vw, cols] + scale * dot_nt(b[kw:vw], lo[:, rank:2 * rank])
            zv = z[vw:, cols] + scale * dot_nt(b[vw:], lo[:, 2 * rank:])
            cos, sin = cos_ref[...], sin_ref[...]

            def rotate(v):
                f, s = v[:half], v[half:]
                return jnp.concatenate([f * cos - s * sin, s * cos + f * sin], axis=0)

            for hh in range(CORES * nq):
                o = hh * hd
                q_scr[slot, o:o + hd, cols] = (rotate(zq[o:o + hd]) * hd ** -0.5).astype(BF16)
            kt = jnp.concatenate([rotate(zk[c * hd:(c + 1) * hd]) for c in range(CORES)], axis=0)
            kk = kt.T.astype(BF16)
            for c in range(CORES):
                k_scr[slot, c, t * S:(t + 1) * S, :] = kk[:, c * hd:(c + 1) * hd]
            v_scr[slot, :, cols] = zv.astype(BF16)

    def consume(it, slot):
        p, i = it // steps, it % steps
        key = lax.broadcasted_iota(jnp.int32, (S, S), 0)
        qry = lax.broadcasted_iota(jnp.int32, (S, S), 1)
        causal = key <= qry
        for c in range(CORES):
            for t in range(chips):
                cols = slice(t * S, (t + 1) * S)
                q = jnp.concatenate([q_scr[slot, c * qw + hh * hd:c * qw + (hh + 1) * hd, cols] for hh in range(nq)], axis=1)
                sc = dot_nn(k_scr[slot, c, cols, :], q)
                ps = []
                for hh in range(nq):
                    sh = jnp.where(causal, sc[:, hh * S:(hh + 1) * S], -1e30)
                    e = jnp.exp(sh - jnp.max(sh, axis=0, keepdims=True))
                    ps.append((e * (1.0 / jnp.sum(e, axis=0, keepdims=True))).astype(BF16))
                o = dot_nn(v_scr[slot, c * hd:(c + 1) * hd, cols], jnp.concatenate(ps, axis=1))
                o = jnp.concatenate([o[:, hh * S:(hh + 1) * S] for hh in range(nq)], axis=0)
                attn[pl.ds(pl.multiple_of(i * M + t * S, S), S),
                     pl.ds(pl.multiple_of((p * CORES + c) * qw, qw), qw)] = o.T.astype(BF16)

    finish(plan_w[0], wsem.at[0])
    produce(0, 0)

    @pl.loop(0, chips * steps)
    def _(it):
        nxt = jnp.minimum(it + 1, chips * steps - 1)
        for p in range(1, chips):
            @pl.when(it == p * steps - 1)
            def _():
                finish(plan_w[p], wsem.at[p])
        consume(it, it % 2)
        produce(nxt, (it + 1) % 2)

    start(plan_o, wsem.at[chips])
    o_base = n_dev * qw + n_ad * rank
    o_slots = 3

    def o_copies(i, slot):
        return [pltpu.make_async_copy(h.at[pl.ds(pl.multiple_of(o_base + slot * M + t * S, S), S)],
                                      out_ref.at[t, i], osem.at[slot]) for t in range(chips)]

    for c in x_copies(0, h, o_base, 0):
        c.start()
    finish(plan_o, wsem.at[chips])
    nt = 256

    @pl.loop(0, steps)
    def _(i):
        slot = i % o_slots
        nslot = (i + 1) % o_slots
        for c in x_copies(i, h, o_base, slot):
            c.wait()

        @pl.when(i + 1 < steps)
        def _():
            @pl.when(i + 1 >= o_slots)
            def _():
                for c in o_copies(i + 1 - o_slots, nslot):
                    c.wait()
            for c in x_copies(i + 1, h, o_base, nslot):
                c.start()

        for t in range(chips):
            rows = pl.ds(pl.multiple_of(i * M + t * S, S), S)
            a = low[pl.ds(pl.multiple_of(seq_id(i, t) * n_dev * qw, qw), n_dev * qw), :rank]
            lowo[pl.ds(t * S, S), :] = dot_nn(attn[rows, :], a).astype(BF16)

        @pl.loop(0, D // nt)
        def _(j):
            cols = pl.ds(pl.multiple_of(j * nt, nt), nt)
            zo = dot_nn(attn[tile(i), :], h[pl.ds(0, n_dev * qw), cols])
            for t in range(chips):
                b = h[pl.ds(pl.multiple_of(n_dev * qw + seq_id(i, t) * rank, rank), rank), cols]
                z = zo[t * S:(t + 1) * S] + scale * dot_nn(lowo[pl.ds(t * S, S), :], b)
                rows = pl.ds(pl.multiple_of(o_base + slot * M + t * S, S), S)
                h[rows, cols] = (h[rows, cols].astype(F32) + z).astype(BF16)
        for c in o_copies(i, slot):
            c.start()

    for i in range(max(0, steps - o_slots), steps):
        for c in o_copies(i, i % o_slots):
            c.wait()


def mlp_body(dims, meta, x_ref, gain_ref, agu_ref, wg0, wg1, wu0, wu1, wd0, wd1, bg0, bg1, bu0, bu1, ad0, ad1,
             out_ref, wg, wu, wd, bg, bu, agu, ad, h_scr, low_scr, hid_scr, sems):
    seqs, S, rank, D, spc, base_step, chips = dims
    scale = ALPHA / rank
    step = pl.program_id(0)
    core = meta[meta.shape[0] - 1]
    fw = wg0.shape[1]
    plans = [[(agu_ref, agu)], [], []]
    for i, (g, u, b1, b2) in enumerate(((wg0, wu0, bg0, bu0), (wg1, wu1, bg1, bu1))):
        c = pl.ds(i * fw, fw)
        plans[1] += [(g, wg.at[:, c]), (u, wu.at[:, c]), (b1, bg.at[:, :, c]), (b2, bu.at[:, :, c])]
    for i, (d, a) in enumerate(((wd0, ad0), (wd1, ad1))):
        c = pl.ds(i * fw, fw)
        plans[2] += [(a, ad.at[:, c]), (d, wd.at[c])]

    @pl.when(step == 0)
    def _():
        for i, plan in enumerate(plans):
            for src, dst in plan:
                pltpu.make_async_copy(src, dst, sems.at[i]).start()

    def arrive(i):
        @pl.when(step == 0)
        def _():
            for src, dst in plans[i]:
                pltpu.make_async_copy(src, dst, sems.at[i]).wait()

    per = seqs // chips
    ids = [meta[t * per + core * (per // CORES) + base_step + step] for t in range(chips)]
    M = chips * S

    def load_x(i, n):
        t = i // (S // n)
        r = i % (S // n)
        return x_ref[t, 0, pl.ds(pl.multiple_of(r * n, n), n), :]

    norm_tile(load_x, gain_ref, h_scr, M)
    arrive(0)
    for t in range(chips):
        low_scr[pl.ds(t * S, S), :] = dot_nn(h_scr[pl.ds(t * S, S), :], agu[ids[t]]).astype(BF16)
    arrive(1)
    nt = 256

    @pl.loop(0, wg.shape[1] // nt)
    def _(j):
        cols = pl.ds(pl.multiple_of(j * nt, nt), nt)
        zg = dot_nn(h_scr[...], wg[:, cols])
        zu = dot_nn(h_scr[...], wu[:, cols])
        for t in range(chips):
            rows = pl.ds(t * S, S)
            g = zg[t * S:(t + 1) * S] + scale * dot_nn(low_scr[rows, :rank], bg[ids[t], :, cols])
            u = zu[t * S:(t + 1) * S] + scale * dot_nn(low_scr[rows, rank:], bu[ids[t], :, cols])
            hid_scr[rows, cols] = (jax.nn.silu(g) * u).astype(BF16)

    arrive(2)
    for t in range(chips):
        out_ref[t, :, D:] = dot_nn(hid_scr[pl.ds(t * S, S), :], ad[ids[t]]).astype(BF16)

    @pl.loop(0, D // nt)
    def _(j):
        cols = pl.ds(pl.multiple_of(j * nt, nt), nt)
        z = dot_nn(hid_scr[...], wd[:, cols])
        for t in range(chips):
            out_ref[t, :, cols] = z[t * S:(t + 1) * S].astype(BF16)


def finish_body(dims, meta, x_ref, rs_ref, bd_ref, out_ref):
    rank, D = dims
    scale = ALPHA / rank
    nt = 256
    low = rs_ref[0, :, D:]

    @pl.loop(0, D // nt)
    def _(j):
        cols = pl.ds(pl.multiple_of(j * nt, nt), nt)
        delta = scale * dot_nn(low, bd_ref[0, :, cols])
        out_ref[0, :, cols] = (x_ref[0, 0, :, cols].astype(F32) + rs_ref[0, :, cols].astype(F32) + delta).astype(BF16)


def solution(mesh):
    n_dev = mesh.shape['tensor']
    chips = n_dev // CORES
    head_split = P(None, 'tensor', None)
    last_split = P(None, None, 'tensor')
    b_head_split = P(None, None, 'tensor', None)
    in_specs = (P('data', None, None), P('data'), P(None), P(None),
                head_split, head_split, head_split, P('tensor', None, None),
                P(None, 'tensor'), P(None, 'tensor'), P('tensor', None),
                last_split, b_head_split, last_split, b_head_split, last_split, b_head_split,
                P(None, 'tensor', None, None), last_split,
                last_split, last_split, last_split, last_split,
                P(None, 'tensor', None), last_split)
    same_core = [[c + CORES * i for i in range(chips)] for c in range(CORES)]
    swap = [(i, i ^ 1) for i in range(n_dev)]
    ANY = pl.BlockSpec(memory_space=pl.ANY)

    def local_layer(x_in, adapter_ids, gain_attn, gain_mlp, w_q, w_k, w_v, w_o, w_gate, w_up, w_down, a_q, b_q, a_k, b_k, a_v, b_v, a_o, b_o, a_gate, b_gate, a_up, b_up, a_down, b_down):
        seqs, S, D = x_in.shape
        nq, hd = w_q.shape[1], w_q.shape[2]
        n_ad, rank = b_q.shape[0], b_q.shape[1]
        rl = a_q.shape[2]
        half = hd // 2
        qw = nq * hd
        me = lax.axis_index('tensor')
        core, chip = me % CORES, me // CORES
        meta = jnp.concatenate([adapter_ids.astype(jnp.int32), core.reshape(1).astype(jnp.int32)])
        per = seqs // chips
        steps = per // CORES
        spc = steps // CHUNKS

        def rows_t(w):
            return jnp.transpose(w, (1, 2, 0)).reshape(-1, w.shape[0])

        gather = functools.partial(lax.all_gather, axis_name='tensor', axis=0)
        swapped = functools.partial(lax.ppermute, axis_name='tensor', perm=swap)

        g_a = gather(jnp.concatenate([jnp.transpose(a, (0, 2, 1)).reshape(n_ad * rl, D)
                                      for a in (a_q, a_k, a_v, a_gate, a_up)], axis=0))
        g_a = g_a.reshape(n_dev, 5, n_ad, rl, D)
        a_qkv = g_a[:, :3].transpose(2, 1, 0, 3, 4).reshape(n_ad * 3 * rank, D)
        a_gu = g_a[:, 3:].transpose(2, 4, 1, 0, 3).reshape(n_ad, D, 2 * rank)
        g_w = gather(jnp.concatenate([rows_t(w_q), rows_t(w_k), rows_t(w_v)], axis=0))

        def b_rows(b):
            return jnp.transpose(b, (1, 2, 0)).reshape(-1, rank)

        b_parts = []
        for a in range(n_ad):
            b_parts += [b_rows(b_q[a]), b_rows(b_k[a]), b_rows(b_v[a])]
        b_parts += [a_o.reshape(n_ad * qw, rank), b_o.reshape(n_ad * rank, qw)]
        g_b = gather(jnp.concatenate(b_parts, axis=0))
        g_wo = gather(w_o.reshape(qw, D))
        g_bd = gather(b_down.reshape(n_ad * rank, qw))
        bd_full = g_bd.reshape(n_dev, n_ad, rank, qw).transpose(1, 2, 0, 3).reshape(n_ad, rank, D)
        mlp_own = (w_gate, w_up, w_down, b_gate, b_up, a_down)
        mlp_other = tuple(swapped(w) for w in mlp_own)

        inv_freq = ROPE_BASE ** (-2.0 * jnp.arange(half, dtype=F32) / hd)
        ang = jnp.arange(S, dtype=F32)[:, None] * inv_freq[None, :]
        cos, sin = jnp.cos(ang), jnp.sin(ang)
        cos_t, sin_t = cos.T, sin.T

        x4 = x_in.reshape(chips, per, S, D)
        M = chips * S
        Fc = CORES * w_gate.shape[1]
        full = lambda shape: pl.BlockSpec(shape, lambda i, m: (0,) * len(shape))
        params = pltpu.CompilerParams(vmem_limit_bytes=VMEM_LIMIT, dimension_semantics=("arbitrary",))
        y = jnp.zeros((n_dev, steps * S, D), BF16)
        x1_all = pl.pallas_call(
            functools.partial(attn_body, (n_dev, seqs, S, hd, nq, rank, D, chips)),
            in_specs=[pl.BlockSpec(memory_space=pltpu.SMEM), ANY] + [pl.BlockSpec(memory_space=pltpu.VMEM)] * 3 + [ANY] * 4,
            out_specs=ANY,
            scratch_shapes=[
                pltpu.VMEM((steps * M, D), BF16), pltpu.VMEM((steps * M, 3 * rank), BF16), pltpu.VMEM((steps * M, n_dev * qw), BF16),
                pltpu.VMEM((chips, CORES * (qw + 2 * hd), D), BF16), pltpu.VMEM((chips, n_ad, CORES * (qw + 2 * hd), rank), BF16),
                pltpu.VMEM((2, CORES * qw, M), BF16), pltpu.VMEM((2, CORES, M, hd), BF16), pltpu.VMEM((2, CORES * hd, M), BF16),
                pltpu.VMEM((M, rank), BF16),
                pltpu.SemaphoreType.DMA((chips + 1,)), pltpu.SemaphoreType.DMA((3,)), pltpu.SemaphoreType.DMA((3,))],
            out_shape=jax.ShapeDtypeStruct((chips, steps, S, D), BF16),
            compiler_params=pltpu.CompilerParams(vmem_limit_bytes=VMEM_LIMIT), name="attn_block",
            cost_estimate=pl.CostEstimate(flops=3 * steps * M * D * (2 * n_dev * qw + 2 * n_dev * hd + 4 * rank),
                                          bytes_accessed=6 * steps * M * D + 33 * 2**20, transcendentals=0),
        )(adapter_ids, x4, gain_attn.reshape(1, D), cos_t, sin_t, g_w, a_qkv, g_b, g_wo)
        for c in range(CHUNKS):
            base_step = c * spc
            tok = M * spc
            pairs = [w for own, other in zip(mlp_own, mlp_other) for w in (own, other)]
            part = pl.pallas_call(
                functools.partial(mlp_body, (seqs, S, rank, D, spc, base_step, chips)),
                grid_spec=pltpu.PrefetchScalarGridSpec(
                    num_scalar_prefetch=1, grid=(spc,),
                    in_specs=[pl.BlockSpec((chips, 1, S, D), lambda i, m, b=base_step: (0, b + i, 0, 0)), full((1, D))] + [ANY] * 13,
                    out_specs=pl.BlockSpec((chips, S, D + rank), lambda i, m: (0, i, 0)),
                    scratch_shapes=[
                        pltpu.VMEM((D, Fc), BF16), pltpu.VMEM((D, Fc), BF16), pltpu.VMEM((Fc, D), BF16),
                        pltpu.VMEM((n_ad, rank, Fc), BF16), pltpu.VMEM((n_ad, rank, Fc), BF16),
                        pltpu.VMEM((n_ad, D, 2 * rank), BF16), pltpu.VMEM((n_ad, Fc, rank), BF16),
                        pltpu.VMEM((M, D), BF16), pltpu.VMEM((M, 2 * rank), BF16), pltpu.VMEM((M, Fc), BF16),
                        pltpu.SemaphoreType.DMA((3,))]),
                out_shape=jax.ShapeDtypeStruct((chips, spc * S, D + rank), BF16),
                compiler_params=params, name="mlp_block",
                cost_estimate=pl.CostEstimate(flops=2 * tok * D * (3 * Fc + 4 * rank),
                                              bytes_accessed=4 * tok * D + 34 * 2**20, transcendentals=tok * Fc),
            )(meta, x1_all, gain_mlp.reshape(1, D), a_gu, *pairs)
            rs = lax.psum_scatter(part, 'tensor', scatter_dimension=0, axis_index_groups=same_core, tiled=True)
            own = [adapter_ids[chip * per + core * steps + base_step + i] for i in range(spc)]
            meta2 = jnp.concatenate([jnp.stack(own).astype(jnp.int32), chip.reshape(1).astype(jnp.int32)])
            y_own = pl.pallas_call(
                functools.partial(finish_body, (rank, D)),
                grid_spec=pltpu.PrefetchScalarGridSpec(
                    num_scalar_prefetch=1, grid=(spc,),
                    in_specs=[pl.BlockSpec((1, 1, S, D), lambda i, m, b=base_step: (m[spc], b + i, 0, 0)),
                              pl.BlockSpec((1, S, D + rank), lambda i, m: (i, 0, 0)),
                              pl.BlockSpec((1, rank, D), lambda i, m: (m[i], 0, 0))],
                    out_specs=pl.BlockSpec((1, S, D), lambda i, m: (i, 0, 0))),
                out_shape=jax.ShapeDtypeStruct((spc, S, D), BF16),
                compiler_params=pltpu.CompilerParams(dimension_semantics=("arbitrary",)), name="finish",
                cost_estimate=pl.CostEstimate(flops=2 * spc * S * rank * D, bytes_accessed=10 * spc * S * D, transcendentals=0),
            )(meta2, x1_all, rs.reshape(spc, S, D + rank), bd_full)
            y_all = gather(y_own.reshape(spc * S, D))
            y = lax.dynamic_update_slice(y, y_all, (0, base_step * S, 0))
        return y.reshape(seqs, S, D)

    return jax.shard_map(local_layer, mesh=mesh, in_specs=in_specs, out_specs=P('data', None, None), check_vma=False)
```

time: 1070 us -> 1010 us (0.944)
  Pallas kernels: 603 us -> 552 us
  waiting for transfers between devices: 344 us -> 356 us
  local copies, waits for them, and re-layouts: 82.5 us -> 70.7 us
    pallas_call x4 -> x1, Pallas kernels: 365 us -> 313 us  [local_layer(): pl.pallas_call(functools.partial(attn_body, (n_dev, seqs, S, hd, nq, rank...]
  transfers between devices with their start and end apart: 19 -> 19, of which waited for: 9 -> 9; matrix products, arithmetic and copies ran while one was open for 7% -> 6% of each run, Pallas kernels for 57% -> 55%
where the time goes in v2:
time: 1010 us
  Pallas kernels  552 us (55%)
  waiting for transfers between devices  356 us (35%)
  local copies, waits for them, and re-layouts  70.7 us (7%)
  between operations  13.7 us (1%)
  other arithmetic  10.3 us (1%)
    pallas_call x1, Pallas kernels, local_layer(): pl.pallas_call(functools.partial(attn_body, (n_dev, seqs, S, hd, nq, rank...  313 us
    pallas_call x4, Pallas kernels, local_layer(): pl.pallas_call(functools.partial(mlp_body, (seqs, S, rank, D, spc, base_s...  215 us
    all_gather x4, waiting for transfers between devices, local_layer(): y_all = gather(y_own.reshape(spc * S, D))  153 us
    all_gather x1, waiting for transfers between devices, local_layer(): gather(jnp.concatenate([rows_t(w_q), rows_t(w_k), rows_t(w_v)], axis=0))  64.9 us
    all_gather x1, waiting for transfers between devices, local_layer(): gather(jnp.concatenate([jnp.transpose(a, (0, 2, 1)).reshape(n_ad * rl, D)...  49.9 us
    all_gather x1, waiting for transfers between devices, local_layer(): g_wo = gather(w_o.reshape(qw, D))  47.3 us
    dynamic_update_slice x4, local copies, waits for them, and re-layouts, local_layer(): y = lax.dynamic_update_slice(y, y_all, (0, base_step * S, 0))  38.8 us
    all_gather x1, waiting for transfers between devices, local_layer(): g_b = gather(jnp.concatenate(b_parts, axis=0))  25 us
  transfers between devices with their start and end apart: 19, of which 9 were waited for; matrix products, arithmetic and copies ran while one was open for 6% of the time, Pallas kernels for 55%

profile of v2, /device:TPU:113, one launch (start us, length us, event | category | flops | bytes accessed | tf_op | source)
XLA Modules:
  0.0 1005.5 jit_solution(1763698513576208516)
XLA Ops:
  6.7 1.1 constant_dynamic-update-slice_fusion.4
  7.8 1.0 constant_dynamic-update-slice_fusion.3
  8.7 1.0 constant_dynamic-update-slice_fusion.2
  9.7 1.0 constant_dynamic-update-slice_fusion.1
  10.7 1.0 constant_dynamic-update-slice_fusion
  11.7 1.0 copy-done
  12.8 1.0 fusion.2
  14.0 0.9 copy-done.1
  15.1 0.7 all-gather.13.cloned.1.call-update
  15.9 1.3 pad_maximum_fusion
  17.3 0.8 collective-permute-start.3
  19.3 0.7 fusion
  20.0 0.6 pad_add_fusion.meta
  20.7 49.9 %all-gather.27.cloned.1.call-done = bf16[2560,2048]{1,0:T(8,128)(2,1)} async-done(((bf16[320,2048]{1,0:T(8,128)(2,1)}), bf16[2560,2048]{1,0:T(8,128)(2,1)}) %all-gather.27.cloned.1.call-update) | async-done | bytes 10485776 | tf_op jit(solution)/shard_map/all_gather | solution.py:357
  70.6 3.4 slice_bitcast_fusion
  74.0 3.2 copy.35
  77.1 2.5 slice_bitcast_fusion.1
  79.6 2.3 copy.36
  82.0 6.2 copy.37.agu_ref
  88.4 25.0 %all-gather.29.cloned.1.call-done = bf16[14336,256]{1,0:T(8,128)(2,1)} async-done(((bf16[1792,256]{1,0:T(8,128)(2,1)}), bf16[14336,256]{1,0:T(8,128)(2,1)}) %all-gather.29.cloned.1.call-update) | async-done | bytes 7340048 | tf_op jit(solution)/shard_map/all_gather | solution.py:371
  113.5 47.3 %all-gather.13.cloned.1.call-done.gwo_ref = bf16[8,256,2048]{2,1,0:T(8,128)(2,1)} async-done(((bf16[1,256,2048]{2,1,0:T(8,128)(2,1)}), bf16[8,256,2048]{2,1,0:T(8,128)(2,1)}) %all-gather.13.cloned.1.call-update) | async-done | bytes 8388624 | tf_op jit(solution)/shard_map/all_gather | solution.py:372
  160.7 64.9 %all-gather.25.cloned.1.call-done = bf16[3072,2048]{1,0:T(8,128)(2,1)} async-done(((bf16[384,2048]{1,0:T(8,128)(2,1)}), bf16[3072,2048]{1,0:T(8,128)(2,1)}) %all-gather.25.cloned.1.call-update) | async-done | bytes 12582928 | tf_op jit(solution)/shard_map/all_gather | solution.py:362
  225.7 313.3 %attn_block.1.x_ref = bf16[4,8,128,2048]{3,2,1,0:T(8,128)(2,1)} custom-call(s32[64]{0:T(128)} %ids_ref.1, bf16[4,16,128,2048]{3,2,1,0:T(8,128)(2,1)} %bitcast.119, f32[1,2048]{1,0:T(1,128)} %bitcast.122, f32[32,128]{1,0:T(8,128)} %get-tuple-element.16.cos_ref, f32[32,128]{1,0:T(8,128)} %get-tuple-element.15.sin_ref, bf16[8,384,2048]{2,1,0:T(8,128)(2,1)} %bitcast.120, ...), custom_call_target="tpu_custom_call" | custom-call | flops 154618822656 | bytes 84934656 | tf_op jit(solution)/shard_map/attn_block/pallas_call | solution.py:389
  539.0 53.8 %mlp_block.4 = bf16[4,256,2304]{2,1,0:T(8,128)(2,1)} custom-call(s32[65]{0:T(128)} %pad_add_fusion.meta, bf16[4,8,128,2048]{3,2,1,0:T(8,128)(2,1)} %attn_block.1.x_ref, f32[1,2048]{1,0:T(1,128)} %bitcast.123, bf16[2,2048,512]{2,1,0:T(8,128)(2,1)} %copy.37.agu_ref, bf16[2048,1024]{1,0:T(8,128)(2,1)} %wg0.7, bf16[2048,1024]{1,0:T(8,128)(2,1)} %collective-permute-done.wg1, ...), custom_call_target="tpu_custom_call" | custom-call | flops 30064771072 | bytes 44040192 | tf_op jit(solution)/shard_map/mlp_block/pallas_call | solution.py:408
  593.0 53.7 %mlp_block.5 = bf16[4,256,2304]{2,1,0:T(8,128)(2,1)} custom-call(s32[65]{0:T(128)} %pad_add_fusion.meta, bf16[4,8,128,2048]{3,2,1,0:T(8,128)(2,1)} %attn_block.1.x_ref, f32[1,2048]{1,0:T(1,128)} %bitcast.124, bf16[2,2048,512]{2,1,0:T(8,128)(2,1)} %copy.37.agu_ref, bf16[2048,1024]{1,0:T(8,128)(2,1)} %wg0.7, bf16[2048,1024]{1,0:T(8,128)(2,1)} %collective-permute-done.wg1, ...), custom_call_target="tpu_custom_call" | custom-call | flops 30064771072 | bytes 44040192 | tf_op jit(solution)/shard_map/mlp_block/pallas_call | solution.py:408
  646.8 53.7 %mlp_block.6 = bf16[4,256,2304]{2,1,0:T(8,128)(2,1)} custom-call(s32[65]{0:T(128)} %pad_add_fusion.meta, bf16[4,8,128,2048]{3,2,1,0:T(8,128)(2,1)} %attn_block.1.x_ref, f32[1,2048]{1,0:T(1,128)} %bitcast.125, bf16[2,2048,512]{2,1,0:T(8,128)(2,1)} %copy.37.agu_ref, bf16[2048,1024]{1,0:T(8,128)(2,1)} %wg0.7, bf16[2048,1024]{1,0:T(8,128)(2,1)} %collective-permute-done.wg1, ...), custom_call_target="tpu_custom_call" | custom-call | flops 30064771072 | bytes 44040192 | tf_op jit(solution)/shard_map/mlp_block/pallas_call | solution.py:408
  700.7 53.9 %mlp_block.7 = bf16[4,256,2304]{2,1,0:T(8,128)(2,1)} custom-call(s32[65]{0:T(128)} %pad_add_fusion.meta, bf16[4,8,128,2048]{3,2,1,0:T(8,128)(2,1)} %attn_block.1.x_ref, f32[1,2048]{1,0:T(1,128)} %bitcast.126, bf16[2,2048,512]{2,1,0:T(8,128)(2,1)} %copy.37.agu_ref, bf16[2048,1024]{1,0:T(8,128)(2,1)} %wg0.7, bf16[2048,1024]{1,0:T(8,128)(2,1)} %collective-permute-done.wg1, ...), custom_call_target="tpu_custom_call" | custom-call | flops 30064771072 | bytes 44040192 | tf_op jit(solution)/shard_map/mlp_block/pallas_call | solution.py:408
  754.8 0.5 copy-done.10
  755.3 0.7 fusion.3
  756.0 1.9 add_add_fusion.meta
  757.8 2.8 copy.43
  760.6 2.4 reshape.130.bd_ref
  763.0 5.9 finish.4
  769.1 1.9 add_add_fusion.1.meta
  771.0 5.9 finish.5
  777.1 1.9 add_add_fusion.2.meta
  779.0 5.9 finish.6
  785.0 1.9 add_add_fusion.3.meta
  786.9 14.6 %reduce-scatter.11.cloned.1.call-done = bf16[1,256,2304]{2,1,0:T(8,128)(2,1)} async-done(((bf16[4,256,2304]{2,1,0:T(8,128)(2,1)}), bf16[1,256,2304]{2,1,0:T(8,128)(2,1)}) %reduce-scatter.11.cloned.1.call-update) | async-done | bytes 1179664 | tf_op jit(solution)/shard_map/reduce_scatter | solution.py:425
  801.5 5.9 finish.7
  807.5 41.3 %all-gather.17.cloned.1.call-done = bf16[8,256,2048]{2,1,0:T(8,128)(2,1)} async-done(((bf16[1,256,2048]{2,1,0:T(8,128)(2,1)}), bf16[8,256,2048]{2,1,0:T(8,128)(2,1)}) %all-gather.17.cloned.1.call-update) | async-done | bytes 8388624 | tf_op jit(solution)/shard_map/all_gather | solution.py:440
  848.8 13.5 %dynamic_update_slice.12 = bf16[8,1024,2048]{2,1,0:T(8,128)(2,1)} pad(bf16[8,256,2048]{2,1,0:T(8,128)(2,1)} %all-gather.17.cloned.1.call-done, bf16[]{:T(256)} %constant.60.clone.1), padding=0_0x0_768x0_0 | pad | bytes 41943040 | tf_op jit(solution)/shard_map/dynamic_update_slice | solution.py:441
  862.3 33.8 %all-gather.19.cloned.1.call-done = bf16[8,256,2048]{2,1,0:T(8,128)(2,1)} async-done(((bf16[1,256,2048]{2,1,0:T(8,128)(2,1)}), bf16[8,256,2048]{2,1,0:T(8,128)(2,1)}) %all-gather.19.cloned.1.call-update) | async-done | bytes 8388624 | tf_op jit(solution)/shard_map/all_gather | solution.py:440
  896.1 8.4 constant_dynamic-update-slice_fusion.11
  904.5 38.7 %all-gather.21.cloned.1.call-done = bf16[8,256,2048]{2,1,0:T(8,128)(2,1)} async-done(((bf16[1,256,2048]{2,1,0:T(8,128)(2,1)}), bf16[8,256,2048]{2,1,0:T(8,128)(2,1)}) %all-gather.21.cloned.1.call-update) | async-done | bytes 8388624 | tf_op jit(solution)/shard_map/all_gather | solution.py:440
  943.2 8.4 constant_dynamic-update-slice_fusion.10
  951.7 38.8 %all-gather.23.cloned.1.call-done = bf16[8,256,2048]{2,1,0:T(8,128)(2,1)} async-done(((bf16[1,256,2048]{2,1,0:T(8,128)(2,1)}), bf16[8,256,2048]{2,1,0:T(8,128)(2,1)}) %all-gather.23.cloned.1.call-update) | async-done | bytes 8388624 | tf_op jit(solution)/shard_map/all_gather | solution.py:440
  990.5 8.4 constant_dynamic-update-slice_fusion.9
  (68 shorter events, 2.9 us)
Async XLA Ops:
  6.5 7.3 copy-start.7
  6.5 7.3 copy-start.8
  6.6 7.4 copy-start.5
  6.6 7.4 copy-start.6
  6.6 9.4 copy-start.3
  6.6 9.4 copy-start.4
  6.6 9.4 copy-start.2
  6.6 64.0 %all-gather.27.cloned.1.call-start = ((), (), s32[]{:S(2)}) async-start(), calls=%async_computation.15 | async-start | bytes 11796480 | tf_op jit(solution)/shard_map/all_gather | solution.py:357
  11.7 1.1 copy-start
  12.8 100.7 %all-gather.29.cloned.1.call-start = ((), (), s32[]{:S(2)}) async-start(), calls=%async_computation.16 | async-start | bytes 8257536 | tf_op jit(solution)/shard_map/all_gather | solution.py:371
  13.9 6.1 copy-start.9
  14.0 1.0 copy-start.1
  15.1 145.7 %all-gather.13.cloned.1.call-start = ((), (), s32[]{:S(2)}) async-start(), calls=%async_computation.4 | async-start | bytes 9437184 | tf_op jit(solution)/shard_map/all_gather | solution.py:372
  15.8 209.8 %all-gather.25.cloned.1.call-start = ((), (), s32[]{:S(2)}) async-start(), calls=%async_computation.14 | async-start | bytes 14155776 | tf_op jit(solution)/shard_map/all_gather | solution.py:362
  17.3 740.6 %all-gather.15.cloned.1.call-start = ((), (), s32[]{:S(2)}) async-start(), calls=%async_computation.6 | async-start | bytes 2359296 | tf_op jit(solution)/shard_map/all_gather | solution.py:373
  17.3 70.8 %collective-permute-start.3 = (bf16[2,256,1024]{2,1,0:T(8,128)(2,1)}, bf16[2,256,1024]{2,1,0:T(8,128)(2,1)}, u32[]{:S(2)}, u32[]{:S(2)}) collective-permute-start(bf16[2,256,1024]{2,1,0:T(8,128)(2,1)} %bg0.7), channel_id=1, source_target_pairs={{0,1},{1,0},{2,3},{3,2},{4,5},{5,4},{6,7},{7,6},{8,9},{9,8},{10,11... | collective-permute-start | bytes 3145736 | tf_op jit(solution)/shard_map/ppermute | solution.py:376
  18.1 520.9 %collective-permute-start.4 = (bf16[2,256,1024]{2,1,0:T(8,128)(2,1)}, bf16[2,256,1024]{2,1,0:T(8,128)(2,1)}, u32[]{:S(2)}, u32[]{:S(2)}) collective-permute-start(bf16[2,256,1024]{2,1,0:T(8,128)(2,1)} %bu0.7), channel_id=1, source_target_pairs={{0,1},{1,0},{2,3},{3,2},{4,5},{5,4},{6,7},{7,6},{8,9},{9,8},{10,11... | collective-permute-start | bytes 3145736 | tf_op jit(solution)/shard_map/ppermute | solution.py:376
  18.2 520.8 %collective-permute-start.5 = (bf16[2,1024,256]{2,1,0:T(8,128)(2,1)}, bf16[2,1024,256]{2,1,0:T(8,128)(2,1)}, u32[]{:S(2)}, u32[]{:S(2)}) collective-permute-start(bf16[2,1024,256]{2,1,0:T(8,128)(2,1)} %ad0.7), channel_id=1, source_target_pairs={{0,1},{1,0},{2,3},{3,2},{4,5},{5,4},{6,7},{7,6},{8,9},{9,8},{10,11... | collective-permute-start | bytes 3145736 | tf_op jit(solution)/shard_map/ppermute | solution.py:376
  18.6 520.4 %collective-permute-start = (bf16[2048,1024]{1,0:T(8,128)(2,1)}, bf16[2048,1024]{1,0:T(8,128)(2,1)}, u32[]{:S(2)}, u32[]{:S(2)}) collective-permute-start(bf16[2048,1024]{1,0:T(8,128)(2,1)} %wg0.7), channel_id=1, source_target_pairs={{0,1},{1,0},{2,3},{3,2},{4,5},{5,4},{6,7},{7,6},{8,9},{9,8},{10,11... | collective-permute-start | bytes 12582920 | tf_op jit(solution)/shard_map/ppermute | solution.py:376
  18.7 520.3 %collective-permute-start.1 = (bf16[2048,1024]{1,0:T(8,128)(2,1)}, bf16[2048,1024]{1,0:T(8,128)(2,1)}, u32[]{:S(2)}, u32[]{:S(2)}) collective-permute-start(bf16[2048,1024]{1,0:T(8,128)(2,1)} %wu0.7), channel_id=1, source_target_pairs={{0,1},{1,0},{2,3},{3,2},{4,5},{5,4},{6,7},{7,6},{8,9},{9,8},{10,11... | collective-permute-start | bytes 12582920 | tf_op jit(solution)/shard_map/ppermute | solution.py:376
  19.2 743.8 %reduce-scatter.5.cloned.1.call-start = ((), (), s32[]{:S(2)}) async-start(), calls=%async_computation.5 | async-start | bytes 5898240 | tf_op jit(solution)/shard_map/reduce_scatter | solution.py:425
  88.2 450.9 %collective-permute-start.2 = (bf16[1024,2048]{1,0:T(8,128)(2,1)}, bf16[1024,2048]{1,0:T(8,128)(2,1)}, u32[]{:S(2)}, u32[]{:S(2)}) collective-permute-start(bf16[1024,2048]{1,0:T(8,128)(2,1)} %wd0.7), channel_id=1, source_target_pairs={{0,1},{1,0},{2,3},{3,2},{4,5},{5,4},{6,7},{7,6},{8,9},{9,8},{10,11... | collective-permute-start | bytes 12582920 | tf_op jit(solution)/shard_map/ppermute | solution.py:376
  592.9 178.1 %reduce-scatter.7.cloned.1.call-start = ((), (), s32[]{:S(2)}) async-start(), calls=%async_computation.8 | async-start | bytes 5898240 | tf_op jit(solution)/shard_map/reduce_scatter | solution.py:425
  646.8 132.2 %reduce-scatter.9.cloned.1.call-start = ((), (), s32[]{:S(2)}) async-start(), calls=%async_computation.10 | async-start | bytes 5898240 | tf_op jit(solution)/shard_map/reduce_scatter | solution.py:425
  700.6 100.9 %reduce-scatter.11.cloned.1.call-start = ((), (), s32[]{:S(2)}) async-start(), calls=%async_computation.12 | async-start | bytes 5898240 | tf_op jit(solution)/shard_map/reduce_scatter | solution.py:425
  754.6 0.7 copy-start.10
  754.7 94.1 %all-gather.17.cloned.1.call-start = ((), (), s32[]{:S(2)}) async-start(), calls=%async_computation.7 | async-start | bytes 9437184 | tf_op jit(solution)/shard_map/all_gather | solution.py:440
  769.0 127.1 %all-gather.19.cloned.1.call-start = ((), (), s32[]{:S(2)}) async-start(), calls=%async_computation.9 | async-start | bytes 9437184 | tf_op jit(solution)/shard_map/all_gather | solution.py:440
  777.0 166.2 %all-gather.21.cloned.1.call-start = ((), (), s32[]{:S(2)}) async-start(), calls=%async_computation.11 | async-start | bytes 9437184 | tf_op jit(solution)/shard_map/all_gather | solution.py:440
  785.0 205.6 %all-gather.23.cloned.1.call-start = ((), (), s32[]{:S(2)}) async-start(), calls=%async_computation.13 | async-start | bytes 9437184 | tf_op jit(solution)/shard_map/all_gather | solution.py:440
Sparse Core Ops, SparseCore 0:
  12.9 57.6 all-gather.26
  72.2 41.2 all-gather.28
  115.1 45.5 all-gather.12
  162.2 63.4 all-gather.24
  227.1 21.4 all-gather.14
  593.1 46.7 reduce-scatter.4
  646.9 46.7 reduce-scatter.6
  700.7 46.6 reduce-scatter.8
  754.8 46.6 reduce-scatter.10
  803.0 45.8 all-gather.16
  850.4 45.6 all-gather.18
  897.6 45.6 all-gather.20
  944.8 45.6 all-gather.22

commit v3 on v2

--- a/solution.py
+++ b/solution.py
@@ -11,7 +11,6 @@
 ROPE_BASE = 10000.0
 EPSILON = 1e-5
 CORES = 2
-CHUNKS = 4
 VMEM_LIMIT = 62 * 1024 * 1024
 F32, BF16 = jnp.float32, jnp.bfloat16
 
@@ -22,17 +21,6 @@
 
 def dot_nt(a, b):
     return lax.dot_general(a, b, (((1,), (1,)), ((), ())), preferred_element_type=F32)
-
-
-def norm_tile(load_rows, gain_ref, dst_ref, n_rows):
-    step_rows = 16
-
-    @pl.loop(0, n_rows // step_rows)
-    def _(i):
-        v = load_rows(i, step_rows).astype(F32)
-        inv = lax.rsqrt(jnp.mean(v * v, axis=-1, keepdims=True) + EPSILON)
-        rows = pl.ds(pl.multiple_of(i * step_rows, step_rows), step_rows)
-        dst_ref[rows, :] = (v * inv * gain_ref[...]).astype(BF16)
 
 
 def attn_body(dims, ids_ref, x_ref, gain_ref, cos_ref, sin_ref, gw_ref, aqkv_ref, gb_ref, gwo_ref, out_ref,
@@ -238,83 +226,227 @@
             c.wait()
 
 
-def mlp_body(dims, meta, x_ref, gain_ref, agu_ref, wg0, wg1, wu0, wu1, wd0, wd1, bg0, bg1, bu0, bu1, ad0, ad1,
-             out_ref, wg, wu, wd, bg, bu, agu, ad, h_scr, low_scr, hid_scr, sems):
-    seqs, S, rank, D, spc, base_step, chips = dims
+def mlp_body(dims, ids_ref, x_ref, gain_ref, agu_ref, wg0, wg1, wu0, wu1, wd0, wd1, bg0, bg1, bu0, bu1, ad0, ad1, bd_ref,
+             y_ref, wg, wu, wd, bg, bu, agu, ad, bd, xt, h_scr, low_scr, hid_scr, part, in_a, in_b, xo, ybuf,
+             wsem, xsem, osem, sa, ra, sb, rb_, sy, ry, sf, rf, sp, rp):
+    seqs, S, rank, D, chips = dims
     scale = ALPHA / rank
-    step = pl.program_id(0)
-    core = meta[meta.shape[0] - 1]
     fw = wg0.shape[1]
-    plans = [[(agu_ref, agu)], [], []]
+    per = seqs // chips
+    steps = per // CORES
+    M = chips * S
+    hs = S // 2
+    me = lax.axis_index('tensor')
+    core, chip = me % CORES, me // CORES
+    right_chip, left_chip = (chip + 1) % chips, (chip + chips - 1) % chips
+    far_chip = (chip + 2) % chips
+    right, left, other = right_chip * CORES + core, left_chip * CORES + core, chip * CORES + (1 - core)
+
+    barrier = pltpu.get_barrier_semaphore()
+    for dev in (right, left, other):
+        pl.semaphore_signal(barrier, inc=1, device_id={'tensor': dev}, device_id_type=pl.DeviceIdType.MESH)
+    pl.semaphore_wait(barrier, 3)
+
+    def remote(src, dst, ssem, rsem, dev):
+        return pltpu.make_async_remote_copy(src_ref=src, dst_ref=dst, send_sem=ssem, recv_sem=rsem,
+                                            device_id={'tensor': dev}, device_id_type=pl.DeviceIdType.MESH)
+
+    def copies_a(j):
+        s, r = j % 3, j % 4
+        return [remote(part.at[s, far_chip, pl.ds(0, hs)], in_a.at[0, r], sa.at[0, j], ra.at[0, j], right),
+                remote(part.at[s, far_chip, pl.ds(hs, hs)], in_a.at[1, r], sa.at[1, j], ra.at[1, j], left)]
+
+    def copies_b(j):
+        s, r = j % 3, j % 3
+        return [remote(part.at[s, right_chip], in_b.at[0, r], sb.at[0, j], rb_.at[0, j], right),
+                remote(part.at[s, left_chip], in_b.at[1, r], sb.at[1, j], rb_.at[1, j], left)]
+
+    def copies_y(j):
+        dst = y_ref.at[me, j]
+        src = ybuf.at[j % 2]
+        return [remote(src, dst, sy.at[0, j], ry.at[0, j], right), remote(src, dst, sy.at[1, j], ry.at[1, j], left)]
+
+    def copies_f(j):
+        from_left = y_ref.at[left, j, pl.ds(0, hs)]
+        from_right = y_ref.at[right, j, pl.ds(hs, hs)]
+        return [remote(from_left, from_left, sf.at[0, j], rf.at[0, j], right),
+                remote(from_right, from_right, sf.at[1, j], rf.at[1, j], left)]
+
+    far = far_chip * CORES + core
+
+    def copies_p(j):
+        out = [remote(ybuf.at[j % 2], y_ref.at[me, j], sp.at[0, j], rp.at[0, j], other)]
+        for n, dev in enumerate((left, right, far)):
+            out.append(remote(y_ref.at[dev, j], y_ref.at[dev, j], sp.at[n + 1, j], rp.at[n + 1, j], other))
+        return out
+
+    def store_y(j):
+        return pltpu.make_async_copy(ybuf.at[j % 2], y_ref.at[me, j], osem.at[j % 2])
+
+    plans = [[(agu_ref, agu)], [], [(bd_ref, bd)]]
     for i, (g, u, b1, b2) in enumerate(((wg0, wu0, bg0, bu0), (wg1, wu1, bg1, bu1))):
         c = pl.ds(i * fw, fw)
         plans[1] += [(g, wg.at[:, c]), (u, wu.at[:, c]), (b1, bg.at[:, :, c]), (b2, bu.at[:, :, c])]
     for i, (d, a) in enumerate(((wd0, ad0), (wd1, ad1))):
         c = pl.ds(i * fw, fw)
         plans[2] += [(a, ad.at[:, c]), (d, wd.at[c])]
-
-    @pl.when(step == 0)
-    def _():
-        for i, plan in enumerate(plans):
-            for src, dst in plan:
-                pltpu.make_async_copy(src, dst, sems.at[i]).start()
-
-    def arrive(i):
+    n_plan = [0]
+    flat = []
+    for plan in plans:
+        group = []
+        for src, dst in plan:
+            group.append(pltpu.make_async_copy(src, dst, wsem.at[n_plan[0]]))
+            n_plan[0] += 1
+        flat.append(group)
+
+    def x_copy(i, slot):
+        return pltpu.make_async_copy(x_ref.at[:, i], xt.at[slot], xsem.at[slot])
+
+    def xo_copy(i):
+        return pltpu.make_async_copy(x_ref.at[chip, i], xo.at[i % 2], xsem.at[2 + i % 2])
+
+    x_copy(0, 0).start()
+    for group in flat:
+        for c in group:
+            c.start()
+
+    def arrive(i, step):
         @pl.when(step == 0)
         def _():
-            for src, dst in plans[i]:
-                pltpu.make_async_copy(src, dst, sems.at[i]).wait()
-
-    per = seqs // chips
-    ids = [meta[t * per + core * (per // CORES) + base_step + step] for t in range(chips)]
-    M = chips * S
-
-    def load_x(i, n):
-        t = i // (S // n)
-        r = i % (S // n)
-        return x_ref[t, 0, pl.ds(pl.multiple_of(r * n, n), n), :]
-
-    norm_tile(load_x, gain_ref, h_scr, M)
-    arrive(0)
-    for t in range(chips):
-        low_scr[pl.ds(t * S, S), :] = dot_nn(h_scr[pl.ds(t * S, S), :], agu[ids[t]]).astype(BF16)
-    arrive(1)
+            for c in flat[i]:
+                c.wait()
+
     nt = 256
-
-    @pl.loop(0, wg.shape[1] // nt)
+    rb = 16
+
+    def compute(k):
+        slot = k % 2
+        x_copy(k, slot).wait()
+
+        @pl.when(k + 1 < steps)
+        def _():
+            x_copy(k + 1, 1 - slot).start()
+
+        ids = [ids_ref[t * per + core * steps + k] for t in range(chips)]
+
+        @pl.loop(0, M // rb)
+        def _(i):
+            t, r = i // (S // rb), i % (S // rb)
+            v = xt[slot, t, pl.ds(pl.multiple_of(r * rb, rb), rb), :].astype(F32)
+            inv = lax.rsqrt(jnp.mean(v * v, axis=-1, keepdims=True) + EPSILON)
+            h_scr[pl.ds(pl.multiple_of(i * rb, rb), rb), :] = (v * inv * gain_ref[...]).astype(BF16)
+
+        arrive(0, k)
+        for t in range(chips):
+            low_scr[pl.ds(t * S, S), :] = dot_nn(h_scr[pl.ds(t * S, S), :], agu[ids[t]]).astype(BF16)
+        arrive(1, k)
+
+        @pl.loop(0, wg.shape[1] // nt)
+        def _(j):
+            cols = pl.ds(pl.multiple_of(j * nt, nt), nt)
+            zg = dot_nn(h_scr[...], wg[:, cols])
+            zu = dot_nn(h_scr[...], wu[:, cols])
+            for t in range(chips):
+                rows = pl.ds(t * S, S)
+                g = zg[t * S:(t + 1) * S] + scale * dot_nn(low_scr[rows, :rank], bg[ids[t], :, cols])
+                u = zu[t * S:(t + 1) * S] + scale * dot_nn(low_scr[rows, rank:], bu[ids[t], :, cols])
+                hid_scr[rows, cols] = (jax.nn.silu(g) * u).astype(BF16)
+
+        arrive(2, k)
+
+        @pl.when(k >= 3)
+        def _():
+            for c in copies_a(k - 3) + copies_b(k - 3):
+                c.wait_send()
+        s = k % 3
+        for t in range(chips):
+            part[s, t, :, D:] = dot_nn(hid_scr[pl.ds(t * S, S), :], ad[ids[t]]).astype(BF16)
+
+        @pl.loop(0, D // nt)
+        def _(j):
+            cols = pl.ds(pl.multiple_of(j * nt, nt), nt)
+            z = dot_nn(hid_scr[...], wd[:, cols])
+            for t in range(chips):
+                part[s, t, :, cols] = z[t * S:(t + 1) * S].astype(BF16)
+
+        for c in copies_a(k):
+            c.start()
+
+    def relay(j):
+        s, r = j % 3, j % 4
+        for n, (dest, lo) in enumerate(((right_chip, 0), (left_chip, hs))):
+            copies_a(j)[n].wait_recv()
+
+            @pl.loop(0, hs // rb)
+            def _(i):
+                rows = pl.ds(pl.multiple_of(lo + i * rb, rb), rb)
+                got = in_a[n, r, pl.ds(pl.multiple_of(i * rb, rb), rb), :]
+                part[s, dest, rows, :] = (part[s, dest, rows, :].astype(F32) + got.astype(F32)).astype(BF16)
+            copies_b(j)[n].start()
+        xo_copy(j).start()
+
+    def settle(j):
+        s = j % 3
+        for c in copies_b(j):
+            c.wait_recv()
+        xo_copy(j).wait()
+
+        @pl.when(j >= 2)
+        def _():
+            store_y(j - 2).wait()
+            for c in copies_y(j - 2) + copies_p(j - 2)[:1]:
+                c.wait_send()
+        idx = ids_ref[chip * per + core * steps + j]
+
+        def total(cols):
+            return (part[s, chip, :, cols].astype(F32) + in_b[0, s, :, cols].astype(F32)) + in_b[1, s, :, cols].astype(F32)
+
+        low = total(pl.ds(D, rank)).astype(BF16)
+
+        @pl.loop(0, D // nt)
+        def _(i):
+            cols = pl.ds(pl.multiple_of(i * nt, nt), nt)
+            z = total(cols) + scale * dot_nn(low, bd[idx, :, cols])
+            ybuf[j % 2, :, cols] = (xo[j % 2, :, cols].astype(F32) + z).astype(BF16)
+        store_y(j).start()
+        for c in copies_y(j) + copies_p(j)[:1]:
+            c.start()
+
+    def forward(j):
+        for n in range(2):
+            copies_y(j)[n].wait_recv()
+            copies_f(j)[n].start()
+            copies_p(j)[1 + n].start()
+
+    def last_hop(j):
+        for c in copies_f(j):
+            c.wait_recv()
+        copies_p(j)[3].start()
+
+    @pl.loop(0, steps + 4)
+    def _(k):
+        @pl.when(k < steps)
+        def _():
+            compute(k)
+        for lag, stage in ((1, relay), (2, settle), (3, forward), (4, last_hop)):
+            @pl.when((k >= lag) & (k < steps + lag))
+            def _():
+                stage(k - lag)
+
+    for j in range(max(0, steps - 3), steps):
+        for c in copies_a(j) + copies_b(j):
+            c.wait_send()
+    for j in range(max(0, steps - 2), steps):
+        store_y(j).wait()
+        for c in copies_y(j) + copies_p(j)[:1]:
+            c.wait_send()
+
+    @pl.loop(0, steps)
     def _(j):
-        cols = pl.ds(pl.multiple_of(j * nt, nt), nt)
-        zg = dot_nn(h_scr[...], wg[:, cols])
-        zu = dot_nn(h_scr[...], wu[:, cols])
-        for t in range(chips):
-            rows = pl.ds(t * S, S)
-            g = zg[t * S:(t + 1) * S] + scale * dot_nn(low_scr[rows, :rank], bg[ids[t], :, cols])
-            u = zu[t * S:(t + 1) * S] + scale * dot_nn(low_scr[rows, rank:], bu[ids[t], :, cols])
-            hid_scr[rows, cols] = (jax.nn.silu(g) * u).astype(BF16)
-
-    arrive(2)
-    for t in range(chips):
-        out_ref[t, :, D:] = dot_nn(hid_scr[pl.ds(t * S, S), :], ad[ids[t]]).astype(BF16)
-
-    @pl.loop(0, D // nt)
-    def _(j):
-        cols = pl.ds(pl.multiple_of(j * nt, nt), nt)
-        z = dot_nn(hid_scr[...], wd[:, cols])
-        for t in range(chips):
-            out_ref[t, :, cols] = z[t * S:(t + 1) * S].astype(BF16)
-
-
-def finish_body(dims, meta, x_ref, rs_ref, bd_ref, out_ref):
-    rank, D = dims
-    scale = ALPHA / rank
-    nt = 256
-    low = rs_ref[0, :, D:]
-
-    @pl.loop(0, D // nt)
-    def _(j):
-        cols = pl.ds(pl.multiple_of(j * nt, nt), nt)
-        delta = scale * dot_nn(low, bd_ref[0, :, cols])
-        out_ref[0, :, cols] = (x_ref[0, 0, :, cols].astype(F32) + rs_ref[0, :, cols].astype(F32) + delta).astype(BF16)
+        for c in copies_f(j) + copies_p(j)[1:]:
+            c.wait_send()
+        for c in copies_p(j):
+            c.wait_recv()
 
 
 def solution(mesh):
@@ -330,7 +462,6 @@
                 P(None, 'tensor', None, None), last_split,
                 last_split, last_split, last_split, last_split,
                 P(None, 'tensor', None), last_split)
-    same_core = [[c + CORES * i for i in range(chips)] for c in range(CORES)]
     swap = [(i, i ^ 1) for i in range(n_dev)]
     ANY = pl.BlockSpec(memory_space=pl.ANY)
 
@@ -341,12 +472,8 @@
         rl = a_q.shape[2]
         half = hd // 2
         qw = nq * hd
-        me = lax.axis_index('tensor')
-        core, chip = me % CORES, me // CORES
-        meta = jnp.concatenate([adapter_ids.astype(jnp.int32), core.reshape(1).astype(jnp.int32)])
         per = seqs // chips
         steps = per // CORES
-        spc = steps // CHUNKS
 
         def rows_t(w):
             return jnp.transpose(w, (1, 2, 0)).reshape(-1, w.shape[0])
@@ -383,9 +510,6 @@
         x4 = x_in.reshape(chips, per, S, D)
         M = chips * S
         Fc = CORES * w_gate.shape[1]
-        full = lambda shape: pl.BlockSpec(shape, lambda i, m: (0,) * len(shape))
-        params = pltpu.CompilerParams(vmem_limit_bytes=VMEM_LIMIT, dimension_semantics=("arbitrary",))
-        y = jnp.zeros((n_dev, steps * S, D), BF16)
         x1_all = pl.pallas_call(
             functools.partial(attn_body, (n_dev, seqs, S, hd, nq, rank, D, chips)),
             in_specs=[pl.BlockSpec(memory_space=pltpu.SMEM), ANY] + [pl.BlockSpec(memory_space=pltpu.VMEM)] * 3 + [ANY] * 4,
@@ -401,44 +525,27 @@
             cost_estimate=pl.CostEstimate(flops=3 * steps * M * D * (2 * n_dev * qw + 2 * n_dev * hd + 4 * rank),
                                           bytes_accessed=6 * steps * M * D + 33 * 2**20, transcendentals=0),
         )(adapter_ids, x4, gain_attn.reshape(1, D), cos_t, sin_t, g_w, a_qkv, g_b, g_wo)
-        for c in range(CHUNKS):
-            base_step = c * spc
-            tok = M * spc
-            pairs = [w for own, other in zip(mlp_own, mlp_other) for w in (own, other)]
-            part = pl.pallas_call(
-                functools.partial(mlp_body, (seqs, S, rank, D, spc, base_step, chips)),
-                grid_spec=pltpu.PrefetchScalarGridSpec(
-                    num_scalar_prefetch=1, grid=(spc,),
-                    in_specs=[pl.BlockSpec((chips, 1, S, D), lambda i, m, b=base_step: (0, b + i, 0, 0)), full((1, D))] + [ANY] * 13,
-                    out_specs=pl.BlockSpec((chips, S, D + rank), lambda i, m: (0, i, 0)),
-                    scratch_shapes=[
-                        pltpu.VMEM((D, Fc), BF16), pltpu.VMEM((D, Fc), BF16), pltpu.VMEM((Fc, D), BF16),
-                        pltpu.VMEM((n_ad, rank, Fc), BF16), pltpu.VMEM((n_ad, rank, Fc), BF16),
-                        pltpu.VMEM((n_ad, D, 2 * rank), BF16), pltpu.VMEM((n_ad, Fc, rank), BF16),
-                        pltpu.VMEM((M, D), BF16), pltpu.VMEM((M, 2 * rank), BF16), pltpu.VMEM((M, Fc), BF16),
-                        pltpu.SemaphoreType.DMA((3,))]),
-                out_shape=jax.ShapeDtypeStruct((chips, spc * S, D + rank), BF16),
-                compiler_params=params, name="mlp_block",
-                cost_estimate=pl.CostEstimate(flops=2 * tok * D * (3 * Fc + 4 * rank),
-                                              bytes_accessed=4 * tok * D + 34 * 2**20, transcendentals=tok * Fc),
-            )(meta, x1_all, gain_mlp.reshape(1, D), a_gu, *pairs)
-            rs = lax.psum_scatter(part, 'tensor', scatter_dimension=0, axis_index_groups=same_core, tiled=True)
-            own = [adapter_ids[chip * per + core * steps + base_step + i] for i in range(spc)]
-            meta2 = jnp.concatenate([jnp.stack(own).astype(jnp.int32), chip.reshape(1).astype(jnp.int32)])
-            y_own = pl.pallas_call(
-                functools.partial(finish_body, (rank, D)),
-                grid_spec=pltpu.PrefetchScalarGridSpec(
-                    num_scalar_prefetch=1, grid=(spc,),
-                    in_specs=[pl.BlockSpec((1, 1, S, D), lambda i, m, b=base_step: (m[spc], b + i, 0, 0)),
-                              pl.BlockSpec((1, S, D + rank), lambda i, m: (i, 0, 0)),
-                              pl.BlockSpec((1, rank, D), lambda i, m: (m[i], 0, 0))],
-                    out_specs=pl.BlockSpec((1, S, D), lambda i, m: (i, 0, 0))),
-                out_shape=jax.ShapeDtypeStruct((spc, S, D), BF16),
-                compiler_params=pltpu.CompilerParams(dimension_semantics=("arbitrary",)), name="finish",
-                cost_estimate=pl.CostEstimate(flops=2 * spc * S * rank * D, bytes_accessed=10 * spc * S * D, transcendentals=0),
-            )(meta2, x1_all, rs.reshape(spc, S, D + rank), bd_full)
-            y_all = gather(y_own.reshape(spc * S, D))
-            y = lax.dynamic_update_slice(y, y_all, (0, base_step * S, 0))
+        pairs = [w for own, other in zip(mlp_own, mlp_other) for w in (own, other)]
+        dma = pltpu.SemaphoreType.DMA
+        y = pl.pallas_call(
+            functools.partial(mlp_body, (seqs, S, rank, D, chips)),
+            in_specs=[pl.BlockSpec(memory_space=pltpu.SMEM), ANY, pl.BlockSpec(memory_space=pltpu.VMEM)] + [ANY] * 14,
+            out_specs=ANY,
+            scratch_shapes=[
+                pltpu.VMEM((D, Fc), BF16), pltpu.VMEM((D, Fc), BF16), pltpu.VMEM((Fc, D), BF16),
+                pltpu.VMEM((n_ad, rank, Fc), BF16), pltpu.VMEM((n_ad, rank, Fc), BF16),
+                pltpu.VMEM((n_ad, D, 2 * rank), BF16), pltpu.VMEM((n_ad, Fc, rank), BF16), pltpu.VMEM((n_ad, rank, D), BF16),
+                pltpu.VMEM((2, chips, S, D), BF16), pltpu.VMEM((M, D), BF16), pltpu.VMEM((M, 2 * rank), BF16), pltpu.VMEM((M, Fc), BF16),
+                pltpu.VMEM((3, chips, S, D + rank), BF16), pltpu.VMEM((2, 4, S // 2, D + rank), BF16),
+                pltpu.VMEM((2, 3, S, D + rank), BF16), pltpu.VMEM((2, S, D), BF16), pltpu.VMEM((2, S, D), BF16),
+                dma((14,)), dma((4,)), dma((2,)), dma((2, steps)), dma((2, steps)), dma((2, steps)), dma((2, steps)),
+                dma((2, steps)), dma((2, steps)), dma((2, steps)), dma((2, steps)), dma((4, steps)), dma((4, steps))],
+            out_shape=jax.ShapeDtypeStruct((n_dev, steps, S, D), BF16),
+            compiler_params=pltpu.CompilerParams(vmem_limit_bytes=VMEM_LIMIT, collective_id=0, has_side_effects=True),
+            name="mlp_ring",
+            cost_estimate=pl.CostEstimate(flops=2 * steps * M * D * (3 * Fc + 4 * rank),
+                                          bytes_accessed=8 * steps * M * D + 34 * 2**20, transcendentals=steps * M * Fc),
+        )(adapter_ids, x1_all, gain_mlp.reshape(1, D), a_gu, *pairs, bd_full)
         return y.reshape(seqs, S, D)
 
     return jax.shard_map(local_layer, mesh=mesh, in_specs=in_specs, out_specs=P('data', None, None), check_vma=False)

time: 1010 us -> 940 us (0.931)
  waiting for transfers between devices: 356 us -> 203 us
  Pallas kernels: 552 us -> 665 us
  local copies, waits for them, and re-layouts: 70.7 us -> 53.8 us
    all_gather x4 -> x0, waiting for transfers between devices: 153 us -> none  [local_layer(): y_all = gather(y_own.reshape(spc * S, D))]
    pallas_call x8 -> x1, Pallas kernels: 239 us -> 351 us  [local_layer(): pl.pallas_call(functools.partial(mlp_body, (seqs, S, rank, D, chips)), in...]
    dynamic_update_slice x4 -> x0, local copies, waits for them, and re-layouts: 38.8 us -> none  [local_layer(): y = lax.dynamic_update_slice(y, y_all, (0, base_step * S, 0))]
    unnamed x33 -> x32, local copies, waits for them, and re-layouts: 6.57 us -> 28.8 us
    reduce_scatter x4 -> x0, waiting for transfers between devices: 14.6 us -> none  [local_layer(): lax.psum_scatter(part, 'tensor', scatter_dimension=0, axis_index_groups=s...]
    all_gather x1, waiting for transfers between devices: 0.01 us -> 13 us  [local_layer(): g_bd = gather(b_down.reshape(n_ad * rank, qw))]
  transfers between devices with their start and end apart: 19 -> 11, of which waited for: 9 -> 5; matrix products, arithmetic and copies ran while one was open for 6% -> 3% of each run, Pallas kernels for 55% -> 33%
where the time goes in v3:
time: 940 us; the launch traced here: 939 us
  Pallas kernels  665 us (71%)
  waiting for transfers between devices  203 us (22%)
  local copies, waits for them, and re-layouts  53.8 us (6%)
  between operations  13.4 us (1%)
    pallas_call x1, Pallas kernels, local_layer(): pl.pallas_call(functools.partial(mlp_body, (seqs, S, rank, D, chips)), in...  351 us
    pallas_call x1, Pallas kernels, local_layer(): pl.pallas_call(functools.partial(attn_body, (n_dev, seqs, S, hd, nq, rank...  313 us
    all_gather x1, waiting for transfers between devices, local_layer(): gather(jnp.concatenate([rows_t(w_q), rows_t(w_k), rows_t(w_v)], axis=0))  64.9 us
    all_gather x1, waiting for transfers between devices, local_layer(): gather(jnp.concatenate([jnp.transpose(a, (0, 2, 1)).reshape(n_ad * rl, D)...  51.2 us
    all_gather x1, waiting for transfers between devices, local_layer(): g_wo = gather(w_o.reshape(qw, D))  47.1 us
    unnamed x32, local copies, waits for them, and re-layouts  28.8 us
    all_gather x1, waiting for transfers between devices, local_layer(): g_b = gather(jnp.concatenate(b_parts, axis=0))  25 us
  transfers between devices with their start and end apart: 11, of which 5 were waited for; matrix products, arithmetic and copies ran while one was open for 3% of the time, Pallas kernels for 33%

profile of v3, /device:TPU:113, one launch (start us, length us, event | category | flops | bytes accessed | tf_op | source)
XLA Modules:
  0.0 939.2 jit_solution(2227265245854601375)
XLA Ops:
  6.6 0.1 all-gather.11.cloned.1.call-start
  6.6 0.7 all-gather.11.cloned.1.call-update
  7.3 0.1 all-gather.15.cloned.1.call-start
  7.4 1.0 constant_dynamic-update-slice_fusion.4
  8.4 1.0 constant_dynamic-update-slice_fusion.3
  9.4 1.0 constant_dynamic-update-slice_fusion.2
  10.3 1.0 constant_dynamic-update-slice_fusion.1
  11.3 0.0 copy-start.2
  11.3 0.0 copy-start.3
  11.3 0.0 copy-start.4
  11.3 1.1 constant_dynamic-update-slice_fusion
  12.4 0.0 copy-start
  12.4 1.0 copy-done
  13.5 0.1 all-gather.15.cloned.1.call-update
  13.6 0.1 all-gather.17.cloned.1.call-start
  13.8 1.0 constant_dynamic-update-slice_fusion.5
  14.8 0.0 copy-start.9
  14.8 0.9 copy-done.1
  15.7 0.1 all-gather.17.cloned.1.call-update
  15.8 0.1 all-gather.9.cloned.1.call-start
  15.9 0.6 all-gather.9.cloned.1.call-update
  16.4 0.1 all-gather.13.cloned.1.call-start
  16.5 1.3 pad_maximum_fusion
  17.8 0.1 all-gather.13.cloned.1.call-update
  17.9 0.8 collective-permute-start.3
  18.6 0.1 collective-permute-start.4
  18.7 0.4 collective-permute-start.5
  19.1 0.1 collective-permute-start
  19.2 0.4 collective-permute-start.1
  19.7 0.8 fusion
  20.4 13.0 %all-gather.11.cloned.1.call-done = bf16[8,512,256]{2,1,0:T(8,128)(2,1)} async-done(((bf16[1,512,256]{2,1,0:T(8,128)(2,1)}), bf16[8,512,256]{2,1,0:T(8,128)(2,1)}) %all-gather.11.cloned.1.call-update) | async-done | bytes 2097168 | tf_op jit(solution)/shard_map/all_gather | solution.py:500
  33.4 2.8 copy.37
  36.2 2.6 reshape.103.bd_ref
  38.7 51.2 %all-gather.15.cloned.1.call-done = bf16[2560,2048]{1,0:T(8,128)(2,1)} async-done(((bf16[320,2048]{1,0:T(8,128)(2,1)}), bf16[2560,2048]{1,0:T(8,128)(2,1)}) %all-gather.15.cloned.1.call-update) | async-done | bytes 10485776 | tf_op jit(solution)/shard_map/all_gather | solution.py:484
  89.9 3.4 slice_bitcast_fusion
  93.3 3.2 copy.32
  96.4 2.5 slice_bitcast_fusion.1
  98.9 2.3 copy.33
  101.2 6.2 copy.35.agu_ref
  107.5 0.3 collective-permute-start.2
  107.7 25.0 %all-gather.17.cloned.1.call-done = bf16[14336,256]{1,0:T(8,128)(2,1)} async-done(((bf16[1792,256]{1,0:T(8,128)(2,1)}), bf16[14336,256]{1,0:T(8,128)(2,1)}) %all-gather.17.cloned.1.call-update) | async-done | bytes 7340048 | tf_op jit(solution)/shard_map/all_gather | solution.py:498
  132.8 47.1 %all-gather.9.cloned.1.call-done.gwo_ref = bf16[8,256,2048]{2,1,0:T(8,128)(2,1)} async-done(((bf16[1,256,2048]{2,1,0:T(8,128)(2,1)}), bf16[8,256,2048]{2,1,0:T(8,128)(2,1)}) %all-gather.9.cloned.1.call-update) | async-done | bytes 8388624 | tf_op jit(solution)/shard_map/all_gather | solution.py:499
  179.9 64.9 %all-gather.13.cloned.1.call-done = bf16[3072,2048]{1,0:T(8,128)(2,1)} async-done(((bf16[384,2048]{1,0:T(8,128)(2,1)}), bf16[3072,2048]{1,0:T(8,128)(2,1)}) %all-gather.13.cloned.1.call-update) | async-done | bytes 12582928 | tf_op jit(solution)/shard_map/all_gather | solution.py:489
  244.8 313.3 %attn_block.1.x_ref = bf16[4,8,128,2048]{3,2,1,0:T(8,128)(2,1)} custom-call(s32[64]{0:T(128)} %ids_ref.3, bf16[4,16,128,2048]{3,2,1,0:T(8,128)(2,1)} %bitcast.102, f32[1,2048]{1,0:T(1,128)} %bitcast.105, f32[32,128]{1,0:T(8,128)} %get-tuple-element.8.cos_ref, f32[32,128]{1,0:T(8,128)} %get-tuple-element.7.sin_ref, bf16[8,384,2048]{2,1,0:T(8,128)(2,1)} %bitcast.103, ...), custom_call_target="tpu_custom_call" | custom-call | flops 154618822656 | bytes 84934656 | tf_op jit(solution)/shard_map/attn_block/pallas_call | solution.py:513
  558.2 0.0 collective-permute-done.wg1
  558.2 0.0 collective-permute-done.1.wu1
  558.2 351.5 %mlp_ring.1 = bf16[8,8,128,2048]{3,2,1,0:T(8,128)(2,1)} custom-call(s32[64]{0:T(128)} %ids_ref.3, bf16[4,8,128,2048]{3,2,1,0:T(8,128)(2,1)} %attn_block.1.x_ref, f32[1,2048]{1,0:T(1,128)} %bitcast.106, bf16[2,2048,512]{2,1,0:T(8,128)(2,1)} %copy.35.agu_ref, bf16[2048,1024]{1,0:T(8,128)(2,1)} %wg0.1, bf16[2048,1024]{1,0:T(8,128)(2,1)} %collective-permute-done.wg1, ...), custom_call_target="tpu_custom_call" | custom-call | flops 120259084288 | bytes 102760448 | tf_op jit(solution)/shard_map/mlp_ring/pallas_call | solution.py:530
  909.7 22.9 %copy.50 = bf16[64,128,2048]{2,1,0:T(8,128)(2,1)} copy(bf16[64,128,2048]{2,1,0:T(8,128)(2,1)} %bitcast.81) | data formatting | bytes 67108864
  (26 shorter events, 0.1 us)
Async XLA Ops:
  6.5 7.1 copy-start.5
  6.5 7.1 copy-start.7
  6.6 7.2 copy-start.8
  6.6 7.2 copy-start.6
  6.6 26.9 %all-gather.11.cloned.1.call-start = ((), (), s32[]{:S(2)}) async-start(), calls=%async_computation.1 | async-start | bytes 2359296 | tf_op jit(solution)/shard_map/all_gather | solution.py:500
  7.3 82.5 %all-gather.15.cloned.1.call-start = ((), (), s32[]{:S(2)}) async-start(), calls=%async_computation.3 | async-start | bytes 11796480 | tf_op jit(solution)/shard_map/all_gather | solution.py:484
  11.3 5.2 copy-start.2
  11.3 5.2 copy-start.3
  11.3 5.2 copy-start.4
  12.4 1.1 copy-start
  13.6 119.2 %all-gather.17.cloned.1.call-start = ((), (), s32[]{:S(2)}) async-start(), calls=%async_computation.4 | async-start | bytes 8257536 | tf_op jit(solution)/shard_map/all_gather | solution.py:498
  14.8 0.9 copy-start.1
  14.8 3.1 copy-start.9
  15.8 164.1 %all-gather.9.cloned.1.call-start = ((), (), s32[]{:S(2)}) async-start(), calls=%async_computation | async-start | bytes 9437184 | tf_op jit(solution)/shard_map/all_gather | solution.py:499
  16.4 228.4 %all-gather.13.cloned.1.call-start = ((), (), s32[]{:S(2)}) async-start(), calls=%async_computation.2 | async-start | bytes 14155776 | tf_op jit(solution)/shard_map/all_gather | solution.py:489
  17.9 89.6 %collective-permute-start.3 = (bf16[2,256,1024]{2,1,0:T(8,128)(2,1)S(1)}, bf16[2,256,1024]{2,1,0:T(8,128)(2,1)}, u32[]{:S(2)}, u32[]{:S(2)}) collective-permute-start(bf16[2,256,1024]{2,1,0:T(8,128)(2,1)S(1)} %copy-done.9), channel_id=1, source_target_pairs={{0,1},{1,0},{2,3},{3,2},{4,5},{5,4},{6,7},{7,6},{8,9},{9,8},{10,11... | collective-permute-start | bytes 3145736 | tf_op jit(solution)/shard_map/ppermute | solution.py:503
  18.6 539.5 %collective-permute-start.4 = (bf16[2,256,1024]{2,1,0:T(8,128)(2,1)}, bf16[2,256,1024]{2,1,0:T(8,128)(2,1)}, u32[]{:S(2)}, u32[]{:S(2)}) collective-permute-start(bf16[2,256,1024]{2,1,0:T(8,128)(2,1)} %bu0.1), channel_id=1, source_target_pairs={{0,1},{1,0},{2,3},{3,2},{4,5},{5,4},{6,7},{7,6},{8,9},{9,8},{10,11... | collective-permute-start | bytes 3145736 | tf_op jit(solution)/shard_map/ppermute | solution.py:503
  18.7 539.4 %collective-permute-start.5 = (bf16[2,1024,256]{2,1,0:T(8,128)(2,1)}, bf16[2,1024,256]{2,1,0:T(8,128)(2,1)}, u32[]{:S(2)}, u32[]{:S(2)}) collective-permute-start(bf16[2,1024,256]{2,1,0:T(8,128)(2,1)} %ad0.1), channel_id=1, source_target_pairs={{0,1},{1,0},{2,3},{3,2},{4,5},{5,4},{6,7},{7,6},{8,9},{9,8},{10,11... | collective-permute-start | bytes 3145736 | tf_op jit(solution)/shard_map/ppermute | solution.py:503
  19.1 539.0 %collective-permute-start = (bf16[2048,1024]{1,0:T(8,128)(2,1)}, bf16[2048,1024]{1,0:T(8,128)(2,1)}, u32[]{:S(2)}, u32[]{:S(2)}) collective-permute-start(bf16[2048,1024]{1,0:T(8,128)(2,1)} %wg0.1), channel_id=1, source_target_pairs={{0,1},{1,0},{2,3},{3,2},{4,5},{5,4},{6,7},{7,6},{8,9},{9,8},{10,11... | collective-permute-start | bytes 12582920 | tf_op jit(solution)/shard_map/ppermute | solution.py:503
  19.2 538.9 %collective-permute-start.1 = (bf16[2048,1024]{1,0:T(8,128)(2,1)}, bf16[2048,1024]{1,0:T(8,128)(2,1)}, u32[]{:S(2)}, u32[]{:S(2)}) collective-permute-start(bf16[2048,1024]{1,0:T(8,128)(2,1)} %wu0.1), channel_id=1, source_target_pairs={{0,1},{1,0},{2,3},{3,2},{4,5},{5,4},{6,7},{7,6},{8,9},{9,8},{10,11... | collective-permute-start | bytes 12582920 | tf_op jit(solution)/shard_map/ppermute | solution.py:503
  107.5 450.7 %collective-permute-start.2 = (bf16[1024,2048]{1,0:T(8,128)(2,1)}, bf16[1024,2048]{1,0:T(8,128)(2,1)}, u32[]{:S(2)}, u32[]{:S(2)}) collective-permute-start(bf16[1024,2048]{1,0:T(8,128)(2,1)} %wd0.1), channel_id=1, source_target_pairs={{0,1},{1,0},{2,3},{3,2},{4,5},{5,4},{6,7},{7,6},{8,9},{9,8},{10,11... | collective-permute-start | bytes 12582920 | tf_op jit(solution)/shard_map/ppermute | solution.py:503
Sparse Core Ops, SparseCore 0:
  9.0 24.3 all-gather.10
  35.0 54.8 all-gather.14
  91.5 41.2 all-gather.16
  134.2 45.5 all-gather.8
  181.3 63.4 all-gather.12

commit v4 on v3

--- a/solution.py
+++ b/solution.py
@@ -23,20 +23,68 @@
     return lax.dot_general(a, b, (((1,), (1,)), ((), ())), preferred_element_type=F32)
 
 
-def attn_body(dims, ids_ref, x_ref, gain_ref, cos_ref, sin_ref, gw_ref, aqkv_ref, gb_ref, gwo_ref, out_ref,
-              h, low, attn, w, bw, q_scr, k_scr, v_scr, lowo, wsem, xsem, osem):
+def attn_body(dims, ids_ref, x_ref, gain_ref, cos_ref, sin_ref, a_own, w_own, b_own, out_ref, ga, gw, gb,
+              h, low, attn, w, bw, q_scr, k_scr, v_scr, asem, wsem, xsem, osem, ss, rs):
     n_dev, seqs, S, hd, nq, rank, D, chips = dims
     half = hd // 2
     qw = nq * hd
     n_ad = 2
     scale = ALPHA / rank
-    core = lax.axis_index('tensor') % CORES
+    me = lax.axis_index('tensor')
+    core, chip = me % CORES, me // CORES
     per = seqs // chips
     steps = per // CORES
     M = chips * S
-    pw = CORES * (qw + 2 * hd)
-    kw = CORES * qw
-    vw = kw + CORES * hd
+    dw = qw + 2 * hd
+    rl = rank // n_dev
+    right_chip, left_chip, far_chip = (chip + 1) % chips, (chip + chips - 1) % chips, (chip + 2) % chips
+    order = [(chip + r) % chips for r in range(chips)]
+    right, left, far = [c * CORES + core for c in (right_chip, left_chip, far_chip)]
+    other = chip * CORES + (1 - core)
+
+    barrier = pltpu.get_barrier_semaphore()
+    for dev in (right, left, other):
+        pl.semaphore_signal(barrier, inc=1, device_id={'tensor': dev}, device_id_type=pl.DeviceIdType.MESH)
+    pl.semaphore_wait(barrier, 3)
+
+    groups = ((a_own, ga), (w_own, gw), (b_own, gb))
+
+    def remote(m, n, src, dst, dev):
+        return pltpu.make_async_remote_copy(src_ref=src, dst_ref=dst, send_sem=ss.at[m, n], recv_sem=rs.at[m, n],
+                                            device_id={'tensor': dev}, device_id_type=pl.DeviceIdType.MESH)
+
+    def copy(m, n):
+        own, buf = groups[m]
+        n_rows = own.shape[0] // 2
+        if n == 0:
+            return remote(m, n, own, buf.at[me], right)
+        if n == 1:
+            return remote(m, n, own, buf.at[me], left)
+        if n == 2:
+            part = buf.at[left, pl.ds(0, n_rows)]
+            return remote(m, n, part, part, right)
+        if n == 3:
+            part = buf.at[right, pl.ds(n_rows, n_rows)]
+            return remote(m, n, part, part, left)
+        if n == 4:
+            return remote(m, n, own, buf.at[me], other)
+        dev = (left, right, far)[n - 5]
+        return remote(m, n, buf.at[dev], buf.at[dev], other)
+
+    def send_own(m):
+        for n in (0, 1, 4):
+            copy(m, n).start()
+
+    def pass_on(m):
+        for n in (0, 1):
+            copy(m, n).wait_recv()
+            copy(m, 2 + n).start()
+            copy(m, 5 + n).start()
+
+    def pass_far(m):
+        for n in (2, 3):
+            copy(m, n).wait_recv()
+        copy(m, 7).start()
 
     def seq_id(i, t):
         return ids_ref[t * per + core * steps + i]
@@ -44,89 +92,97 @@
     def tile(i):
         return pl.ds(pl.multiple_of(i * M, M), M)
 
-    a_rows = n_ad * 3 * rank
-    x_base = 4 * M
-    plan_a = [(aqkv_ref, attn.at[pl.ds(0, a_rows)])]
-    plan_w = []
-    for p in range(chips):
-        plan = []
-        for c in range(CORES):
-            d = p * CORES + c
-            plan += [(gw_ref.at[d, pl.ds(0, qw)], w.at[p, pl.ds(c * qw, qw)]),
-                     (gw_ref.at[d, pl.ds(qw, hd)], w.at[p, pl.ds(kw + c * hd, hd)]),
-                     (gw_ref.at[d, pl.ds(qw + hd, hd)], w.at[p, pl.ds(vw + c * hd, hd)])]
+    x_base = 4
+
+    def a_copies(dev, src, n):
+        out = []
+        for pr in range(3):
             for a in range(n_ad):
-                o = a * (qw + 2 * hd)
-                plan += [(gb_ref.at[d, pl.ds(o, qw)], bw.at[p, a, pl.ds(c * qw, qw)]),
-                         (gb_ref.at[d, pl.ds(o + qw, hd)], bw.at[p, a, pl.ds(kw + c * hd, hd)]),
-                         (gb_ref.at[d, pl.ds(o + qw + hd, hd)], bw.at[p, a, pl.ds(vw + c * hd, hd)])]
-        plan_w.append(plan)
-    plan_o = []
-    off = n_ad * (qw + 2 * hd)
-    for d in range(n_dev):
-        plan_o.append((gwo_ref.at[d], h.at[pl.ds(d * qw, qw)]))
-        for a in range(n_ad):
-            plan_o.append((gb_ref.at[d, pl.ds(off + a * qw, qw)], low.at[pl.ds((a * n_dev + d) * qw, qw), pl.ds(0, rank)]))
-            plan_o.append((gb_ref.at[d, pl.ds(off + n_ad * qw + a * rank, rank)],
-                           h.at[pl.ds(n_dev * qw + a * rank, rank), pl.ds(d * qw, qw)]))
-
-    def start(plan, sem):
-        for s, d in plan:
-            pltpu.make_async_copy(s, d, sem).start()
-
-    def finish(plan, sem):
-        for s, d in plan:
-            pltpu.make_async_copy(s, d, sem).wait()
-
-    def x_copies(i, buf, base, slot):
+                k = pr * n_ad + a
+                o = pl.multiple_of(dev * rl, rl)
+                dst = attn.at[a, pl.ds(pr * rank + o, rl)] if pr < 2 else attn.at[n_ad + a, pl.ds(o, rl)]
+                out.append(pltpu.make_async_copy(src.at[pl.ds(k * rl, rl)], dst, asem.at[n, k]))
+        return out
+
+    def w_copies(r):
+        out = []
+        for n, c in enumerate((core, 1 - core)):
+            src = w_own if r == 0 and n == 0 else gw.at[order[r] * CORES + c]
+            out.append(pltpu.make_async_copy(src, w.at[r, pl.ds(pl.multiple_of(c * dw, dw), dw)], wsem.at[r, n, 0]))
+        return out
+
+    def b_copies(r):
+        out = []
+        for n, c in enumerate((core, 1 - core)):
+            src = b_own if r == 0 and n == 0 else gb.at[order[r] * CORES + c]
+            for a in range(n_ad):
+                out.append(pltpu.make_async_copy(src.at[pl.ds(a * dw, dw)],
+                                                 bw.at[r, a, pl.ds(pl.multiple_of(c * dw, dw), dw)], wsem.at[r, n, 1 + a]))
+        return out
+
+    def x_copies(i, slot):
         return [pltpu.make_async_copy(x_ref.at[t, core * steps + i],
-                                      buf.at[pl.ds(pl.multiple_of(base + slot * M + t * S, S), S)], xsem.at[slot])
+                                      attn.at[x_base + slot, pl.ds(t * S, S)], xsem.at[slot, t])
                 for t in range(chips)]
 
-    start(plan_a, wsem.at[chips])
-    for c in x_copies(0, attn, x_base, 0):
+    send_own(0)
+    for c in x_copies(0, 0):
         c.start()
-    for p in range(chips):
-        start(plan_w[p], wsem.at[p])
-
     rb = 16
 
     @pl.loop(0, steps)
     def _(i):
         slot = i % 2
-        for c in x_copies(i, attn, x_base, slot):
+        for c in x_copies(i, slot):
             c.wait()
 
         @pl.when(i + 1 < steps)
         def _():
-            for c in x_copies(i + 1, attn, x_base, 1 - slot):
+            for c in x_copies(i + 1, 1 - slot):
                 c.start()
 
         @pl.loop(0, M // rb)
         def _(r):
-            v = attn[pl.ds(pl.multiple_of(x_base + slot * M + r * rb, rb), rb), :].astype(F32)
+            v = attn[x_base + slot, pl.ds(pl.multiple_of(r * rb, rb), rb), :].astype(F32)
             inv = lax.rsqrt(jnp.mean(v * v, axis=-1, keepdims=True) + EPSILON)
             h[pl.ds(pl.multiple_of(i * M + r * rb, rb), rb), :] = (v * inv * gain_ref[...]).astype(BF16)
 
-        @pl.when(i == 0)
-        def _():
-            finish(plan_a, wsem.at[chips])
+    pass_on(0)
+    send_own(1)
+    send_own(2)
+    devs = [order[r] * CORES + c for r in range(chips) for c in (core, 1 - core)]
+    pass_far(0)
+    for n in range(4):
+        copy(0, 4 + n).wait_recv()
+    stacks = [c for n, dev in enumerate(devs) for c in a_copies(dev, a_own if n == 0 else ga.at[dev], n)]
+    for c in stacks:
+        c.start()
+    for c in stacks:
+        c.wait()
+
+    @pl.loop(0, steps)
+    def _(i):
         for t in range(chips):
             rows = pl.ds(pl.multiple_of(i * M + t * S, S), S)
-            a = attn[pl.ds(pl.multiple_of(seq_id(i, t) * 3 * rank, 3 * rank), 3 * rank), :]
-            low[rows, :] = dot_nt(h[rows, :], a).astype(BF16)
+            idx = seq_id(i, t)
+            low[rows, :2 * rank] = dot_nt(h[rows, :], attn[idx]).astype(BF16)
+            low[rows, 2 * rank:] = dot_nt(h[rows, :], attn[n_ad + idx, :rank]).astype(BF16)
 
     def produce(it, slot):
-        p, i = it // steps, it % steps
-        z = dot_nt(w[p], h[tile(i), :])
+        r, i = it // steps, it % steps
+        z = dot_nt(w[r], h[tile(i), :])
         for t in range(chips):
             rows = pl.ds(pl.multiple_of(i * M + t * S, S), S)
-            b = bw[p, seq_id(i, t)]
+            b = bw[r, seq_id(i, t)]
             lo = low[rows, :]
             cols = slice(t * S, (t + 1) * S)
-            zq = z[:kw, cols] + scale * dot_nt(b[:kw], lo[:, :rank])
-            zk = z[kw:vw, cols] + scale * dot_nt(b[kw:vw], lo[:, rank:2 * rank])
-            zv = z[vw:, cols] + scale * dot_nt(b[vw:], lo[:, 2 * rank:])
+
+            def project(o, n, c0):
+                zz = jnp.concatenate([z[c * dw + o:c * dw + o + n, cols] for c in range(CORES)], axis=0)
+                bb = jnp.concatenate([b[c * dw + o:c * dw + o + n] for c in range(CORES)], axis=0)
+                return zz + scale * dot_nt(bb, lo[:, c0:c0 + rank])
+
+            zq, zk, zv = project(0, qw, 0), project(qw, hd, rank), project(qw + hd, hd, 2 * rank)
             cos, sin = cos_ref[...], sin_ref[...]
 
             def rotate(v):
@@ -143,7 +199,8 @@
             v_scr[slot, :, cols] = zv.astype(BF16)
 
     def consume(it, slot):
-        p, i = it // steps, it % steps
+        r, i = it // steps, it % steps
+        p = (chip + r) % chips
         key = lax.broadcasted_iota(jnp.int32, (S, S), 0)
         qry = lax.broadcasted_iota(jnp.int32, (S, S), 1)
         causal = key <= qry
@@ -159,71 +216,94 @@
                     ps.append((e * (1.0 / jnp.sum(e, axis=0, keepdims=True))).astype(BF16))
                 o = dot_nn(v_scr[slot, c * hd:(c + 1) * hd, cols], jnp.concatenate(ps, axis=1))
                 o = jnp.concatenate([o[:, hh * S:(hh + 1) * S] for hh in range(nq)], axis=0)
-                attn[pl.ds(pl.multiple_of(i * M + t * S, S), S),
+                attn[i, pl.ds(t * S, S),
                      pl.ds(pl.multiple_of((p * CORES + c) * qw, qw), qw)] = o.T.astype(BF16)
 
-    finish(plan_w[0], wsem.at[0])
+    def out_copy(i):
+        return pltpu.make_async_copy(attn.at[i], out_ref.at[i], osem.at[i])
+
+    for m in (1, 2):
+        copy(m, 4).wait_recv()
+    for c in w_copies(0) + b_copies(0):
+        c.start()
+    for c in w_copies(0) + b_copies(0):
+        c.wait()
     produce(0, 0)
 
     @pl.loop(0, chips * steps)
     def _(it):
         nxt = jnp.minimum(it + 1, chips * steps - 1)
-        for p in range(1, chips):
-            @pl.when(it == p * steps - 1)
+
+        @pl.when(it == 2)
+        def _():
+            pass_on(1)
+            pass_on(2)
+
+        @pl.when(it == steps)
+        def _():
+            pass_far(1)
+            pass_far(2)
+        for r in range(1, chips):
+            @pl.when(it == r * steps - 2)
             def _():
-                finish(plan_w[p], wsem.at[p])
+                for m in (1, 2):
+                    copy(m, (4, 6, 7, 5)[r]).wait_recv()
+                for c in w_copies(r):
+                    c.start()
+
+            @pl.when(it == r * steps - 1)
+            def _():
+                for c in b_copies(r):
+                    c.start()
+                for c in w_copies(r) + b_copies(r):
+                    c.wait()
         consume(it, it % 2)
+
+        @pl.when(it >= (chips - 1) * steps)
+        def _():
+            out_copy(it % steps).start()
         produce(nxt, (it + 1) % 2)
 
-    start(plan_o, wsem.at[chips])
-    o_base = n_dev * qw + n_ad * rank
-    o_slots = 3
-
-    def o_copies(i, slot):
-        return [pltpu.make_async_copy(h.at[pl.ds(pl.multiple_of(o_base + slot * M + t * S, S), S)],
-                                      out_ref.at[t, i], osem.at[slot]) for t in range(chips)]
-
-    for c in x_copies(0, h, o_base, 0):
-        c.start()
-    finish(plan_o, wsem.at[chips])
+    for i in range(steps):
+        out_copy(i).wait()
+    for m in range(3):
+        for n in range(8):
+            copy(m, n).wait_send()
+
+
+def oproj_body(dims, meta, attn_ref, x_ref, gwo_ref, gb_ref, out_ref, wo, ao, bo, low, sems):
+    n_dev, seqs, S, qw, rank, D, chips = dims
+    n_ad = 2
+    scale = ALPHA / rank
+    step = pl.program_id(0)
+    core = meta[seqs]
+    per = seqs // chips
+    steps = per // CORES
+    plan = [(gwo_ref, wo)]
+    for d in range(n_dev):
+        for a in range(n_ad):
+            plan.append((gb_ref.at[d, pl.ds(a * qw, qw)], ao.at[a, pl.ds(d * qw, qw)]))
+            plan.append((gb_ref.at[d, pl.ds(n_ad * qw + a * rank, rank)], bo.at[a, :, pl.ds(d * qw, qw)]))
+
+    @pl.when(step == 0)
+    def _():
+        for s, d in plan:
+            pltpu.make_async_copy(s, d, sems.at[0]).start()
+        for s, d in plan:
+            pltpu.make_async_copy(s, d, sems.at[0]).wait()
+
+    ids = [meta[t * per + core * steps + step] for t in range(chips)]
+    for t in range(chips):
+        low[pl.ds(t * S, S), :] = dot_nn(attn_ref[0, pl.ds(t * S, S), :], ao[ids[t]]).astype(BF16)
     nt = 256
 
-    @pl.loop(0, steps)
-    def _(i):
-        slot = i % o_slots
-        nslot = (i + 1) % o_slots
-        for c in x_copies(i, h, o_base, slot):
-            c.wait()
-
-        @pl.when(i + 1 < steps)
-        def _():
-            @pl.when(i + 1 >= o_slots)
-            def _():
-                for c in o_copies(i + 1 - o_slots, nslot):
-                    c.wait()
-            for c in x_copies(i + 1, h, o_base, nslot):
-                c.start()
-
+    @pl.loop(0, D // nt)
+    def _(j):
+        cols = pl.ds(pl.multiple_of(j * nt, nt), nt)
+        zo = dot_nn(attn_ref[0], wo[:, cols])
         for t in range(chips):
-            rows = pl.ds(pl.multiple_of(i * M + t * S, S), S)
-            a = low[pl.ds(pl.multiple_of(seq_id(i, t) * n_dev * qw, qw), n_dev * qw), :rank]
-            lowo[pl.ds(t * S, S), :] = dot_nn(attn[rows, :], a).astype(BF16)
-
-        @pl.loop(0, D // nt)
-        def _(j):
-            cols = pl.ds(pl.multiple_of(j * nt, nt), nt)
-            zo = dot_nn(attn[tile(i), :], h[pl.ds(0, n_dev * qw), cols])
-            for t in range(chips):
-                b = h[pl.ds(pl.multiple_of(n_dev * qw + seq_id(i, t) * rank, rank), rank), cols]
-                z = zo[t * S:(t + 1) * S] + scale * dot_nn(lowo[pl.ds(t * S, S), :], b)
-                rows = pl.ds(pl.multiple_of(o_base + slot * M + t * S, S), S)
-                h[rows, cols] = (h[rows, cols].astype(F32) + z).astype(BF16)
-        for c in o_copies(i, slot):
-            c.start()
-
-    for i in range(max(0, steps - o_slots), steps):
-        for c in o_copies(i, i % o_slots):
-            c.wait()
+            z = zo[t * S:(t + 1) * S] + scale * dot_nn(low[pl.ds(t * S, S), :], bo[ids[t], :, cols])
+            out_ref[t, 0, :, cols] = (x_ref[t, 0, :, cols].astype(F32) + z).astype(BF16)
 
 
 def mlp_body(dims, ids_ref, x_ref, gain_ref, agu_ref, wg0, wg1, wu0, wu1, wd0, wd1, bg0, bg1, bu0, bu1, ad0, ad1, bd_ref,
@@ -481,24 +561,21 @@
         gather = functools.partial(lax.all_gather, axis_name='tensor', axis=0)
         swapped = functools.partial(lax.ppermute, axis_name='tensor', perm=swap)
 
-        g_a = gather(jnp.concatenate([jnp.transpose(a, (0, 2, 1)).reshape(n_ad * rl, D)
-                                      for a in (a_q, a_k, a_v, a_gate, a_up)], axis=0))
-        g_a = g_a.reshape(n_dev, 5, n_ad, rl, D)
-        a_qkv = g_a[:, :3].transpose(2, 1, 0, 3, 4).reshape(n_ad * 3 * rank, D)
-        a_gu = g_a[:, 3:].transpose(2, 4, 1, 0, 3).reshape(n_ad, D, 2 * rank)
-        g_w = gather(jnp.concatenate([rows_t(w_q), rows_t(w_k), rows_t(w_v)], axis=0))
+        def rows_a(stacks):
+            return jnp.concatenate([jnp.transpose(a, (0, 2, 1)).reshape(n_ad * rl, D) for a in stacks], axis=0)
 
         def b_rows(b):
             return jnp.transpose(b, (1, 2, 0)).reshape(-1, rank)
 
-        b_parts = []
-        for a in range(n_ad):
-            b_parts += [b_rows(b_q[a]), b_rows(b_k[a]), b_rows(b_v[a])]
-        b_parts += [a_o.reshape(n_ad * qw, rank), b_o.reshape(n_ad * rank, qw)]
-        g_b = gather(jnp.concatenate(b_parts, axis=0))
+        a_own = rows_a((a_q, a_k, a_v))
+        w_own = jnp.concatenate([rows_t(w_q), rows_t(w_k), rows_t(w_v)], axis=0)
+        b_own = jnp.concatenate([b_rows(b[a]) for a in range(n_ad) for b in (b_q, b_k, b_v)], axis=0)
         g_wo = gather(w_o.reshape(qw, D))
-        g_bd = gather(b_down.reshape(n_ad * rank, qw))
-        bd_full = g_bd.reshape(n_dev, n_ad, rank, qw).transpose(1, 2, 0, 3).reshape(n_ad, rank, D)
+        g_b = gather(jnp.concatenate([a_o.reshape(n_ad * qw, rank), b_o.reshape(n_ad * rank, qw),
+                                      b_down.reshape(n_ad * rank, qw)], axis=0))
+        bd_full = g_b[:, n_ad * (qw + rank):].reshape(n_dev, n_ad, rank, qw).transpose(1, 2, 0, 3).reshape(n_ad, rank, D)
+        g_gu = gather(rows_a((a_gate, a_up))).reshape(n_dev, 2, n_ad, rl, D)
+        a_gu = g_gu.transpose(2, 4, 1, 0, 3).reshape(n_ad, D, 2 * rank)
         mlp_own = (w_gate, w_up, w_down, b_gate, b_up, a_down)
         mlp_other = tuple(swapped(w) for w in mlp_own)
 
@@ -510,23 +587,41 @@
         x4 = x_in.reshape(chips, per, S, D)
         M = chips * S
         Fc = CORES * w_gate.shape[1]
+        dma = pltpu.SemaphoreType.DMA
+        dw = qw + 2 * hd
+        attn_all = pl.pallas_call(
+            functools.partial(attn_body, (n_dev, seqs, S, hd, nq, rank, D, chips)),
+            in_specs=[pl.BlockSpec(memory_space=pltpu.SMEM), ANY] + [pl.BlockSpec(memory_space=pltpu.VMEM)] * 3 + [ANY] * 3,
+            out_specs=[ANY] * 4,
+            scratch_shapes=[
+                pltpu.VMEM((steps * M, D), BF16), pltpu.VMEM((steps * M, 3 * rank), BF16), pltpu.VMEM((steps, M, n_dev * qw), BF16),
+                pltpu.VMEM((chips, CORES * dw, D), BF16), pltpu.VMEM((chips, n_ad, CORES * dw, rank), BF16),
+                pltpu.VMEM((2, CORES * qw, M), BF16), pltpu.VMEM((2, CORES, M, hd), BF16), pltpu.VMEM((2, CORES * hd, M), BF16),
+                dma((n_dev, 3 * n_ad)), dma((chips, CORES, 1 + n_ad)), dma((2, chips)), dma((steps,)), dma((3, 8)), dma((3, 8))],
+            out_shape=[jax.ShapeDtypeStruct((steps, M, n_dev * qw), BF16), jax.ShapeDtypeStruct((n_dev,) + a_own.shape, BF16),
+                       jax.ShapeDtypeStruct((n_dev,) + w_own.shape, BF16), jax.ShapeDtypeStruct((n_dev,) + b_own.shape, BF16)],
+            compiler_params=pltpu.CompilerParams(vmem_limit_bytes=VMEM_LIMIT, collective_id=1, has_side_effects=True),
+            name="attn_ring",
+            cost_estimate=pl.CostEstimate(flops=3 * steps * M * D * (n_dev * qw + 2 * n_dev * hd + 3 * rank),
+                                          bytes_accessed=6 * steps * M * D + 33 * 2**20, transcendentals=0),
+        )(adapter_ids, x4, gain_attn.reshape(1, D), cos_t, sin_t, a_own, w_own, b_own)[0]
+        core = lax.axis_index('tensor') % CORES
+        meta = jnp.concatenate([adapter_ids.astype(jnp.int32), core.reshape(1).astype(jnp.int32)])
         x1_all = pl.pallas_call(
-            functools.partial(attn_body, (n_dev, seqs, S, hd, nq, rank, D, chips)),
-            in_specs=[pl.BlockSpec(memory_space=pltpu.SMEM), ANY] + [pl.BlockSpec(memory_space=pltpu.VMEM)] * 3 + [ANY] * 4,
-            out_specs=ANY,
-            scratch_shapes=[
-                pltpu.VMEM((steps * M, D), BF16), pltpu.VMEM((steps * M, 3 * rank), BF16), pltpu.VMEM((steps * M, n_dev * qw), BF16),
-                pltpu.VMEM((chips, CORES * (qw + 2 * hd), D), BF16), pltpu.VMEM((chips, n_ad, CORES * (qw + 2 * hd), rank), BF16),
-                pltpu.VMEM((2, CORES * qw, M), BF16), pltpu.VMEM((2, CORES, M, hd), BF16), pltpu.VMEM((2, CORES * hd, M), BF16),
-                pltpu.VMEM((M, rank), BF16),
-                pltpu.SemaphoreType.DMA((chips + 1,)), pltpu.SemaphoreType.DMA((3,)), pltpu.SemaphoreType.DMA((3,))],
+            functools.partial(oproj_body, (n_dev, seqs, S, qw, rank, D, chips)),
+            grid_spec=pltpu.PrefetchScalarGridSpec(
+                num_scalar_prefetch=1, grid=(steps,),
+                in_specs=[pl.BlockSpec((1, M, n_dev * qw), lambda i, m: (i, 0, 0)),
+                          pl.BlockSpec((chips, 1, S, D), lambda i, m: (0, m[seqs] * steps + i, 0, 0)), ANY, ANY],
+                out_specs=pl.BlockSpec((chips, 1, S, D), lambda i, m: (0, i, 0, 0)),
+                scratch_shapes=[pltpu.VMEM((n_dev * qw, D), BF16), pltpu.VMEM((n_ad, n_dev * qw, rank), BF16),
+                                pltpu.VMEM((n_ad, rank, D), BF16), pltpu.VMEM((M, rank), BF16), dma((1,))]),
             out_shape=jax.ShapeDtypeStruct((chips, steps, S, D), BF16),
-            compiler_params=pltpu.CompilerParams(vmem_limit_bytes=VMEM_LIMIT), name="attn_block",
-            cost_estimate=pl.CostEstimate(flops=3 * steps * M * D * (2 * n_dev * qw + 2 * n_dev * hd + 4 * rank),
-                                          bytes_accessed=6 * steps * M * D + 33 * 2**20, transcendentals=0),
-        )(adapter_ids, x4, gain_attn.reshape(1, D), cos_t, sin_t, g_w, a_qkv, g_b, g_wo)
+            compiler_params=pltpu.CompilerParams(vmem_limit_bytes=VMEM_LIMIT, dimension_semantics=("arbitrary",)), name="oproj",
+            cost_estimate=pl.CostEstimate(flops=2 * steps * M * D * (D + 2 * rank),
+                                          bytes_accessed=6 * steps * M * D + 12 * 2**20, transcendentals=0),
+        )(meta, attn_all, x4, g_wo.reshape(n_dev * qw, D), g_b)
         pairs = [w for own, other in zip(mlp_own, mlp_other) for w in (own, other)]
-        dma = pltpu.SemaphoreType.DMA
         y = pl.pallas_call(
             functools.partial(mlp_body, (seqs, S, rank, D, chips)),
             in_specs=[pl.BlockSpec(memory_space=pltpu.SMEM), ANY, pl.BlockSpec(memory_space=pltpu.VMEM)] + [ANY] * 14,

time: 940 us -> 759 us (0.81)
  waiting for transfers between devices: 203 us -> 0.85 us
  Pallas kernels: 665 us -> 693 us
  local copies, waits for them, and re-layouts: 53.8 us -> 39.3 us
    all_gather x4 -> x2, waiting for transfers between devices: 154 us -> 0.01 us  [the longest x1 0.01 us: local_layer(): g_gu = gather(rows_a((a_gate, a_up))).reshape(n_dev, 2, n_ad, rl, D)]
    pallas_call x0 -> x1, Pallas kernels: none -> 66.6 us  [local_layer(): pl.pallas_call(functools.partial(oproj_body, (n_dev, seqs, S, qw, rank, D...]
    all_gather x1, waiting for transfers between devices: 47.1 us -> 0.01 us  [local_layer(): g_wo = gather(w_o.reshape(qw, D))]
    pallas_call x1, Pallas kernels: 313 us -> 274 us  [local_layer(): pl.pallas_call(functools.partial(attn_body, (n_dev, seqs, S, hd, nq, rank...]
    unnamed x32 -> x30, local copies, waits for them, and re-layouts: 28.8 us -> 23 us
  transfers between devices with their start and end apart: 11 -> 9, of which waited for: 5 -> 0; matrix products, arithmetic and copies ran while one was open for 3% -> 3% of each run, Pallas kernels for 33% -> 45%
where the time goes in v4:
time: 759 us
  Pallas kernels  693 us (91%)
  local copies, waits for them, and re-layouts  39.3 us (5%)
  between operations  13.4 us (2%)
  other arithmetic  7.72 us (1%)
    pallas_call x1, Pallas kernels, local_layer(): pl.pallas_call(functools.partial(mlp_body, (seqs, S, rank, D, chips)), in...  352 us
    pallas_call x1, Pallas kernels, local_layer(): pl.pallas_call(functools.partial(attn_body, (n_dev, seqs, S, hd, nq, rank...  274 us
    pallas_call x1, Pallas kernels, local_layer(): pl.pallas_call(functools.partial(oproj_body, (n_dev, seqs, S, qw, rank, D...  66.6 us
    unnamed x30, local copies, waits for them, and re-layouts  23 us
  transfers between devices with their start and end apart: 9, of which 0 were waited for; matrix products, arithmetic and copies ran while one was open for 3% of the time, Pallas kernels for 45%

profile of v4, /device:TPU:113, one launch (start us, length us, event | category | flops | bytes accessed | tf_op | source)
XLA Modules:
  0.0 758.8 jit_solution(17701494424213091136)
XLA Ops:
  6.6 0.0 all-gather.10.cloned.1.call-start
  6.6 0.0 copy-start.5
  6.6 0.0 copy-start.6
  6.6 2.0 pad_maximum_fusion.3
  8.5 0.1 all-gather.10.cloned.1.call-update
  8.6 0.1 all-gather.8.cloned.1.call-start
  8.7 0.0 copy-start
  8.7 0.0 copy-start.1
  8.7 0.0 copy-start.2
  8.7 2.2 pad_maximum_fusion.2
  10.9 0.1 all-gather.8.cloned.1.call-update
  10.9 0.1 all-gather.6.cloned.1.call-start
  11.0 0.7 all-gather.6.cloned.1.call-update
  11.7 0.8 collective-permute-start
  12.5 0.1 collective-permute-start.1
  12.6 0.4 collective-permute-start.2
  13.0 0.1 collective-permute-start.3
  13.1 0.4 collective-permute-start.4
  13.5 0.0 copy-done.3
  13.6 0.0 copy-done.7
  13.6 0.0 copy-done.8
  13.7 0.7 fusion
  14.4 0.0 copy-start.9
  14.4 0.0 copy-done.4
  14.4 0.0 copy-done.5
  14.4 0.0 copy-done.6
  14.5 1.0 pad_maximum_fusion.1.a_own
  15.4 0.0 copy-done
  15.5 1.2 pad_maximum_fusion.w_own
  16.7 274.4 %attn_ring.1 = (bf16[8,512,2048]{2,1,0:T(8,128)(2,1)}, bf16[8,192,2048]{2,1,0:T(8,128)(2,1)}, bf16[8,384,2048]{2,1,0:T(8,128)(2,1)}, bf16[8,768,256]{2,1,0:T(8,128)(2,1)}) custom-call(s32[64]{0:T(128)} %ids_ref.3, bf16[4,16,128,2048]{3,2,1,0:T(8,128)(2,1)} %bitcast.100, f32[1,2048]{1,0:T(1,128)} %bitcast.103, f32[32,128]{1,0:T(8,128)} %get-tuple-element.10.cos_ref, ...), custom_call_target="tpu_custom_call" | custom-call | flops 96636764160 | bytes 84934656 | tf_op jit(solution)/shard_map/attn_ring/pallas_call | solution.py:592
  291.1 0.0 copy-done.11
  291.1 0.6 pad_add_fusion.meta
  291.7 4.8 copy.30
  296.5 6.2 copy.32.agu_ref
  302.7 1.7 slice.28
  304.5 1.2 copy.34
  305.6 0.0 copy-start.10
  305.7 2.4 reshape.111.bd_ref
  308.0 0.0 collective-permute-done.3.bg1
  308.0 2.3 collective-permute-start.5
  310.3 66.6 %oproj.1.x_ref = bf16[4,8,128,2048]{3,2,1,0:T(8,128)(2,1)} custom-call(s32[65]{0:T(128)} %pad_add_fusion.meta, bf16[8,512,2048]{2,1,0:T(8,128)(2,1)} %get-tuple-element.6.attn_ref, bf16[4,16,128,2048]{3,2,1,0:T(8,128)(2,1)} %bitcast.101, bf16[2048,2048]{1,0:T(8,128)(2,1)} %bitcast.102, bf16[8,1536,256]{2,1,0:T(8,128)(2,1)} %bitcast.87), custom_call_target="tpu_custom_call" | custom-call | flops 42949672960 | bytes 62914560 | tf_op jit(solution)/shard_map/oproj/pallas_call | solution.py:610
  376.9 0.0 collective-permute-done.4.bu1
  376.9 0.0 collective-permute-done.5.ad1
  376.9 0.0 collective-permute-done.wg1
  377.0 0.0 collective-permute-done.1.wu1
  377.0 0.0 collective-permute-done.2.wd1
  377.0 352.4 %mlp_ring.1 = bf16[8,8,128,2048]{3,2,1,0:T(8,128)(2,1)} custom-call(s32[64]{0:T(128)} %ids_ref.3, bf16[4,8,128,2048]{3,2,1,0:T(8,128)(2,1)} %oproj.1.x_ref, f32[1,2048]{1,0:T(1,128)} %bitcast.104, bf16[2,2048,512]{2,1,0:T(8,128)(2,1)} %copy.32.agu_ref, bf16[2048,1024]{1,0:T(8,128)(2,1)} %wg0.1, bf16[2048,1024]{1,0:T(8,128)(2,1)} %collective-permute-done.wg1, ...), custom_call_target="tpu_custom_call" | custom-call | flops 120259084288 | bytes 102760448 | tf_op jit(solution)/shard_map/mlp_ring/pallas_call | solution.py:625
  729.4 22.9 %copy.41 = bf16[64,128,2048]{2,1,0:T(8,128)(2,1)} copy(bf16[64,128,2048]{2,1,0:T(8,128)(2,1)} %bitcast.79) | data formatting | bytes 67108864
  (20 shorter events, 0.1 us)
Async XLA Ops:
  6.5 7.0 copy-start.3
  6.5 7.0 copy-start.7
  6.6 7.1 copy-start.8
  6.6 285.2 %all-gather.10.cloned.1.call-start = ((), (), s32[]{:S(2)}) async-start(), calls=%async_computation.2 | async-start | bytes 4718592 | tf_op jit(solution)/shard_map/all_gather | solution.py:577
  6.6 7.9 %copy-start.4 = (bf16[2,2048,32]{1,2,0:T(8,128)(2,1)S(1)}, bf16[2,2048,32]{1,2,0:T(8,128)(2,1)}, u32[]{:S(2)}) copy-start(bf16[2,2048,32]{1,2,0:T(8,128)(2,1)} %param.40) | copy-start | bytes 786436
  6.6 7.9 %copy-start.5 = (bf16[2,2048,32]{1,2,0:T(8,128)(2,1)S(1)}, bf16[2,2048,32]{1,2,0:T(8,128)(2,1)}, u32[]{:S(2)}) copy-start(bf16[2,2048,32]{1,2,0:T(8,128)(2,1)} %param.38) | copy-start | bytes 786436
  6.6 7.9 %copy-start.6 = (bf16[2,2048,32]{1,2,0:T(8,128)(2,1)S(1)}, bf16[2,2048,32]{1,2,0:T(8,128)(2,1)}, u32[]{:S(2)}) copy-start(bf16[2,2048,32]{1,2,0:T(8,128)(2,1)} %param.36) | copy-start | bytes 786436
  8.6 294.1 %all-gather.8.cloned.1.call-start = ((), (), s32[]{:S(2)}) async-start(), calls=%async_computation.1 | async-start | bytes 7077888 | tf_op jit(solution)/shard_map/all_gather | solution.py:574
  8.7 6.8 copy-start
  8.7 6.8 copy-start.1
  8.7 6.8 copy-start.2
  10.9 299.4 %all-gather.6.cloned.1.call-start = ((), (), s32[]{:S(2)}) async-start(), calls=%async_computation | async-start | bytes 9437184 | tf_op jit(solution)/shard_map/all_gather | solution.py:573
  11.7 365.2 %collective-permute-start = (bf16[2048,1024]{1,0:T(8,128)(2,1)}, bf16[2048,1024]{1,0:T(8,128)(2,1)}, u32[]{:S(2)}, u32[]{:S(2)}) collective-permute-start(bf16[2048,1024]{1,0:T(8,128)(2,1)} %wg0.1), channel_id=1, source_target_pairs={{0,1},{1,0},{2,3},{3,2},{4,5},{5,4},{6,7},{7,6},{8,9},{9,8},{10,11... | collective-permute-start | bytes 12582920 | tf_op jit(solution)/shard_map/ppermute | solution.py:580
  12.5 364.4 %collective-permute-start.1 = (bf16[2048,1024]{1,0:T(8,128)(2,1)}, bf16[2048,1024]{1,0:T(8,128)(2,1)}, u32[]{:S(2)}, u32[]{:S(2)}) collective-permute-start(bf16[2048,1024]{1,0:T(8,128)(2,1)} %wu0.1), channel_id=1, source_target_pairs={{0,1},{1,0},{2,3},{3,2},{4,5},{5,4},{6,7},{7,6},{8,9},{9,8},{10,11... | collective-permute-start | bytes 12582920 | tf_op jit(solution)/shard_map/ppermute | solution.py:580
  12.6 364.4 %collective-permute-start.2 = (bf16[1024,2048]{1,0:T(8,128)(2,1)}, bf16[1024,2048]{1,0:T(8,128)(2,1)}, u32[]{:S(2)}, u32[]{:S(2)}) collective-permute-start(bf16[1024,2048]{1,0:T(8,128)(2,1)} %wd0.1), channel_id=1, source_target_pairs={{0,1},{1,0},{2,3},{3,2},{4,5},{5,4},{6,7},{7,6},{8,9},{9,8},{10,11... | collective-permute-start | bytes 12582920 | tf_op jit(solution)/shard_map/ppermute | solution.py:580
  13.0 295.0 %collective-permute-start.3 = (bf16[2,256,1024]{2,1,0:T(8,128)(2,1)}, bf16[2,256,1024]{2,1,0:T(8,128)(2,1)}, u32[]{:S(2)}, u32[]{:S(2)}) collective-permute-start(bf16[2,256,1024]{2,1,0:T(8,128)(2,1)} %bg0.1), channel_id=1, source_target_pairs={{0,1},{1,0},{2,3},{3,2},{4,5},{5,4},{6,7},{7,6},{8,9},{9,8},{10,11... | collective-permute-start | bytes 3145736 | tf_op jit(solution)/shard_map/ppermute | solution.py:580
  13.1 363.8 %collective-permute-start.4 = (bf16[2,256,1024]{2,1,0:T(8,128)(2,1)}, bf16[2,256,1024]{2,1,0:T(8,128)(2,1)}, u32[]{:S(2)}, u32[]{:S(2)}) collective-permute-start(bf16[2,256,1024]{2,1,0:T(8,128)(2,1)} %bu0.1), channel_id=1, source_target_pairs={{0,1},{1,0},{2,3},{3,2},{4,5},{5,4},{6,7},{7,6},{8,9},{9,8},{10,11... | collective-permute-start | bytes 3145736 | tf_op jit(solution)/shard_map/ppermute | solution.py:580
  14.4 2.3 copy-start.9
  16.7 274.4 %copy-start.11 = (s32[64]{0:T(128)S(1)}, s32[64]{0:T(128)}, u32[]{:S(2)}) copy-start(s32[64]{0:T(128)} %ids_ref.3) | copy-start | bytes 772
  305.6 2.4 copy-start.10
  308.0 68.9 %collective-permute-start.5 = (bf16[2,1024,256]{2,1,0:T(8,128)(2,1)S(1)}, bf16[2,1024,256]{2,1,0:T(8,128)(2,1)}, u32[]{:S(2)}, u32[]{:S(2)}) collective-permute-start(bf16[2,1024,256]{2,1,0:T(8,128)(2,1)S(1)} %copy-done.10), channel_id=1, source_target_pairs={{0,1},{1,0},{2,3},{3,2},{4,5},{5,4},{6,7},{7,6},{8,9},{9,8},{10,11... | collective-permute-start | bytes 3145736 | tf_op jit(solution)/shard_map/ppermute | solution.py:580
Sparse Core Ops, SparseCore 0:
  9.0 46.9 all-gather.9
  57.5 61.7 all-gather.7
  120.9 68.4 all-gather.5

commit v5 on v4

--- a/solution.py
+++ b/solution.py
@@ -89,9 +89,6 @@
     def seq_id(i, t):
         return ids_ref[t * per + core * steps + i]
 
-    def tile(i):
-        return pl.ds(pl.multiple_of(i * M, M), M)
-
     x_base = 4
 
     def a_copies(dev, src, n):
@@ -145,7 +142,12 @@
         def _(r):
             v = attn[x_base + slot, pl.ds(pl.multiple_of(r * rb, rb), rb), :].astype(F32)
             inv = lax.rsqrt(jnp.mean(v * v, axis=-1, keepdims=True) + EPSILON)
-            h[pl.ds(pl.multiple_of(i * M + r * rb, rb), rb), :] = (v * inv * gain_ref[...]).astype(BF16)
+            attn[x_base + 2, pl.ds(pl.multiple_of(r * rb, rb), rb), :] = (v * inv * gain_ref[...]).astype(BF16)
+
+        @pl.loop(0, D // S)
+        def _(c):
+            block = pl.ds(pl.multiple_of(c * S, S), S)
+            h[i, block, :] = attn[x_base + 2, :, block].T
 
     pass_on(0)
     send_own(1)
@@ -163,24 +165,22 @@
     @pl.loop(0, steps)
     def _(i):
         for t in range(chips):
-            rows = pl.ds(pl.multiple_of(i * M + t * S, S), S)
             idx = seq_id(i, t)
-            low[rows, :2 * rank] = dot_nt(h[rows, :], attn[idx]).astype(BF16)
-            low[rows, 2 * rank:] = dot_nt(h[rows, :], attn[n_ad + idx, :rank]).astype(BF16)
+            cols = slice(t * S, (t + 1) * S)
+            low[i, :2 * rank, cols] = dot_nn(attn[idx], h[i, :, cols]).astype(BF16)
+            low[i, 2 * rank:, cols] = dot_nn(attn[n_ad + idx, :rank], h[i, :, cols]).astype(BF16)
 
     def produce(it, slot):
         r, i = it // steps, it % steps
-        z = dot_nt(w[r], h[tile(i), :])
+        z = dot_nn(w[r], h[i])
         for t in range(chips):
-            rows = pl.ds(pl.multiple_of(i * M + t * S, S), S)
             b = bw[r, seq_id(i, t)]
-            lo = low[rows, :]
             cols = slice(t * S, (t + 1) * S)
 
             def project(o, n, c0):
                 zz = jnp.concatenate([z[c * dw + o:c * dw + o + n, cols] for c in range(CORES)], axis=0)
                 bb = jnp.concatenate([b[c * dw + o:c * dw + o + n] for c in range(CORES)], axis=0)
-                return zz + scale * dot_nt(bb, lo[:, c0:c0 + rank])
+                return zz + scale * dot_nn(bb, low[i, c0:c0 + rank, cols])
 
             zq, zk, zv = project(0, qw, 0), project(qw, hd, rank), project(qw + hd, hd, 2 * rank)
             cos, sin = cos_ref[...], sin_ref[...]
@@ -363,7 +363,16 @@
     def store_y(j):
         return pltpu.make_async_copy(ybuf.at[j % 2], y_ref.at[me, j], osem.at[j % 2])
 
-    plans = [[(agu_ref, agu)], [], [(bd_ref, bd)]]
+    n_dev = chips * CORES
+    rl = rank // n_dev
+    ow = D // n_dev
+    n_ad = agu.shape[0]
+    plans = [[], [], []]
+    for d in range(n_dev):
+        for a in range(n_ad):
+            for pr in range(2):
+                plans[0].append((agu_ref.at[d, pl.ds((pr * n_ad + a) * rl, rl)], agu.at[a, pl.ds(pr * rank + d * rl, rl)]))
+            plans[2].append((bd_ref.at[d, pl.ds(n_ad * (ow + rank) + a * rank, rank)], bd.at[a, :, pl.ds(d * ow, ow)]))
     for i, (g, u, b1, b2) in enumerate(((wg0, wu0, bg0, bu0), (wg1, wu1, bg1, bu1))):
         c = pl.ds(i * fw, fw)
         plans[1] += [(g, wg.at[:, c]), (u, wu.at[:, c]), (b1, bg.at[:, :, c]), (b2, bu.at[:, :, c])]
@@ -418,7 +427,7 @@
 
         arrive(0, k)
         for t in range(chips):
-            low_scr[pl.ds(t * S, S), :] = dot_nn(h_scr[pl.ds(t * S, S), :], agu[ids[t]]).astype(BF16)
+            low_scr[pl.ds(t * S, S), :] = dot_nt(h_scr[pl.ds(t * S, S), :], agu[ids[t]]).astype(BF16)
         arrive(1, k)
 
         @pl.loop(0, wg.shape[1] // nt)
@@ -573,9 +582,7 @@
         g_wo = gather(w_o.reshape(qw, D))
         g_b = gather(jnp.concatenate([a_o.reshape(n_ad * qw, rank), b_o.reshape(n_ad * rank, qw),
                                       b_down.reshape(n_ad * rank, qw)], axis=0))
-        bd_full = g_b[:, n_ad * (qw + rank):].reshape(n_dev, n_ad, rank, qw).transpose(1, 2, 0, 3).reshape(n_ad, rank, D)
-        g_gu = gather(rows_a((a_gate, a_up))).reshape(n_dev, 2, n_ad, rl, D)
-        a_gu = g_gu.transpose(2, 4, 1, 0, 3).reshape(n_ad, D, 2 * rank)
+        g_gu = gather(rows_a((a_gate, a_up)))
         mlp_own = (w_gate, w_up, w_down, b_gate, b_up, a_down)
         mlp_other = tuple(swapped(w) for w in mlp_own)
 
@@ -594,7 +601,7 @@
             in_specs=[pl.BlockSpec(memory_space=pltpu.SMEM), ANY] + [pl.BlockSpec(memory_space=pltpu.VMEM)] * 3 + [ANY] * 3,
             out_specs=[ANY] * 4,
             scratch_shapes=[
-                pltpu.VMEM((steps * M, D), BF16), pltpu.VMEM((steps * M, 3 * rank), BF16), pltpu.VMEM((steps, M, n_dev * qw), BF16),
+                pltpu.VMEM((steps, D, M), BF16), pltpu.VMEM((steps, 3 * rank, M), BF16), pltpu.VMEM((steps, M, n_dev * qw), BF16),
                 pltpu.VMEM((chips, CORES * dw, D), BF16), pltpu.VMEM((chips, n_ad, CORES * dw, rank), BF16),
                 pltpu.VMEM((2, CORES * qw, M), BF16), pltpu.VMEM((2, CORES, M, hd), BF16), pltpu.VMEM((2, CORES * hd, M), BF16),
                 dma((n_dev, 3 * n_ad)), dma((chips, CORES, 1 + n_ad)), dma((2, chips)), dma((steps,)), dma((3, 8)), dma((3, 8))],
@@ -629,18 +636,18 @@
             scratch_shapes=[
                 pltpu.VMEM((D, Fc), BF16), pltpu.VMEM((D, Fc), BF16), pltpu.VMEM((Fc, D), BF16),
                 pltpu.VMEM((n_ad, rank, Fc), BF16), pltpu.VMEM((n_ad, rank, Fc), BF16),
-                pltpu.VMEM((n_ad, D, 2 * rank), BF16), pltpu.VMEM((n_ad, Fc, rank), BF16), pltpu.VMEM((n_ad, rank, D), BF16),
+                pltpu.VMEM((n_ad, 2 * rank, D), BF16), pltpu.VMEM((n_ad, Fc, rank), BF16), pltpu.VMEM((n_ad, rank, D), BF16),
                 pltpu.VMEM((2, chips, S, D), BF16), pltpu.VMEM((M, D), BF16), pltpu.VMEM((M, 2 * rank), BF16), pltpu.VMEM((M, Fc), BF16),
                 pltpu.VMEM((3, chips, S, D + rank), BF16), pltpu.VMEM((2, 4, S // 2, D + rank), BF16),
                 pltpu.VMEM((2, 3, S, D + rank), BF16), pltpu.VMEM((2, S, D), BF16), pltpu.VMEM((2, S, D), BF16),
-                dma((14,)), dma((4,)), dma((2,)), dma((2, steps)), dma((2, steps)), dma((2, steps)), dma((2, steps)),
+                dma((12 + n_dev * n_ad * 3,)), dma((4,)), dma((2,)), dma((2, steps)), dma((2, steps)), dma((2, steps)), dma((2, steps)),
                 dma((2, steps)), dma((2, steps)), dma((2, steps)), dma((2, steps)), dma((4, steps)), dma((4, steps))],
             out_shape=jax.ShapeDtypeStruct((n_dev, steps, S, D), BF16),
             compiler_params=pltpu.CompilerParams(vmem_limit_bytes=VMEM_LIMIT, collective_id=0, has_side_effects=True),
             name="mlp_ring",
             cost_estimate=pl.CostEstimate(flops=2 * steps * M * D * (3 * Fc + 4 * rank),
                                           bytes_accessed=8 * steps * M * D + 34 * 2**20, transcendentals=steps * M * Fc),
-        )(adapter_ids, x1_all, gain_mlp.reshape(1, D), a_gu, *pairs, bd_full)
+        )(adapter_ids, x1_all, gain_mlp.reshape(1, D), g_gu, *pairs, g_b)
         return y.reshape(seqs, S, D)
 
     return jax.shard_map(local_layer, mesh=mesh, in_specs=in_specs, out_specs=P('data', None, None), check_vma=False)

time: 759 us -> 752 us (level)
  local copies, waits for them, and re-layouts: 39.3 us -> 23 us
  Pallas kernels: 693 us -> 704 us
    reshape x3 -> x0, local copies, waits for them, and re-layouts: 9.75 us -> none  [the longest x1 6.19 us: local_layer(): a_gu = g_gu.transpose(2, 4, 1, 0, 3).reshape(n_ad, D, 2 * rank)]
    unnamed x30 -> x34, local copies, waits for them, and re-layouts: 23 us -> 23 us
  transfers between devices with their start and end apart: 9 -> 9, of which waited for: 0 -> 0; matrix products, arithmetic and copies ran while one was open for 3% -> 1% of each run, Pallas kernels for 45% -> 46%
where the time goes in v5:
time: 752 us
  Pallas kernels  704 us (94%)
  local copies, waits for them, and re-layouts  23 us (3%)
  between operations  13.4 us (2%)
    pallas_call x1, Pallas kernels, local_layer(): pl.pallas_call(functools.partial(mlp_body, (seqs, S, rank, D, chips)), in...  359 us
    pallas_call x1, Pallas kernels, local_layer(): pl.pallas_call(functools.partial(attn_body, (n_dev, seqs, S, hd, nq, rank...  279 us
    pallas_call x1, Pallas kernels, local_layer(): pl.pallas_call(functools.partial(oproj_body, (n_dev, seqs, S, qw, rank, D...  66.4 us
    unnamed x34, local copies, waits for them, and re-layouts  23 us
  transfers between devices with their start and end apart: 9, of which 0 were waited for; matrix products, arithmetic and copies ran while one was open for 1% of the time, Pallas kernels for 46%

profile of v5, /device:TPU:113, one launch (start us, length us, event | category | flops | bytes accessed | tf_op | source)
XLA Modules:
  0.0 752.0 jit_solution(14503040276799199892)
XLA Ops:
  6.5 0.0 copy-start.4
  6.6 0.1 all-gather.8.cloned.1.call-start
  6.6 0.0 copy-start.6
  6.6 0.0 copy-start.7
  6.7 0.0 copy-start.8
  6.7 2.2 pad_maximum_fusion.2
  8.8 0.1 all-gather.8.cloned.1.call-update
  8.9 0.1 all-gather.6.cloned.1.call-start
  9.0 0.7 all-gather.6.cloned.1.call-update
  9.7 0.1 all-gather.10.cloned.1.call-start
  9.8 0.8 collective-permute-start.3
  10.6 0.1 collective-permute-start.4
  10.7 0.4 collective-permute-start
  11.1 0.1 collective-permute-start.1
  11.2 0.4 collective-permute-start.2
  11.6 0.0 copy-done.4
  11.6 0.0 copy-done.5
  11.6 0.8 pad_maximum_fusion.3
  12.4 0.1 all-gather.10.cloned.1.call-update
  12.5 0.8 fusion
  13.2 0.0 copy-done.3
  13.3 0.0 copy-done.9
  13.3 0.0 copy-done.10
  13.4 0.0 copy-start.11
  13.4 0.0 copy-done.6
  13.4 0.0 copy-done.7
  13.4 0.0 copy-done.8
  13.4 1.0 pad_maximum_fusion.1.a_own
  14.4 0.0 copy-done
  14.4 0.0 copy-done.1
  14.4 0.0 copy-done.2
  14.4 1.2 pad_maximum_fusion.w_own
  15.6 0.0 copy-done.11
  15.6 279.0 %attn_ring.1 = (bf16[8,512,2048]{2,1,0:T(8,128)(2,1)}, bf16[8,192,2048]{2,1,0:T(8,128)(2,1)}, bf16[8,384,2048]{2,1,0:T(8,128)(2,1)}, bf16[8,768,256]{2,1,0:T(8,128)(2,1)}) custom-call(s32[64]{0:T(128)} %ids_ref.3, bf16[4,16,128,2048]{3,2,1,0:T(8,128)(2,1)} %bitcast.85, f32[1,2048]{1,0:T(1,128)} %bitcast.91, f32[32,128]{1,0:T(8,128)} %get-tuple-element.10.cos_ref, ...), custom_call_target="tpu_custom_call" | custom-call | flops 96636764160 | bytes 84934656 | tf_op jit(solution)/shard_map/attn_ring/pallas_call | solution.py:599
  294.6 0.0 copy-done.13
  294.7 0.7 pad_add_fusion.meta
  295.3 0.0 collective-permute-done.3.bg1
  295.3 0.0 copy-done.12
  295.3 2.0 collective-permute-start.5
  297.3 66.4 %oproj.1.x_ref = bf16[4,8,128,2048]{3,2,1,0:T(8,128)(2,1)} custom-call(s32[65]{0:T(128)} %pad_add_fusion.meta, bf16[8,512,2048]{2,1,0:T(8,128)(2,1)} %get-tuple-element.6.attn_ref, bf16[4,16,128,2048]{3,2,1,0:T(8,128)(2,1)} %bitcast.86, bf16[2048,2048]{1,0:T(8,128)(2,1)} %bitcast.87, bf16[8,1536,256]{2,1,0:T(8,128)(2,1)} %bitcast.88), custom_call_target="tpu_custom_call" | custom-call | flops 42949672960 | bytes 62914560 | tf_op jit(solution)/shard_map/oproj/pallas_call | solution.py:617
  363.7 0.0 collective-permute-done.4.bu1
  363.7 0.0 collective-permute-done.5.ad1
  363.8 0.0 collective-permute-done.wg1
  363.8 0.0 collective-permute-done.1.wu1
  363.8 0.0 collective-permute-done.2.wd1
  363.8 0.0 all-gather.10.cloned.1.call-done
  363.8 358.8 %mlp_ring.1 = bf16[8,8,128,2048]{3,2,1,0:T(8,128)(2,1)} custom-call(s32[64]{0:T(128)} %ids_ref.3, bf16[4,8,128,2048]{3,2,1,0:T(8,128)(2,1)} %oproj.1.x_ref, f32[1,2048]{1,0:T(1,128)} %bitcast.92, bf16[8,128,2048]{2,1,0:T(8,128)(2,1)} %bitcast.90, bf16[2048,1024]{1,0:T(8,128)(2,1)} %wg0.1, bf16[2048,1024]{1,0:T(8,128)(2,1)} %collective-permute-done.wg1, ...), custom_call_target="tpu_custom_call" | custom-call | flops 120259084288 | bytes 102760448 | tf_op jit(solution)/shard_map/mlp_ring/pallas_call | solution.py:632
  722.6 22.9 %copy.32 = bf16[64,128,2048]{2,1,0:T(8,128)(2,1)} copy(bf16[64,128,2048]{2,1,0:T(8,128)(2,1)} %bitcast.70) | data formatting | bytes 67108864
  (19 shorter events, 0.1 us)
Async XLA Ops:
  6.5 5.0 copy-start.4
  6.5 5.0 copy-start.5
  6.6 6.7 copy-start.3
  6.6 6.7 copy-start.9
  6.6 6.7 copy-start.10
  6.6 290.7 %all-gather.8.cloned.1.call-start = ((), (), s32[]{:S(2)}) async-start(), calls=%async_computation.1 | async-start | bytes 7077888 | tf_op jit(solution)/shard_map/all_gather | solution.py:583
  6.6 6.7 copy-start.6
  6.6 6.7 copy-start.7
  6.7 6.7 copy-start.8
  8.8 5.6 copy-start
  8.8 5.6 copy-start.1
  8.8 5.6 copy-start.2
  8.9 288.4 %all-gather.6.cloned.1.call-start = ((), (), s32[]{:S(2)}) async-start(), calls=%async_computation | async-start | bytes 9437184 | tf_op jit(solution)/shard_map/all_gather | solution.py:582
  9.7 354.1 %all-gather.10.cloned.1.call-start = ((), (), s32[]{:S(2)}) async-start(), calls=%async_computation.2 | async-start | bytes 4718592 | tf_op jit(solution)/shard_map/all_gather | solution.py:585
  9.8 285.5 %collective-permute-start.3 = (bf16[2,256,1024]{2,1,0:T(8,128)(2,1)}, bf16[2,256,1024]{2,1,0:T(8,128)(2,1)}, u32[]{:S(2)}, u32[]{:S(2)}) collective-permute-start(bf16[2,256,1024]{2,1,0:T(8,128)(2,1)} %bg0.1), channel_id=1, source_target_pairs={{0,1},{1,0},{2,3},{3,2},{4,5},{5,4},{6,7},{7,6},{8,9},{9,8},{10,11... | collective-permute-start | bytes 3145736 | tf_op jit(solution)/shard_map/ppermute | solution.py:587
  10.6 353.2 %collective-permute-start.4 = (bf16[2,256,1024]{2,1,0:T(8,128)(2,1)}, bf16[2,256,1024]{2,1,0:T(8,128)(2,1)}, u32[]{:S(2)}, u32[]{:S(2)}) collective-permute-start(bf16[2,256,1024]{2,1,0:T(8,128)(2,1)} %bu0.1), channel_id=1, source_target_pairs={{0,1},{1,0},{2,3},{3,2},{4,5},{5,4},{6,7},{7,6},{8,9},{9,8},{10,11... | collective-permute-start | bytes 3145736 | tf_op jit(solution)/shard_map/ppermute | solution.py:587
  10.7 353.1 %collective-permute-start = (bf16[2048,1024]{1,0:T(8,128)(2,1)}, bf16[2048,1024]{1,0:T(8,128)(2,1)}, u32[]{:S(2)}, u32[]{:S(2)}) collective-permute-start(bf16[2048,1024]{1,0:T(8,128)(2,1)} %wg0.1), channel_id=1, source_target_pairs={{0,1},{1,0},{2,3},{3,2},{4,5},{5,4},{6,7},{7,6},{8,9},{9,8},{10,11... | collective-permute-start | bytes 12582920 | tf_op jit(solution)/shard_map/ppermute | solution.py:587
  11.1 352.7 %collective-permute-start.1 = (bf16[2048,1024]{1,0:T(8,128)(2,1)}, bf16[2048,1024]{1,0:T(8,128)(2,1)}, u32[]{:S(2)}, u32[]{:S(2)}) collective-permute-start(bf16[2048,1024]{1,0:T(8,128)(2,1)} %wu0.1), channel_id=1, source_target_pairs={{0,1},{1,0},{2,3},{3,2},{4,5},{5,4},{6,7},{7,6},{8,9},{9,8},{10,11... | collective-permute-start | bytes 12582920 | tf_op jit(solution)/shard_map/ppermute | solution.py:587
  11.2 352.6 %collective-permute-start.2 = (bf16[1024,2048]{1,0:T(8,128)(2,1)}, bf16[1024,2048]{1,0:T(8,128)(2,1)}, u32[]{:S(2)}, u32[]{:S(2)}) collective-permute-start(bf16[1024,2048]{1,0:T(8,128)(2,1)} %wd0.1), channel_id=1, source_target_pairs={{0,1},{1,0},{2,3},{3,2},{4,5},{5,4},{6,7},{7,6},{8,9},{9,8},{10,11... | collective-permute-start | bytes 12582920 | tf_op jit(solution)/shard_map/ppermute | solution.py:587
  13.4 2.3 copy-start.11
  15.6 279.0 %copy-start.13 = (s32[64]{0:T(128)S(1)}, s32[64]{0:T(128)}, u32[]{:S(2)}) copy-start(s32[64]{0:T(128)} %ids_ref.3) | copy-start | bytes 772
  15.6 279.7 %copy-start.12 = (bf16[2,1024,256]{2,1,0:T(8,128)(2,1)S(1)}, bf16[2,1024,256]{2,1,0:T(8,128)(2,1)}, u32[]{:S(2)}) copy-start(bf16[2,1024,256]{2,1,0:T(8,128)(2,1)} %ad0.1) | copy-start | bytes 3145732
  295.3 68.4 %collective-permute-start.5 = (bf16[2,1024,256]{2,1,0:T(8,128)(2,1)S(1)}, bf16[2,1024,256]{2,1,0:T(8,128)(2,1)}, u32[]{:S(2)}, u32[]{:S(2)}) collective-permute-start(bf16[2,1024,256]{2,1,0:T(8,128)(2,1)S(1)} %copy-done.12), channel_id=1, source_target_pairs={{0,1},{1,0},{2,3},{3,2},{4,5},{5,4},{6,7},{7,6},{8,9},{9,8},{10,11... | collective-permute-start | bytes 3145736 | tf_op jit(solution)/shard_map/ppermute | solution.py:587
Sparse Core Ops, SparseCore 0:
  9.0 56.8 all-gather.7
  67.5 79.5 all-gather.5
  148.7 39.3 all-gather.9

commit v6 on v5

--- a/solution.py
+++ b/solution.py
@@ -23,7 +23,8 @@
     return lax.dot_general(a, b, (((1,), (1,)), ((), ())), preferred_element_type=F32)
 
 
-def attn_body(dims, ids_ref, x_ref, gain_ref, cos_ref, sin_ref, a_own, w_own, b_own, out_ref, ga, gw, gb,
+def attn_body(dims, ids_ref, x_ref, gain_ref, cos_ref, sin_ref, a_own, w_own, b_own, o_own, l_own, u_own,
+              out_ref, ga, gw, gb, go, gl, gu,
               h, low, attn, w, bw, q_scr, k_scr, v_scr, asem, wsem, xsem, osem, ss, rs):
     n_dev, seqs, S, hd, nq, rank, D, chips = dims
     half = hd // 2
@@ -47,7 +48,8 @@
         pl.semaphore_signal(barrier, inc=1, device_id={'tensor': dev}, device_id_type=pl.DeviceIdType.MESH)
     pl.semaphore_wait(barrier, 3)
 
-    groups = ((a_own, ga), (w_own, gw), (b_own, gb))
+    groups = ((a_own, ga), (w_own, gw), (b_own, gb), (o_own, go), (l_own, gl), (u_own, gu))
+    now, later = (1, 2), (3, 4, 5)
 
     def remote(m, n, src, dst, dev):
         return pltpu.make_async_remote_copy(src_ref=src, dst_ref=dst, send_sem=ss.at[m, n], recv_sem=rs.at[m, n],
@@ -236,13 +238,25 @@
 
         @pl.when(it == 2)
         def _():
-            pass_on(1)
-            pass_on(2)
+            for m in now:
+                pass_on(m)
+            for m in later:
+                send_own(m)
 
         @pl.when(it == steps)
         def _():
-            pass_far(1)
-            pass_far(2)
+            for m in now:
+                pass_far(m)
+
+        @pl.when(it == 2 * steps + 2)
+        def _():
+            for m in later:
+                pass_on(m)
+
+        @pl.when(it == 3 * steps + 3)
+        def _():
+            for m in later:
+                pass_far(m)
         for r in range(1, chips):
             @pl.when(it == r * steps - 2)
             def _():
@@ -266,7 +280,10 @@
 
     for i in range(steps):
         out_copy(i).wait()
-    for m in range(3):
+    for m in later:
+        for n in range(4):
+            copy(m, 4 + n).wait_recv()
+    for m in range(len(groups)):
         for n in range(8):
             copy(m, n).wait_send()
 
@@ -567,7 +584,6 @@
         def rows_t(w):
             return jnp.transpose(w, (1, 2, 0)).reshape(-1, w.shape[0])
 
-        gather = functools.partial(lax.all_gather, axis_name='tensor', axis=0)
         swapped = functools.partial(lax.ppermute, axis_name='tensor', perm=swap)
 
         def rows_a(stacks):
@@ -579,10 +595,10 @@
         a_own = rows_a((a_q, a_k, a_v))
         w_own = jnp.concatenate([rows_t(w_q), rows_t(w_k), rows_t(w_v)], axis=0)
         b_own = jnp.concatenate([b_rows(b[a]) for a in range(n_ad) for b in (b_q, b_k, b_v)], axis=0)
-        g_wo = gather(w_o.reshape(qw, D))
-        g_b = gather(jnp.concatenate([a_o.reshape(n_ad * qw, rank), b_o.reshape(n_ad * rank, qw),
-                                      b_down.reshape(n_ad * rank, qw)], axis=0))
-        g_gu = gather(rows_a((a_gate, a_up)))
+        o_own = w_o.reshape(qw, D)
+        l_own = jnp.concatenate([a_o.reshape(n_ad * qw, rank), b_o.reshape(n_ad * rank, qw), b_down.reshape(n_ad * rank, qw)], axis=0)
+        u_own = rows_a((a_gate, a_up))
+        owned = (a_own, w_own, b_own, o_own, l_own, u_own)
         mlp_own = (w_gate, w_up, w_down, b_gate, b_up, a_down)
         mlp_other = tuple(swapped(w) for w in mlp_own)
 
@@ -596,23 +612,26 @@
         Fc = CORES * w_gate.shape[1]
         dma = pltpu.SemaphoreType.DMA
         dw = qw + 2 * hd
-        attn_all = pl.pallas_call(
+        attn_all, _, _, _, g_wo, g_b, g_gu = pl.pallas_call(
             functools.partial(attn_body, (n_dev, seqs, S, hd, nq, rank, D, chips)),
-            in_specs=[pl.BlockSpec(memory_space=pltpu.SMEM), ANY] + [pl.BlockSpec(memory_space=pltpu.VMEM)] * 3 + [ANY] * 3,
-            out_specs=[ANY] * 4,
+            in_specs=[pl.BlockSpec(memory_space=pltpu.SMEM), ANY] + [pl.BlockSpec(memory_space=pltpu.VMEM)] * 3 + [ANY] * len(owned),
+            out_specs=[ANY] * (1 + len(owned)),
             scratch_shapes=[
                 pltpu.VMEM((steps, D, M), BF16), pltpu.VMEM((steps, 3 * rank, M), BF16), pltpu.VMEM((steps, M, n_dev * qw), BF16),
                 pltpu.VMEM((chips, CORES * dw, D), BF16), pltpu.VMEM((chips, n_ad, CORES * dw, rank), BF16),
                 pltpu.VMEM((2, CORES * qw, M), BF16), pltpu.VMEM((2, CORES, M, hd), BF16), pltpu.VMEM((2, CORES * hd, M), BF16),
-                dma((n_dev, 3 * n_ad)), dma((chips, CORES, 1 + n_ad)), dma((2, chips)), dma((steps,)), dma((3, 8)), dma((3, 8))],
-            out_shape=[jax.ShapeDtypeStruct((steps, M, n_dev * qw), BF16), jax.ShapeDtypeStruct((n_dev,) + a_own.shape, BF16),
-                       jax.ShapeDtypeStruct((n_dev,) + w_own.shape, BF16), jax.ShapeDtypeStruct((n_dev,) + b_own.shape, BF16)],
+                dma((n_dev, 3 * n_ad)), dma((chips, CORES, 1 + n_ad)), dma((2, chips)), dma((steps,)), dma((len(owned), 8)), dma((len(owned), 8))],
+            out_shape=[jax.ShapeDtypeStruct((steps, M, n_dev * qw), BF16)] + [
+                jax.ShapeDtypeStruct((n_dev,) + v.shape, BF16) for v in owned],
             compiler_params=pltpu.CompilerParams(vmem_limit_bytes=VMEM_LIMIT, collective_id=1, has_side_effects=True),
             name="attn_ring",
             cost_estimate=pl.CostEstimate(flops=3 * steps * M * D * (n_dev * qw + 2 * n_dev * hd + 3 * rank),
                                           bytes_accessed=6 * steps * M * D + 33 * 2**20, transcendentals=0),
-        )(adapter_ids, x4, gain_attn.reshape(1, D), cos_t, sin_t, a_own, w_own, b_own)[0]
-        core = lax.axis_index('tensor') % CORES
+        )(adapter_ids, x4, gain_attn.reshape(1, D), cos_t, sin_t, *owned)
+        me = lax.axis_index('tensor')
+        g_wo, g_b, g_gu = [lax.dynamic_update_slice(g, own[None], (me, 0, 0))
+                           for g, own in zip((g_wo, g_b, g_gu), owned[3:])]
+        core = me % CORES
         meta = jnp.concatenate([adapter_ids.astype(jnp.int32), core.reshape(1).astype(jnp.int32)])
         x1_all = pl.pallas_call(
             functools.partial(oproj_body, (n_dev, seqs, S, qw, rank, D, chips)),

time: 752 us -> 717 us (0.953)
  Pallas kernels: 704 us -> 673 us
  between operations: 13.4 us -> 0.14 us
  local copies, waits for them, and re-layouts: 23 us -> 32.9 us
    pallas_call x1, Pallas kernels: 279 us -> 249 us  [local_layer(): pl.pallas_call(functools.partial(attn_body, (n_dev, seqs, S, hd, nq, rank...]
  transfers between devices with their start and end apart: 9 -> 6, of which waited for: 0 -> 0; matrix products, arithmetic and copies ran while one was open for 1% -> 3% of each run, Pallas kernels for 46% -> 44%
where the time goes in v6:
time: 717 us
  Pallas kernels  673 us (94%)
  local copies, waits for them, and re-layouts  32.9 us (5%)
  other arithmetic  9.26 us (1%)
    pallas_call x1, Pallas kernels, local_layer(): pl.pallas_call(functools.partial(mlp_body, (seqs, S, rank, D, chips)), in...  357 us
    pallas_call x1, Pallas kernels, local_layer(): pl.pallas_call(functools.partial(attn_body, (n_dev, seqs, S, hd, nq, rank...  249 us
    pallas_call x1, Pallas kernels, local_layer(): pl.pallas_call(functools.partial(oproj_body, (n_dev, seqs, S, qw, rank, D...  66.6 us
    unnamed x34, local copies, waits for them, and re-layouts  29.4 us
  transfers between devices with their start and end apart: 6, of which 0 were waited for; matrix products, arithmetic and copies ran while one was open for 3% of the time, Pallas kernels for 44%

profile of v6, /device:TPU:113, one launch (start us, length us, event | category | flops | bytes accessed | tf_op | source)
XLA Modules:
  0.0 716.9 jit_solution(923373099520332460)
XLA Ops:
  0.0 0.7 collective-permute-start
  0.7 0.1 collective-permute-start.1
  0.8 0.4 collective-permute-start.2
  1.2 0.1 collective-permute-start.3
  1.3 0.4 collective-permute-start.4
  1.8 1.0 fusion.2
  2.7 0.7 constant_dynamic-update-slice_fusion.1
  3.4 1.4 bitcast_dynamic-update-slice_fusion.6
  4.8 1.4 bitcast_dynamic-update-slice_fusion.5
  6.2 0.7 constant_dynamic-update-slice_fusion
  6.9 1.4 bitcast_dynamic-update-slice_fusion.4
  8.3 1.4 bitcast_dynamic-update-slice_fusion.3.b_own
  9.6 0.7 fusion
  10.4 1.9 pad_maximum_fusion.3.u_own
  12.2 2.0 pad_maximum_fusion.2.l_own
  14.3 0.0 copy-done
  14.3 0.0 copy-done.8
  14.3 0.0 copy-done.7
  14.3 1.2 pad_maximum_fusion.w_own
  15.5 0.0 copy-done.9
  15.5 0.0 copy-done.10
  15.6 0.0 copy-done.11
  15.6 1.0 pad_maximum_fusion.1.a_own
  16.5 0.0 copy-start.1
  16.5 249.0 %attn_ring.1 = (bf16[8,512,2048]{2,1,0:T(8,128)(2,1)}, bf16[8,192,2048]{2,1,0:T(8,128)(2,1)}, bf16[8,384,2048]{2,1,0:T(8,128)(2,1)}, bf16[8,768,256]{2,1,0:T(8,1...) custom-call(s32[64]{0:T(128)} %ids_ref.3, ...), custom_call_target="tpu_custom_call" | custom-call | flops 96636764160 | bytes 84934656 | tf_op jit(solution)/shard_map/attn_ring/pallas_call | solution.py:615
  265.6 0.0 copy-done.13
  265.6 0.6 pad_add_fusion.meta
  266.2 0.0 copy-done.2
  266.2 0.0 copy-done.3
  266.2 0.0 copy-done.4
  266.2 0.9 bitcast_dynamic-update-slice_fusion.1.gb_ref.bd_ref
  267.1 0.0 copy-done.1
  267.1 1.1 bitcast_dynamic-update-slice_fusion
  268.2 0.0 collective-permute-done.3.bg1
  268.2 0.0 collective-permute-start.5
  268.2 0.0 copy-start.6
  268.2 66.6 %oproj.1.x_ref = bf16[4,8,128,2048]{3,2,1,0:T(8,128)(2,1)} custom-call(s32[65]{0:T(128)} %pad_add_fusion.meta, bf16[8,512,2048]{2,1,0:T(8,128)(2,1)} %get-tuple-element.9.attn_ref, bf16[4,16,128,2048]{3,2,1,0:T(8,128)(2,1)} %bitcast.97, bf16[2048,2048]{1,0:T(8,128)(2,1)} %bitcast.98, bf16[8,1536,256]{2,1,0:T(8,128)(2,1)} %bitcast_dynamic-update-slice_fusion.1.gb_ref.bd_ref), custom_call_target="tpu_custom_call" | custom-call | flops 42949672960 | bytes 62914560 | tf_op jit(solution)/shard_map/oproj/pallas_call | solution.py:636
  334.8 0.0 copy-done.5
  334.8 0.0 copy-done.6
  334.8 0.8 bitcast_dynamic-update-slice_fusion.2.agu_ref
  335.7 0.0 collective-permute-done.4.bu1
  335.7 0.0 collective-permute-done.5.ad1
  335.7 0.0 collective-permute-done.wg1
  335.7 0.0 collective-permute-done.1.wu1
  335.7 0.0 collective-permute-done.2.wd1
  335.7 1.0 copy-done.12
  336.7 357.3 %mlp_ring.1 = bf16[8,8,128,2048]{3,2,1,0:T(8,128)(2,1)} custom-call(s32[64]{0:T(128)} %ids_ref.3, bf16[4,8,128,2048]{3,2,1,0:T(8,128)(2,1)} %oproj.1.x_ref, f32[1,2048]{1,0:T(1,128)} %bitcast.100, bf16[8,128,2048]{2,1,0:T(8,128)(2,1)} %bitcast_dynamic-update-slice_fusion.2.agu_ref, bf16[2048,1024]{1,0:T(8,128)(2,1)} %wg0.1, ...), custom_call_target="tpu_custom_call" | custom-call | flops 120259084288 | bytes 102760448 | tf_op jit(solution)/shard_map/mlp_ring/pallas_call | solution.py:651
  694.0 22.9 %copy.35 = bf16[64,128,2048]{2,1,0:T(8,128)(2,1)} copy(bf16[64,128,2048]{2,1,0:T(8,128)(2,1)} %bitcast.75) | data formatting | bytes 67108864
  (13 shorter events, 0.0 us)
Async XLA Ops:
  0.0 14.3 %copy-start = (bf16[2048,4,64]{0,2,1:T(8,128)(2,1)S(1)}, bf16[2048,4,64]{0,2,1:T(8,128)(2,1)}, u32[]{:S(2)}) copy-start(bf16[2048,4,64]{0,2,1:T(8,128)(2,1)} %param.29) | copy-start | bytes 3145732
  0.0 14.3 %copy-start.8 = (bf16[2048,1,64]{0,2,1:T(8,128)(2,1)S(1)}, bf16[2048,1,64]{0,2,1:T(8,128)(2,1)}, u32[]{:S(2)}) copy-start(bf16[2048,1,64]{0,2,1:T(8,128)(2,1)} %param.30) | copy-start | bytes 786436
  0.0 14.3 %copy-start.7 = (bf16[2048,1,64]{0,2,1:T(8,128)(2,1)S(1)}, bf16[2048,1,64]{0,2,1:T(8,128)(2,1)}, u32[]{:S(2)}) copy-start(bf16[2048,1,64]{0,2,1:T(8,128)(2,1)} %param.31) | copy-start | bytes 786436
  0.0 335.7 %collective-permute-start = (bf16[2048,1024]{1,0:T(8,128)(2,1)}, bf16[2048,1024]{1,0:T(8,128)(2,1)}, u32[]{:S(2)}, u32[]{:S(2)}) collective-permute-start(bf16[2048,1024]{1,0:T(8,128)(2,1)} %wg0.1), channel_id=1, source_target_pairs={{0,1},{1,0},{2,3},{3,2},{4,5},{5,4},{6,7},{7,6},{8,9},{9,8},{10,11... | collective-permute-start | bytes 12582920 | tf_op jit(solution)/shard_map/ppermute | solution.py:603
  0.7 335.0 %collective-permute-start.1 = (bf16[2048,1024]{1,0:T(8,128)(2,1)}, bf16[2048,1024]{1,0:T(8,128)(2,1)}, u32[]{:S(2)}, u32[]{:S(2)}) collective-permute-start(bf16[2048,1024]{1,0:T(8,128)(2,1)} %wu0.1), channel_id=1, source_target_pairs={{0,1},{1,0},{2,3},{3,2},{4,5},{5,4},{6,7},{7,6},{8,9},{9,8},{10,11... | collective-permute-start | bytes 12582920 | tf_op jit(solution)/shard_map/ppermute | solution.py:603
  0.8 334.9 %collective-permute-start.2 = (bf16[1024,2048]{1,0:T(8,128)(2,1)}, bf16[1024,2048]{1,0:T(8,128)(2,1)}, u32[]{:S(2)}, u32[]{:S(2)}) collective-permute-start(bf16[1024,2048]{1,0:T(8,128)(2,1)} %wd0.1), channel_id=1, source_target_pairs={{0,1},{1,0},{2,3},{3,2},{4,5},{5,4},{6,7},{7,6},{8,9},{9,8},{10,11... | collective-permute-start | bytes 12582920 | tf_op jit(solution)/shard_map/ppermute | solution.py:603
  1.2 267.0 %collective-permute-start.3 = (bf16[2,256,1024]{2,1,0:T(8,128)(2,1)}, bf16[2,256,1024]{2,1,0:T(8,128)(2,1)}, u32[]{:S(2)}, u32[]{:S(2)}) collective-permute-start(bf16[2,256,1024]{2,1,0:T(8,128)(2,1)} %bg0.1), channel_id=1, source_target_pairs={{0,1},{1,0},{2,3},{3,2},{4,5},{5,4},{6,7},{7,6},{8,9},{9,8},{10,11... | collective-permute-start | bytes 3145736 | tf_op jit(solution)/shard_map/ppermute | solution.py:603
  1.3 334.4 %collective-permute-start.4 = (bf16[2,256,1024]{2,1,0:T(8,128)(2,1)}, bf16[2,256,1024]{2,1,0:T(8,128)(2,1)}, u32[]{:S(2)}, u32[]{:S(2)}) collective-permute-start(bf16[2,256,1024]{2,1,0:T(8,128)(2,1)} %bu0.1), channel_id=1, source_target_pairs={{0,1},{1,0},{2,3},{3,2},{4,5},{5,4},{6,7},{7,6},{8,9},{9,8},{10,11... | collective-permute-start | bytes 3145736 | tf_op jit(solution)/shard_map/ppermute | solution.py:603
  4.8 10.8 %copy-start.9 = (bf16[2,2048,32]{1,2,0:T(8,128)(2,1)S(1)}, bf16[2,2048,32]{1,2,0:T(8,128)(2,1)}, u32[]{:S(2)}) copy-start(bf16[2,2048,32]{1,2,0:T(8,128)(2,1)} %param.40) | copy-start | bytes 786436
  4.8 10.8 %copy-start.10 = (bf16[2,2048,32]{1,2,0:T(8,128)(2,1)S(1)}, bf16[2,2048,32]{1,2,0:T(8,128)(2,1)}, u32[]{:S(2)}) copy-start(bf16[2,2048,32]{1,2,0:T(8,128)(2,1)} %param.38) | copy-start | bytes 786436
  4.8 10.8 %copy-start.11 = (bf16[2,2048,32]{1,2,0:T(8,128)(2,1)S(1)}, bf16[2,2048,32]{1,2,0:T(8,128)(2,1)}, u32[]{:S(2)}) copy-start(bf16[2,2048,32]{1,2,0:T(8,128)(2,1)} %param.36) | copy-start | bytes 786436
  16.5 249.0 %copy-start.13 = (s32[64]{0:T(128)S(1)}, s32[64]{0:T(128)}, u32[]{:S(2)}) copy-start(s32[64]{0:T(128)} %ids_ref.3) | copy-start | bytes 772
  16.5 249.6 %copy-start.2 = (bf16[2,256,256]{2,1,0:T(8,128)(2,1)S(1)}, bf16[2,256,256]{2,1,0:T(8,128)(2,1)}, u32[]{:S(2)}) copy-start(bf16[2,256,256]{2,1,0:T(8,128)(2,1)} %param.49) | copy-start | bytes 786436
  16.5 249.6 %copy-start.3 = (bf16[2,256,256]{2,1,0:T(8,128)(2,1)S(1)}, bf16[2,256,256]{2,1,0:T(8,128)(2,1)}, u32[]{:S(2)}) copy-start(bf16[2,256,256]{2,1,0:T(8,128)(2,1)} %param.43) | copy-start | bytes 786436
  16.5 249.6 %copy-start.4 = (bf16[2,4,64,256]{3,2,1,0:T(8,128)(2,1)S(1)}, bf16[2,4,64,256]{3,2,1,0:T(8,128)(2,1)}, u32[]{:S(2)}) copy-start(bf16[2,4,64,256]{3,2,1,0:T(8,128)(2,1)} %param.42) | copy-start | bytes 786436
  16.5 250.6 %copy-start.1 = (bf16[4,64,2048]{2,1,0:T(8,128)(2,1)S(1)}, bf16[4,64,2048]{2,1,0:T(8,128)(2,1)}, u32[]{:S(2)}) copy-start(bf16[4,64,2048]{2,1,0:T(8,128)(2,1)} %param.32) | copy-start | bytes 3145732
  268.2 67.5 %collective-permute-start.5 = (bf16[2,1024,256]{2,1,0:T(8,128)(2,1)}, bf16[2,1024,256]{2,1,0:T(8,128)(2,1)S(1)}, u32[]{:S(2)}, u32[]{:S(2)}) collective-permute-start(bf16[2,1024,256]{2,1,0:T(8,128)(2,1)} %ad0.1), channel_id=1, source_target_pairs={{0,1},{1,0},{2,3},{3,2},{4,5},{5,4},{6,7},{7,6},{8,9},{9,8},{10,11... | collective-permute-start | bytes 3145736 | tf_op jit(solution)/shard_map/ppermute | solution.py:603
  268.2 66.6 %copy-start.5 = (bf16[2,2048,32]{1,2,0:T(8,128)(2,1)S(1)}, bf16[2,2048,32]{1,2,0:T(8,128)(2,1)}, u32[]{:S(2)}) copy-start(bf16[2,2048,32]{1,2,0:T(8,128)(2,1)} %param.46) | copy-start | bytes 786436
  268.2 66.6 %copy-start.6 = (bf16[2,2048,32]{1,2,0:T(8,128)(2,1)S(1)}, bf16[2,2048,32]{1,2,0:T(8,128)(2,1)}, u32[]{:S(2)}) copy-start(bf16[2,2048,32]{1,2,0:T(8,128)(2,1)} %param.44) | copy-start | bytes 786436
  335.7 1.0 copy-start.12
